TPU v7x, 256 devices: a 4x2x16 block of a 4x16x16 slice. The times are simulated.
256 devices in a mesh: parts: 2 (over y), dp: 64 (over x, z), tensor: 2 (over core).
Axes of the slice: x: 4, y: 2, z: 16, core: 2. Of those that a mesh axis runs over, the one named last changes fastest.
The devices are a block of a 4x16x16 slice.
Arguments:
- normed: bfloat16 [128, 256, 4096], P(('parts', 'dp')), parts along dimension 0, may hold values from -28 to 28
- q_weight: bfloat16 [4096, 2048], P('dp', 'tensor'), may hold values from -0.09375 to 0.09375
- kv_weight: bfloat16 [4096, 2, 512], P('dp', None, 'tensor'), may hold values from -0.09375 to 0.09375
- o_weight: bfloat16 [2048, 4096], P('tensor', 'dp'), may hold values from -0.5 to 0.5
- lengths: int32 [128], P(('parts', 'dp')), parts along dimension 0, may hold values from 64 to 256
- destinations: int32 [128], P(('parts', 'dp')), parts along dimension 0, may hold values from 0 to 63, each once
Outputs:
- projected: bfloat16 [128, 256, 4096], P(('parts', 'dp'), None, 'tensor'), parts along dimension 0
- kv_cache: bfloat16 [128, 2, 4, 256, 128], P(('parts', 'dp'), None, None, 'tensor'), parts along dimension 0
There are 2 independent parts, one for each index of `parts`. A program takes and returns all parts, laid end to end along the dimension named above; an argument that names none is the same for every part. Nothing has to cross between parts.
All inputs are finite; a program needn't handle non-finite values.
Results may differ from a plain program's by a relative error of at most 0.012.
The roundings to bfloat16 on the way count: a program that leaves them out, or rounds other values in their place, can miss the bound.
Values may be sent and summed in bfloat16 or wider, within the bound.
No kernel may reach another device: no remote copies, remote signals or barrier semaphores. Data moves between devices by JAX's collectives and lax.ppermute only.
A program may use at most 128 MiB of HBM per device.

v0:
```python
import functools
import math

import jax
import jax.numpy as jnp
import numpy as np
from jax import lax
from jax.experimental import pallas as pl
from jax.experimental.pallas import tpu as pltpu
from jax.sharding import PartitionSpec as P

HD = 128
ROPE_BASE = 500000.0
X = 4


def mover(ring):
    def move(array, where):
        pairs = []
        for x in range(X):
            for z in range(ring):
                for t in range(2):
                    a, b, c = where(x, z, t)
                    target = ((a % X) * ring + b % ring) * 2 + c
                    pairs.append(((x * ring + z) * 2 + t, target))
        return lax.ppermute(array, ("dp", "tensor"), pairs)

    return move


def project_kernel(pair_ref, x_ref, w_ref, out_ref):
    slots, total, depth = x_ref.shape
    weights = w_ref[...].reshape(depth, w_ref.shape[2])
    product = jnp.dot(
        x_ref[...].reshape(slots * total, depth), weights, preferred_element_type=jnp.float32
    ).reshape(slots, total, -1)
    width = weights.shape[1]
    columns = pl.ds(pl.multiple_of(pl.program_id(1) * width, width), width)

    @pl.when(pl.program_id(0) == 0)
    def _():
        out_ref[:, :, columns] = product

    @pl.when(pl.program_id(0) > 0)
    def _():
        out_ref[:, :, columns] += product


def project_in(states, weights, pair, pieces=3):
    _, total, half = states.shape
    ring, rows, both = weights.shape
    wide = both // 2
    return pl.pallas_call(
        project_kernel,
        grid_spec=pltpu.PrefetchScalarGridSpec(
            num_scalar_prefetch=1,
            grid=(2, pieces),
            in_specs=[
                pl.BlockSpec((2, total, half // 2), lambda b, n, p: (p[0], 0, b)),
                pl.BlockSpec((ring, rows, wide // pieces), lambda b, n, p: (0, 0, b * pieces + n)),
            ],
            out_specs=pl.BlockSpec((2, total, wide), lambda b, n, p: (0, 0, 0)),
        ),
        out_shape=jax.ShapeDtypeStruct((2, total, wide), jnp.float32),
        compiler_params=pltpu.CompilerParams(vmem_limit_bytes=24 << 20),
        name="project_in",
    )(pair.reshape(1), states, weights)


def attend_kernel(heads, a_ref, b_ref, l0_ref, l1_ref, turn_ref, out_ref, cache_ref):
    note = jnp.where(pl.program_id(0) == 0, l0_ref[:1, :1], l1_ref[:1, :1])
    length = note.astype(jnp.float32).astype(jnp.int32)
    cosine = jnp.concatenate([turn_ref[:, : HD // 2]] * 2, axis=1)
    sine = jnp.concatenate([-turn_ref[:, HD // 2 :], turn_ref[:, HD // 2 :]], axis=1)
    total = a_ref.shape[1]

    def part(index):
        columns = slice(index * HD, (index + 1) * HD)
        return a_ref[0, :, columns] + b_ref[0, :, columns]

    def turned(values):
        swapped = pltpu.roll(values, HD // 2, 1)
        return (values * cosine + swapped * sine).astype(jnp.bfloat16)

    keys = turned(part(heads))
    values = part(heads + 1).astype(jnp.bfloat16)
    live = lax.broadcasted_iota(jnp.int32, (total, HD), 0) < length
    zero = jnp.zeros((), jnp.bfloat16)
    cache_ref[0, 0] = jnp.where(live, keys, zero)
    cache_ref[0, 1] = jnp.where(live, values, zero)
    row = lax.broadcasted_iota(jnp.int32, (total, total), 0)
    column = lax.broadcasted_iota(jnp.int32, (total, total), 1)
    allowed = (row >= column) & (column < length)
    for h in range(heads):
        scores = lax.dot_general(
            turned(part(h)), keys, (((1,), (1,)), ((), ())), preferred_element_type=jnp.float32
        ) * (1.0 / math.sqrt(HD))
        scores = jnp.where(allowed, scores, -jnp.inf)
        peak = jnp.max(scores, axis=-1, keepdims=True)
        expo = jnp.exp(scores - peak)
        share = 1.0 / jnp.sum(expo, axis=-1, keepdims=True)
        weights = (expo * share).astype(jnp.bfloat16)
        out_ref[:, h * HD : (h + 1) * HD] = jnp.dot(
            weights, values, preferred_element_type=jnp.float32
        ).astype(jnp.bfloat16)


def turns(total):
    steps = np.arange(HD // 2, dtype=np.float32) * np.float32(2.0 / HD)
    freq = np.power(np.float32(ROPE_BASE), -steps)
    angle = np.arange(total, dtype=np.float32)[:, None] * freq[None, :]
    return np.concatenate([np.cos(angle), np.sin(angle)], axis=1).astype(np.float32)


def attend(kept, other, first, second, heads):
    _, total, wide = kept.shape
    rows = pl.BlockSpec((1, total, wide), lambda s: (s, 0, 0))
    note = pl.BlockSpec((16, HD), lambda s: (0, wide // HD))
    return pl.pallas_call(
        functools.partial(attend_kernel, heads),
        grid=(2,),
        in_specs=[rows, rows, note, note, pl.BlockSpec((total, HD), lambda s: (0, 0))],
        out_specs=[
            pl.BlockSpec((total, heads * HD), lambda s: (s, 0)),
            pl.BlockSpec((1, 2, total, HD), lambda s: (s, 0, 0, 0)),
        ],
        out_shape=[
            jax.ShapeDtypeStruct((2 * total, heads * HD), jnp.bfloat16),
            jax.ShapeDtypeStruct((2, 2, total, HD), jnp.bfloat16),
        ],
        compiler_params=pltpu.CompilerParams(vmem_limit_bytes=24 << 20),
        name="attend",
    )(kept, other, first, second, turns(total))


def output_kernel(shift_ref, a0, a1, a2, a3, a4, near_ref, far_ref, out_ref, line_ref):
    half = a0.shape[0] // 2

    @pl.when(pl.program_id(0) == 0)
    def _():
        for d, start, rows in ((0, 0, a0), (1, 0, a1), (2, 0, a2), (2, half, a3), (3, 0, a4)):
            place = (d + shift_ref[0]) % X
            line_ref[place, start : start + rows.shape[0], :] = rows[...]

    group = a0.shape[1]
    total = 0.0
    for place in range(X):
        ref = near_ref if place < X // 2 else far_ref
        start = place % (X // 2) * group
        total += lax.dot_general(
            line_ref[place],
            ref[:, start : start + group],
            (((1,), (1,)), ((), ())),
            preferred_element_type=jnp.float32,
        )
    out_ref[...] = total.astype(out_ref.dtype)


def project_out(mine, after, across, before, near, far, shift, pieces=4):
    total, group = mine.shape
    columns = near.shape[0]
    whole = pl.BlockSpec((total, group), lambda i, w: (0, 0))
    part = pl.BlockSpec((total // 2, group), lambda i, w: (0, 0))
    weights = pl.BlockSpec((columns // pieces, near.shape[1]), lambda i, w: (i, 0))
    return pl.pallas_call(
        output_kernel,
        grid_spec=pltpu.PrefetchScalarGridSpec(
            num_scalar_prefetch=1,
            grid=(pieces,),
            in_specs=[whole, whole, part, part, whole, weights, weights],
            out_specs=pl.BlockSpec((total, columns // pieces), lambda i, w: (0, i)),
            scratch_shapes=[pltpu.VMEM((X, total, group), mine.dtype)],
        ),
        out_shape=jax.ShapeDtypeStruct((total, columns), jnp.bfloat16),
        compiler_params=pltpu.CompilerParams(vmem_limit_bytes=24 << 20),
        name="project_out",
    )(shift.reshape(1), mine, after, *across, before, near, far)


def on_device(normed, q_weight, kv_weight, o_weight, lengths, destinations):
    count = lax.axis_size("dp")
    ring = count // X
    move = mover(ring)
    spot = lax.axis_index("dp")
    x, z, t = spot // ring, spot % ring, lax.axis_index("tensor")
    odd = x % 2 == 1

    total, width = normed.shape[1:]
    rows = q_weight.shape[0]
    group = q_weight.shape[1] // 2
    heads = group // HD
    plus = lambda x, z, t: (x + 1, z, t)
    minus = lambda x, z, t: (x - 1, z, t)
    up = lambda x, z, t: (x, z + 1, t)
    down = lambda x, z, t: (x, z - 1, t)
    swap = lambda x, z, t: (x, z, 1 - t)

    note = jnp.broadcast_to(lengths.astype(jnp.bfloat16), (rows, HD))

    def columns(b):
        q = lax.dynamic_slice(q_weight, (0, b * group), (rows, group))
        kv = lax.dynamic_slice(kv_weight, (0, 0, b * HD), (rows, 2, HD))
        return jnp.concatenate([q, kv[:, 0], kv[:, 1], note], axis=1)

    part0 = move(columns(x % 2), lambda x, z, t: (2 * t + x % 2, z, x // 2))
    part1 = move(columns((x + 1) % 2), lambda x, z, t: (2 * t + (x + 1) % 2, z, x // 2))
    first = jnp.where(odd, part1, part0)
    second = jnp.where(odd, part0, part1)
    wide = group + 2 * HD

    block = jnp.concatenate([first[:, :wide], second[:, :wide], o_weight.T], axis=1)
    full_in = jnp.zeros((ring, rows, 2 * wide), block.dtype)
    full_out = jnp.zeros((ring, rows, block.shape[1] - 2 * wide), block.dtype)

    def place(full, block, index, row=0):
        at = (index % ring, row, 0)
        return (
            lax.dynamic_update_slice(full[0], block[None, :, : 2 * wide], at),
            lax.dynamic_update_slice(full[1], block[None, :, 2 * wide :], at),
        )

    full = full_in, full_out
    rising = falling = block
    last = ring // 2
    for k in range(1, last):
        placed = place(full, rising, z - k + 1)
        if k > 1:
            placed = place(placed, falling, z + k - 1)
        rising = move(rising, up)
        falling = move(falling, down)
        rising, falling, full = lax.optimization_barrier((rising, falling, placed))
        if k == 1:
            half = width // 2
            rising, normed = lax.optimization_barrier((rising, normed))
            own = lax.dynamic_slice(normed[0], (0, t * half), (total, half))
            before = move(own, plus)
            after = move(own, minus)
            across0 = move(before[: total // 2], plus)
            across1 = move(after[total // 2 :], minus)
    full = place(place(full, rising, z - last + 1), falling, z + last - 1)
    cut = rows // 2
    full = place(full, move(rising[:cut], up), z - last)
    full_in, full_out = place(full, move(falling[cut:], down), z + last, cut)

    o_half = full_out.reshape(ring * rows, -1)
    o_other = move(o_half, swap)

    states = jnp.zeros((X, total, half), own.dtype)
    for piece, d, row in (
        (own, 0, 0),
        (before, -1, 0),
        (after, 1, 0),
        (across0, 2, 0),
        (across1, 2, total // 2),
    ):
        states = lax.dynamic_update_slice(states, piece[None], ((x + d) % X, row, 0))
    other = move(project_in(states, full_in, 1 - t), swap)
    kept = project_in(states, full_in, t)

    mixed, cache = attend(kept, other, first, second, heads)
    from_before = move(mixed, plus)
    from_after = move(mixed, minus)
    across = move(from_before[:total], plus), move(from_after[total:], minus)
    out = project_out(
        mixed, from_after, across, from_before, o_half, o_other, (x - 2 * t) % X
    )
    out0 = lax.dynamic_slice(out, (x % 2 * total, 0), (total, out.shape[1]))
    out1 = lax.dynamic_slice(out, ((x + 1) % 2 * total, 0), (total, out.shape[1]))
    home0 = move(out0, lambda x, z, t: (2 * t + x % 2, z, x // 2))
    home1 = move(out1, lambda x, z, t: (2 * t + (x + 1) % 2, z, x // 2))
    projected = jnp.concatenate(
        [jnp.where(odd, home1, home0), jnp.where(odd, home0, home1)], axis=1
    )

    cache = cache.reshape(2, 2, 2, total // 2, HD)
    mine = lax.dynamic_index_in_dim(cache, t, 2, keepdims=False)
    theirs = move(lax.dynamic_index_in_dim(cache, 1 - t, 2, keepdims=False), swap)
    four = jnp.concatenate([mine, theirs], axis=0)
    flat = four.reshape(X, count, -1).transpose(1, 0, 2)
    label = jnp.broadcast_to(destinations.astype(jnp.bfloat16), (count, 1, flat.shape[2]))
    spread = lax.all_to_all(
        jnp.concatenate([flat, label], axis=1), "dp", 0, 0, tiled=True
    )
    sent_to = spread[:, X, 0].astype(jnp.int32)
    slots = jnp.arange(count, dtype=jnp.int32)
    match = sent_to[None, :] == slots[:, None]
    source = jnp.sum(jnp.where(match, slots[None, :], 0), axis=1)
    head = jnp.arange(X, dtype=jnp.int32)[None]
    index = (head * ring + (source % ring)[:, None]) * (X + 1)
    index = index + ((source // ring)[:, None] ^ (2 * t))
    outgoing = jnp.take(spread.reshape(count * (X + 1), -1), index.reshape(-1), axis=0)
    arrived = lax.all_to_all(
        outgoing.reshape(count, X, -1), "dp", split_axis=0, concat_axis=0, tiled=True
    )
    routed = arrived.transpose(1, 0, 2).reshape(X, 2, total // 2, HD).transpose(1, 0, 2, 3)
    return (projected[None], routed[None])


def solution(mesh):
    placed = (
        P(("parts", "dp"), None, None),
        P("dp", "tensor"),
        P("dp", None, "tensor"),
        P("tensor", "dp"),
        P(("parts", "dp")),
        P(("parts", "dp")),
    )

    return jax.shard_map(
        on_device,
        mesh=mesh,
        in_specs=placed,
        out_specs=(
            P(("parts", "dp"), None, "tensor"),
            P(("parts", "dp"), None, None, "tensor", None),
        ),
        check_vma=False,
    )
```

profile of v0, /device:TPU:38, one launch (start us, length us, event | category | flops | bytes accessed | tf_op | source)
XLA Modules:
  0.0 222.2 jit_solution(1424166302234147373)
XLA Ops:
  1.4 1.0 constant_dynamic-slice_fusion
  3.5 4.4 %collective-permute-start.1 = (bf16[64,896]{1,0:T(8,128)(2,1)S(1)}, bf16[64,896]{1,0:T(8,128)(2,1)S(1)}, u32[]{:S(2)}, u32[]{:S(2)}) collective-permute-start(bf16[64,896]{1,0:T(8,128)(2,1)S(1)} %get-tuple-element.93), channel_id=1, source_target_pairs={{0,0},{1,64},{2,2},{3,66},{4,4},{5,68},{6,6},{7,70},{8,8},{9,72},{... | collective-permute-start | bytes 344072 | tf_op jit(solution)/shard_map/ppermute | solution.py:26
  7.9 1.0 collective-permute-done
  8.9 2.2 %collective-permute-done.1 = bf16[64,896]{1,0:T(8,128)(2,1)S(1)} collective-permute-done((bf16[64,896]{1,0:T(8,128)(2,1)S(1)}, bf16[64,896]{1,0:T(8,128)(2,1)S(1)}, u32[]{:S(2)}, u32[]{:S(2)}) %collective-permute-start.1) | collective-permute-done | bytes 114720 | tf_op jit(solution)/shard_map/ppermute | solution.py:26
  11.9 1.6 pad_maximum_fusion
  13.5 2.8 %collective-permute-start.2 = (bf16[64,2560]{1,0:T(8,128)(2,1)}, bf16[64,2560]{1,0:T(8,128)(2,1)}, u32[]{:S(2)}, u32[]{:S(2)}) collective-permute-start(bf16[64,2560]{1,0:T(8,128)(2,1)} %pad_maximum_fusion), channel_id=1, source_target_pairs={{0,2},{1,3},{2,4},{3,5},{4,6},{5,7},{6,8},{7,9},{8,10},{9,11},{10,... | collective-permute-start | bytes 983048 | tf_op jit(solution)/shard_map/ppermute | solution.py:26
  16.3 19.6 %collective-permute-start.3 = (bf16[64,2560]{1,0:T(8,128)(2,1)}, bf16[64,2560]{1,0:T(8,128)(2,1)}, u32[]{:S(2)}, u32[]{:S(2)}) collective-permute-start(bf16[64,2560]{1,0:T(8,128)(2,1)} %pad_maximum_fusion), channel_id=1, source_target_pairs={{0,30},{1,31},{2,0},{3,1},{4,2},{5,3},{6,4},{7,5},{8,6},{9,7},{10,... | collective-permute-start | bytes 983048 | tf_op jit(solution)/shard_map/ppermute | solution.py:26
  35.9 1.7 broadcast_in_dim.170
  39.1 2.1 collective-permute-done.2
  42.1 2.0 collective-permute-start.5
  44.1 3.2 %collective-permute-start.9 = (bf16[64,2560]{1,0:T(8,128)(2,1)}, bf16[64,2560]{1,0:T(8,128)(2,1)S(1)}, u32[]{:S(2)}, u32[]{:S(2)}) collective-permute-start(bf16[64,2560]{1,0:T(8,128)(2,1)} %collective-permute-done.3), channel_id=1, source_target_pairs={{0,30},{1,31},{2,0},{3,1},{4,2},{5,3},{6,4},{7,5},{8,6},{9,7},{10,... | collective-permute-start | bytes 983048 | tf_op jit(solution)/shard_map/ppermute | solution.py:26
  47.4 0.9 bitcast_dynamic-update-slice_fusion.17
  48.3 0.9 bitcast_dynamic-update-slice_fusion.16
  49.3 1.6 bitcast_dynamic-update-slice_fusion.32
  50.8 1.6 bitcast_dynamic-update-slice_fusion.31
  52.4 2.9 %collective-permute-done.8 = bf16[64,2560]{1,0:T(8,128)(2,1)S(1)} collective-permute-done((bf16[64,2560]{1,0:T(8,128)(2,1)}, bf16[64,2560]{1,0:T(8,128)(2,1)S(1)}, u32[]{:S(2)}, u32[]{:S(2)}) %collective-permute-start.8) | collective-permute-done | bytes 327712 | tf_op jit(solution)/shard_map/ppermute | solution.py:26
  55.3 3.2 %collective-permute-start.11 = (bf16[64,2560]{1,0:T(8,128)(2,1)S(1)}, bf16[64,2560]{1,0:T(8,128)(2,1)S(1)}, u32[]{:S(2)}, u32[]{:S(2)}) collective-permute-start(bf16[64,2560]{1,0:T(8,128)(2,1)S(1)} %collective-permute-done.9), channel_id=1, source_target_pairs={{0,30},{1,31},{2,0},{3,1},{4,2},{5,3},{6,4},{7,5},{8,6},{9,7},{10,... | collective-permute-start | bytes 983048 | tf_op jit(solution)/shard_map/ppermute | solution.py:26
  59.9 5.5 %collective-permute-done.10 = bf16[64,2560]{1,0:T(8,128)(2,1)S(1)} collective-permute-done((bf16[64,2560]{1,0:T(8,128)(2,1)S(1)}, bf16[64,2560]{1,0:T(8,128)(2,1)S(1)}, u32[]{:S(2)}, u32[]{:S(2)}) %collective-permute-start.10) | collective-permute-done | bytes 327712 | tf_op jit(solution)/shard_map/ppermute | solution.py:26
  65.4 3.2 %collective-permute-start.13 = (bf16[64,2560]{1,0:T(8,128)(2,1)S(1)}, bf16[64,2560]{1,0:T(8,128)(2,1)S(1)}, u32[]{:S(2)}, u32[]{:S(2)}) collective-permute-start(bf16[64,2560]{1,0:T(8,128)(2,1)S(1)} %collective-permute-done.11), channel_id=1, source_target_pairs={{0,30},{1,31},{2,0},{3,1},{4,2},{5,3},{6,4},{7,5},{8,6},{9,7},{10,... | collective-permute-start | bytes 983048 | tf_op jit(solution)/shard_map/ppermute | solution.py:26
  70.0 4.6 %collective-permute-done.12 = bf16[64,2560]{1,0:T(8,128)(2,1)S(1)} collective-permute-done((bf16[64,2560]{1,0:T(8,128)(2,1)S(1)}, bf16[64,2560]{1,0:T(8,128)(2,1)S(1)}, u32[]{:S(2)}, u32[]{:S(2)}) %collective-permute-start.12) | collective-permute-done | bytes 327712 | tf_op jit(solution)/shard_map/ppermute | solution.py:26
  74.7 3.2 %collective-permute-start.15 = (bf16[64,2560]{1,0:T(8,128)(2,1)S(1)}, bf16[64,2560]{1,0:T(8,128)(2,1)S(1)}, u32[]{:S(2)}, u32[]{:S(2)}) collective-permute-start(bf16[64,2560]{1,0:T(8,128)(2,1)S(1)} %collective-permute-done.13), channel_id=1, source_target_pairs={{0,30},{1,31},{2,0},{3,1},{4,2},{5,3},{6,4},{7,5},{8,6},{9,7},{10,... | collective-permute-start | bytes 983048 | tf_op jit(solution)/shard_map/ppermute | solution.py:26
  79.4 5.0 %collective-permute-start.6 = (bf16[128,2048]{1,0:T(8,128)(2,1)S(1)}, bf16[128,2048]{1,0:T(8,128)(2,1)S(1)}, u32[]{:S(2)}, u32[]{:S(2)}) collective-permute-start(bf16[128,2048]{1,0:T(8,128)(2,1)S(1)} %slice.186), channel_id=1, source_target_pairs={{0,32},{1,33},{2,34},{3,35},{4,36},{5,37},{6,38},{7,39},{8,40},{9,... | collective-permute-start | bytes 1572872 | tf_op jit(solution)/shard_map/ppermute | solution.py:26
  84.9 3.2 %collective-permute-start.17 = (bf16[64,2560]{1,0:T(8,128)(2,1)S(1)}, bf16[64,2560]{1,0:T(8,128)(2,1)S(1)}, u32[]{:S(2)}, u32[]{:S(2)}) collective-permute-start(bf16[64,2560]{1,0:T(8,128)(2,1)S(1)} %collective-permute-done.15), channel_id=1, source_target_pairs={{0,30},{1,31},{2,0},{3,1},{4,2},{5,3},{6,4},{7,5},{8,6},{9,7},{10,... | collective-permute-start | bytes 983048 | tf_op jit(solution)/shard_map/ppermute | solution.py:26
  89.5 4.8 %collective-permute-done.6 = bf16[128,2048]{1,0:T(8,128)(2,1)S(1)} collective-permute-done((bf16[128,2048]{1,0:T(8,128)(2,1)S(1)}, bf16[128,2048]{1,0:T(8,128)(2,1)S(1)}, u32[]{:S(2)}, u32[]{:S(2)}) %collective-permute-start.6) | collective-permute-done | bytes 524320 | tf_op jit(solution)/shard_map/ppermute | solution.py:26
  94.4 3.5 %collective-permute-done.7 = bf16[128,2048]{1,0:T(8,128)(2,1)S(1)} collective-permute-done((bf16[128,2048]{1,0:T(8,128)(2,1)S(1)}, bf16[128,2048]{1,0:T(8,128)(2,1)S(1)}, u32[]{:S(2)}, u32[]{:S(2)}) %collective-permute-start.7) | collective-permute-done | bytes 524320 | tf_op jit(solution)/shard_map/ppermute | solution.py:26
  98.1 3.2 %collective-permute-start.19 = (bf16[64,2560]{1,0:T(8,128)(2,1)S(1)}, bf16[64,2560]{1,0:T(8,128)(2,1)S(1)}, u32[]{:S(2)}, u32[]{:S(2)}) collective-permute-start(bf16[64,2560]{1,0:T(8,128)(2,1)S(1)} %collective-permute-done.17), channel_id=1, source_target_pairs={{0,30},{1,31},{2,0},{3,1},{4,2},{5,3},{6,4},{7,5},{8,6},{9,7},{10,... | collective-permute-start | bytes 983048 | tf_op jit(solution)/shard_map/ppermute | solution.py:26
  102.7 3.7 %collective-permute-done.18 = bf16[64,2560]{1,0:T(8,128)(2,1)S(1)} collective-permute-done((bf16[64,2560]{1,0:T(8,128)(2,1)S(1)}, bf16[64,2560]{1,0:T(8,128)(2,1)S(1)}, u32[]{:S(2)}, u32[]{:S(2)}) %collective-permute-start.18) | collective-permute-done | bytes 327712 | tf_op jit(solution)/shard_map/ppermute | solution.py:26
  106.6 3.3 %collective-permute-start.21 = (bf16[32,2560]{1,0:T(8,128)(2,1)S(1)}, bf16[32,2560]{1,0:T(8,128)(2,1)S(1)}, u32[]{:S(2)}, u32[]{:S(2)}) collective-permute-start(bf16[32,2560]{1,0:T(8,128)(2,1)S(1)} %slice.173), channel_id=1, source_target_pairs={{0,30},{1,31},{2,0},{3,1},{4,2},{5,3},{6,4},{7,5},{8,6},{9,7},{10,... | collective-permute-start | bytes 491528 | tf_op jit(solution)/shard_map/ppermute | solution.py:26
  110.0 3.1 %collective-permute-done.20 = bf16[32,2560]{1,0:T(8,128)(2,1)S(1)} collective-permute-done((bf16[32,2560]{1,0:T(8,128)(2,1)S(1)}, bf16[32,2560]{1,0:T(8,128)(2,1)S(1)}, u32[]{:S(2)}, u32[]{:S(2)}) %collective-permute-start.20) | collective-permute-done | bytes 163872 | tf_op jit(solution)/shard_map/ppermute | solution.py:26
  113.1 4.5 %project_in.3 = f32[2,256,768]{2,1,0:T(8,128)} custom-call(s32[1]{0:T(128)} %bitcast.43.pair_ref, bf16[4,256,2048]{2,1,0:T(8,128)(2,1)S(1)} %bitcast_dynamic-update-slice_fusion.2.x_ref, bf16[16,64,1536]{2,1,0:T(8,128)(2,1)S(1)} %fusion.1.w_ref), custom_call_target="tpu_custom_call" | custom-call | tf_op jit(solution)/shard_map/project_in/pallas_call | solution.py:53
  120.8 2.2 copy-done.1
  123.0 3.3 %project_in.2.a_ref = f32[2,256,768]{2,1,0:T(8,128)S(1)} custom-call(s32[1]{0:T(128)} %bitcast.1.pair_ref, bf16[4,256,2048]{2,1,0:T(8,128)(2,1)S(1)} %copy-done.1, bf16[16,64,1536]{2,1,0:T(8,128)(2,1)S(1)} %fusion.1.w_ref), custom_call_target="tpu_custom_call" | custom-call | tf_op jit(solution)/shard_map/project_in/pallas_call | solution.py:53
  126.3 3.8 %attend.1 = (bf16[512,512]{1,0:T(8,128)(2,1)S(1)}, bf16[2,2,256,128]{3,2,1,0:T(8,128)(2,1)S(1)}) custom-call(f32[2,256,768]{2,1,0:T(8,128)S(1)} %project_in.2.a_ref, f32[2,256,768]{2,1,0:T(8,128)} %collective-permute-done.22.b_ref, bf16[64,896]{1,0:T(8,128)(2,1)S(1)} %get-tuple-element.84.l0_ref, bf16[64,896]{1,0:T(8,128)(2,1)S(1)} %get-tuple-element.85.l1_ref, ...), custom_call_target="tpu_custom_call" | custom-call | tf_op jit(solution)/shard_map/attend/pallas_call | solution.py:119
  131.9 0.9 concatenate.34.clone
  132.8 11.0 %all-to-all-start = ((bf16[64,5,512]{2,1,0:T(8,128)(2,1)}), bf16[64,5,512]{2,1,0:T(8,128)(2,1)S(1)}, u32[]{:S(2)}, u32[]{:S(2)}) async-start(bf16[64,5,512]{2,1,0:T(8,128)(2,1)} %concatenate.34.clone), calls=%async_computation | async-start | bytes 1048576 | tf_op jit(solution)/shard_map/all_to_all | solution.py:281
  144.6 1.3 collective-permute-start.23
  145.9 14.8 %collective-permute-done.24.a4 = bf16[512,512]{1,0:T(8,128)(2,1)S(1)} collective-permute-done((bf16[512,512]{1,0:T(8,128)(2,1)S(1)}, bf16[512,512]{1,0:T(8,128)(2,1)S(1)}, u32[]{:S(2)}, u32[]{:S(2)}) %collective-permute-start.24) | collective-permute-done | bytes 524320 | tf_op jit(solution)/shard_map/ppermute | solution.py:26
  160.7 2.2 collective-permute-start.25
  163.1 5.7 %collective-permute-done.25.a2 = bf16[256,512]{1,0:T(8,128)(2,1)S(1)} collective-permute-done((bf16[256,512]{1,0:T(8,128)(2,1)S(1)}, bf16[256,512]{1,0:T(8,128)(2,1)S(1)}, u32[]{:S(2)}, u32[]{:S(2)}) %collective-permute-start.25) | collective-permute-done | bytes 262176 | tf_op jit(solution)/shard_map/ppermute | solution.py:26
  168.8 3.2 %collective-permute-done.26.a3 = bf16[256,512]{1,0:T(8,128)(2,1)S(1)} collective-permute-done((bf16[256,512]{1,0:T(8,128)(2,1)S(1)}, bf16[256,512]{1,0:T(8,128)(2,1)S(1)}, u32[]{:S(2)}, u32[]{:S(2)}) %collective-permute-start.26) | collective-permute-done | bytes 262176 | tf_op jit(solution)/shard_map/ppermute | solution.py:26
  172.0 5.0 %project_out.1 = bf16[512,1024]{1,0:T(8,128)(2,1)S(1)} custom-call(s32[1]{0:T(128)} %bitcast.shift_ref, bf16[512,512]{1,0:T(8,128)(2,1)S(1)} %get-tuple-element.63.a0, bf16[512,512]{1,0:T(8,128)(2,1)S(1)} %collective-permute-done.23.a1, bf16[256,512]{1,0:T(8,128)(2,1)S(1)} %collective-permute-done.25.a2, bf16[256,512]{1,0:T(8,128)(2,1)S(1)} %collective-permute-done.26.a3, ...), custom_call_target="tpu_custom_call" | custom-call | tf_op jit(solution)/shard_map/project_out/pallas_call | solution.py:165
  177.8 3.5 %collective-permute-start.29 = (bf16[256,1024]{1,0:T(8,128)(2,1)S(1)}, bf16[256,1024]{1,0:T(8,128)(2,1)S(1)}, u32[]{:S(2)}, u32[]{:S(2)}) collective-permute-start(bf16[256,1024]{1,0:T(8,128)(2,1)S(1)} %get-tuple-element.81), channel_id=1, source_target_pairs={{0,0},{1,64},{2,2},{3,66},{4,4},{5,68},{6,6},{7,70},{8,8},{9,72},{... | collective-permute-start | bytes 1572872 | tf_op jit(solution)/shard_map/ppermute | solution.py:26
  181.3 1.2 fusion.5
  183.2 1.2 gather_fusion
  184.6 0.9 broadcast_select_fusion.2
  185.5 17.6 %all-to-all-start.1 = ((bf16[64,4,512]{2,1,0:T(4,128)(2,1)}), bf16[64,4,512]{2,1,0:T(4,128)(2,1)S(1)}, u32[]{:S(2)}, u32[]{:S(2)}) async-start(bf16[64,4,512]{2,1,0:T(4,128)(2,1)} %broadcast_select_fusion.2), calls=%async_computation.1 | async-start | bytes 524288 | tf_op jit(solution)/shard_map/all_to_all | solution.py:292
  203.2 1.1 maximum_bitcast_fusion
  204.3 17.0 %all-to-all-done.1 = bf16[64,4,512]{2,1,0:T(4,128)(2,1)S(1)} async-done(((bf16[64,4,512]{2,1,0:T(4,128)(2,1)}), bf16[64,4,512]{2,1,0:T(4,128)(2,1)S(1)}, u32[]{:S(2)}, u32[]{:S(2)}) %all-to-all-start.1) | async-done | bytes 262176 | tf_op jit(solution)/shard_map/all_to_all | solution.py:292
  (122 shorter events, 20.1 us)
Async XLA Ops:
  0.6 36.9 %copy-start.5 = (bf16[1024,64]{0,1:T(8,128)(2,1)S(1)}, bf16[1024,64]{0,1:T(8,128)(2,1)}, u32[]{:S(2)}) copy-start(bf16[1024,64]{0,1:T(8,128)(2,1)} %param.10) | copy-start | bytes 393220
  3.4 5.6 %collective-permute-start = (bf16[64,896]{1,0:T(8,128)(2,1)S(1)}, bf16[64,896]{1,0:T(8,128)(2,1)S(1)}, u32[]{:S(2)}, u32[]{:S(2)}) collective-permute-start(bf16[64,896]{1,0:T(8,128)(2,1)S(1)} %get-tuple-element.92), channel_id=1, source_target_pairs={{0,32},{1,96},{2,34},{3,98},{4,36},{5,100},{6,38},{7,102},{8,40},{... | collective-permute-start | bytes 344072 | tf_op jit(solution)/shard_map/ppermute | solution.py:26
  3.5 7.6 %collective-permute-start.1 = (bf16[64,896]{1,0:T(8,128)(2,1)S(1)}, bf16[64,896]{1,0:T(8,128)(2,1)S(1)}, u32[]{:S(2)}, u32[]{:S(2)}) collective-permute-start(bf16[64,896]{1,0:T(8,128)(2,1)S(1)} %get-tuple-element.93), channel_id=1, source_target_pairs={{0,0},{1,64},{2,2},{3,66},{4,4},{5,68},{6,6},{7,70},{8,8},{9,72},{... | collective-permute-start | bytes 344072 | tf_op jit(solution)/shard_map/ppermute | solution.py:26
  11.2 0.6 copy-start.3
  13.5 27.7 %collective-permute-start.2 = (bf16[64,2560]{1,0:T(8,128)(2,1)}, bf16[64,2560]{1,0:T(8,128)(2,1)}, u32[]{:S(2)}, u32[]{:S(2)}) collective-permute-start(bf16[64,2560]{1,0:T(8,128)(2,1)} %pad_maximum_fusion), channel_id=1, source_target_pairs={{0,2},{1,3},{2,4},{3,5},{4,6},{5,7},{6,8},{7,9},{8,10},{9,11},{10,... | collective-permute-start | bytes 983048 | tf_op jit(solution)/shard_map/ppermute | solution.py:26
  16.3 25.0 %collective-permute-start.3 = (bf16[64,2560]{1,0:T(8,128)(2,1)}, bf16[64,2560]{1,0:T(8,128)(2,1)}, u32[]{:S(2)}, u32[]{:S(2)}) collective-permute-start(bf16[64,2560]{1,0:T(8,128)(2,1)} %pad_maximum_fusion), channel_id=1, source_target_pairs={{0,30},{1,31},{2,0},{3,1},{4,2},{5,3},{6,4},{7,5},{8,6},{9,7},{10,... | collective-permute-start | bytes 983048 | tf_op jit(solution)/shard_map/ppermute | solution.py:26
  38.2 0.9 copy-start.4
  38.2 3.6 %copy-start.6 = (bf16[1,256,4096]{2,1,0:T(8,128)(2,1)S(1)}, bf16[1,256,4096]{2,1,0:T(8,128)(2,1)}, u32[]{:S(2)}) copy-start(bf16[1,256,4096]{2,1,0:T(8,128)(2,1)} %param.7) | copy-start | bytes 6291460
  42.0 37.3 %collective-permute-start.4 = (bf16[256,2048]{1,0:T(8,128)(2,1)S(1)}, bf16[256,2048]{1,0:T(8,128)(2,1)S(1)}, u32[]{:S(2)}, u32[]{:S(2)}) collective-permute-start(bf16[256,2048]{1,0:T(8,128)(2,1)S(1)} %get-tuple-element.76), channel_id=1, source_target_pairs={{0,32},{1,33},{2,34},{3,35},{4,36},{5,37},{6,38},{7,39},{8,40},{9,... | collective-permute-start | bytes 3145736 | tf_op jit(solution)/shard_map/ppermute | solution.py:26
  42.1 42.2 %collective-permute-start.5 = (bf16[256,2048]{1,0:T(8,128)(2,1)S(1)}, bf16[256,2048]{1,0:T(8,128)(2,1)S(1)}, u32[]{:S(2)}, u32[]{:S(2)}) collective-permute-start(bf16[256,2048]{1,0:T(8,128)(2,1)S(1)} %get-tuple-element.76), channel_id=1, source_target_pairs={{0,96},{1,97},{2,98},{3,99},{4,100},{5,101},{6,102},{7,103},{8,104... | collective-permute-start | bytes 3145736 | tf_op jit(solution)/shard_map/ppermute | solution.py:26
  44.1 11.2 %collective-permute-start.8 = (bf16[64,2560]{1,0:T(8,128)(2,1)}, bf16[64,2560]{1,0:T(8,128)(2,1)S(1)}, u32[]{:S(2)}, u32[]{:S(2)}) collective-permute-start(bf16[64,2560]{1,0:T(8,128)(2,1)} %collective-permute-done.2), channel_id=1, source_target_pairs={{0,2},{1,3},{2,4},{3,5},{4,6},{5,7},{6,8},{7,9},{8,10},{9,11},{10,... | collective-permute-start | bytes 983048 | tf_op jit(solution)/shard_map/ppermute | solution.py:26
  44.1 11.2 %collective-permute-start.9 = (bf16[64,2560]{1,0:T(8,128)(2,1)}, bf16[64,2560]{1,0:T(8,128)(2,1)S(1)}, u32[]{:S(2)}, u32[]{:S(2)}) collective-permute-start(bf16[64,2560]{1,0:T(8,128)(2,1)} %collective-permute-done.3), channel_id=1, source_target_pairs={{0,30},{1,31},{2,0},{3,1},{4,2},{5,3},{6,4},{7,5},{8,6},{9,7},{10,... | collective-permute-start | bytes 983048 | tf_op jit(solution)/shard_map/ppermute | solution.py:26
  55.3 10.1 %collective-permute-start.10 = (bf16[64,2560]{1,0:T(8,128)(2,1)S(1)}, bf16[64,2560]{1,0:T(8,128)(2,1)S(1)}, u32[]{:S(2)}, u32[]{:S(2)}) collective-permute-start(bf16[64,2560]{1,0:T(8,128)(2,1)S(1)} %collective-permute-done.8), channel_id=1, source_target_pairs={{0,2},{1,3},{2,4},{3,5},{4,6},{5,7},{6,8},{7,9},{8,10},{9,11},{10,... | collective-permute-start | bytes 983048 | tf_op jit(solution)/shard_map/ppermute | solution.py:26
  55.3 10.1 %collective-permute-start.11 = (bf16[64,2560]{1,0:T(8,128)(2,1)S(1)}, bf16[64,2560]{1,0:T(8,128)(2,1)S(1)}, u32[]{:S(2)}, u32[]{:S(2)}) collective-permute-start(bf16[64,2560]{1,0:T(8,128)(2,1)S(1)} %collective-permute-done.9), channel_id=1, source_target_pairs={{0,30},{1,31},{2,0},{3,1},{4,2},{5,3},{6,4},{7,5},{8,6},{9,7},{10,... | collective-permute-start | bytes 983048 | tf_op jit(solution)/shard_map/ppermute | solution.py:26
  65.4 9.3 %collective-permute-start.12 = (bf16[64,2560]{1,0:T(8,128)(2,1)S(1)}, bf16[64,2560]{1,0:T(8,128)(2,1)S(1)}, u32[]{:S(2)}, u32[]{:S(2)}) collective-permute-start(bf16[64,2560]{1,0:T(8,128)(2,1)S(1)} %collective-permute-done.10), channel_id=1, source_target_pairs={{0,2},{1,3},{2,4},{3,5},{4,6},{5,7},{6,8},{7,9},{8,10},{9,11},{10,... | collective-permute-start | bytes 983048 | tf_op jit(solution)/shard_map/ppermute | solution.py:26
  65.4 9.3 %collective-permute-start.13 = (bf16[64,2560]{1,0:T(8,128)(2,1)S(1)}, bf16[64,2560]{1,0:T(8,128)(2,1)S(1)}, u32[]{:S(2)}, u32[]{:S(2)}) collective-permute-start(bf16[64,2560]{1,0:T(8,128)(2,1)S(1)} %collective-permute-done.11), channel_id=1, source_target_pairs={{0,30},{1,31},{2,0},{3,1},{4,2},{5,3},{6,4},{7,5},{8,6},{9,7},{10,... | collective-permute-start | bytes 983048 | tf_op jit(solution)/shard_map/ppermute | solution.py:26
  74.7 10.1 %collective-permute-start.14 = (bf16[64,2560]{1,0:T(8,128)(2,1)S(1)}, bf16[64,2560]{1,0:T(8,128)(2,1)S(1)}, u32[]{:S(2)}, u32[]{:S(2)}) collective-permute-start(bf16[64,2560]{1,0:T(8,128)(2,1)S(1)} %collective-permute-done.12), channel_id=1, source_target_pairs={{0,2},{1,3},{2,4},{3,5},{4,6},{5,7},{6,8},{7,9},{8,10},{9,11},{10,... | collective-permute-start | bytes 983048 | tf_op jit(solution)/shard_map/ppermute | solution.py:26
  74.7 10.1 %collective-permute-start.15 = (bf16[64,2560]{1,0:T(8,128)(2,1)S(1)}, bf16[64,2560]{1,0:T(8,128)(2,1)S(1)}, u32[]{:S(2)}, u32[]{:S(2)}) collective-permute-start(bf16[64,2560]{1,0:T(8,128)(2,1)S(1)} %collective-permute-done.13), channel_id=1, source_target_pairs={{0,30},{1,31},{2,0},{3,1},{4,2},{5,3},{6,4},{7,5},{8,6},{9,7},{10,... | collective-permute-start | bytes 983048 | tf_op jit(solution)/shard_map/ppermute | solution.py:26
  79.4 15.0 %collective-permute-start.6 = (bf16[128,2048]{1,0:T(8,128)(2,1)S(1)}, bf16[128,2048]{1,0:T(8,128)(2,1)S(1)}, u32[]{:S(2)}, u32[]{:S(2)}) collective-permute-start(bf16[128,2048]{1,0:T(8,128)(2,1)S(1)} %slice.186), channel_id=1, source_target_pairs={{0,32},{1,33},{2,34},{3,35},{4,36},{5,37},{6,38},{7,39},{8,40},{9,... | collective-permute-start | bytes 1572872 | tf_op jit(solution)/shard_map/ppermute | solution.py:26
  84.4 13.5 %collective-permute-start.7 = (bf16[128,2048]{1,0:T(8,128)(2,1)S(1)}, bf16[128,2048]{1,0:T(8,128)(2,1)S(1)}, u32[]{:S(2)}, u32[]{:S(2)}) collective-permute-start(bf16[128,2048]{1,0:T(8,128)(2,1)S(1)} %slice.187), channel_id=1, source_target_pairs={{0,96},{1,97},{2,98},{3,99},{4,100},{5,101},{6,102},{7,103},{8,104... | collective-permute-start | bytes 1572872 | tf_op jit(solution)/shard_map/ppermute | solution.py:26
  84.8 13.2 %collective-permute-start.16 = (bf16[64,2560]{1,0:T(8,128)(2,1)S(1)}, bf16[64,2560]{1,0:T(8,128)(2,1)S(1)}, u32[]{:S(2)}, u32[]{:S(2)}) collective-permute-start(bf16[64,2560]{1,0:T(8,128)(2,1)S(1)} %collective-permute-done.14), channel_id=1, source_target_pairs={{0,2},{1,3},{2,4},{3,5},{4,6},{5,7},{6,8},{7,9},{8,10},{9,11},{10,... | collective-permute-start | bytes 983048 | tf_op jit(solution)/shard_map/ppermute | solution.py:26
  84.9 13.1 %collective-permute-start.17 = (bf16[64,2560]{1,0:T(8,128)(2,1)S(1)}, bf16[64,2560]{1,0:T(8,128)(2,1)S(1)}, u32[]{:S(2)}, u32[]{:S(2)}) collective-permute-start(bf16[64,2560]{1,0:T(8,128)(2,1)S(1)} %collective-permute-done.15), channel_id=1, source_target_pairs={{0,30},{1,31},{2,0},{3,1},{4,2},{5,3},{6,4},{7,5},{8,6},{9,7},{10,... | collective-permute-start | bytes 983048 | tf_op jit(solution)/shard_map/ppermute | solution.py:26
  98.0 19.7 %copy-start = (bf16[4,256,2048]{2,1,0:T(8,128)(2,1)}, bf16[4,256,2048]{2,1,0:T(8,128)(2,1)S(1)}, u32[]{:S(2)}) copy-start(bf16[4,256,2048]{2,1,0:T(8,128)(2,1)S(1)} %bitcast_dynamic-update-slice_fusion.2.x_ref) | copy-start | bytes 12582916
  98.0 8.4 %collective-permute-start.18 = (bf16[64,2560]{1,0:T(8,128)(2,1)S(1)}, bf16[64,2560]{1,0:T(8,128)(2,1)S(1)}, u32[]{:S(2)}, u32[]{:S(2)}) collective-permute-start(bf16[64,2560]{1,0:T(8,128)(2,1)S(1)} %collective-permute-done.16), channel_id=1, source_target_pairs={{0,2},{1,3},{2,4},{3,5},{4,6},{5,7},{6,8},{7,9},{8,10},{9,11},{10,... | collective-permute-start | bytes 983048 | tf_op jit(solution)/shard_map/ppermute | solution.py:26
  98.1 8.3 %collective-permute-start.19 = (bf16[64,2560]{1,0:T(8,128)(2,1)S(1)}, bf16[64,2560]{1,0:T(8,128)(2,1)S(1)}, u32[]{:S(2)}, u32[]{:S(2)}) collective-permute-start(bf16[64,2560]{1,0:T(8,128)(2,1)S(1)} %collective-permute-done.17), channel_id=1, source_target_pairs={{0,30},{1,31},{2,0},{3,1},{4,2},{5,3},{6,4},{7,5},{8,6},{9,7},{10,... | collective-permute-start | bytes 983048 | tf_op jit(solution)/shard_map/ppermute | solution.py:26
  106.5 6.6 %collective-permute-start.20 = (bf16[32,2560]{1,0:T(8,128)(2,1)S(1)}, bf16[32,2560]{1,0:T(8,128)(2,1)S(1)}, u32[]{:S(2)}, u32[]{:S(2)}) collective-permute-start(bf16[32,2560]{1,0:T(8,128)(2,1)S(1)} %slice.171), channel_id=1, source_target_pairs={{0,2},{1,3},{2,4},{3,5},{4,6},{5,7},{6,8},{7,9},{8,10},{9,11},{10,... | collective-permute-start | bytes 491528 | tf_op jit(solution)/shard_map/ppermute | solution.py:26
  106.6 6.5 %collective-permute-start.21 = (bf16[32,2560]{1,0:T(8,128)(2,1)S(1)}, bf16[32,2560]{1,0:T(8,128)(2,1)S(1)}, u32[]{:S(2)}, u32[]{:S(2)}) collective-permute-start(bf16[32,2560]{1,0:T(8,128)(2,1)S(1)} %slice.173), channel_id=1, source_target_pairs={{0,30},{1,31},{2,0},{3,1},{4,2},{5,3},{6,4},{7,5},{8,6},{9,7},{10,... | collective-permute-start | bytes 491528 | tf_op jit(solution)/shard_map/ppermute | solution.py:26
  117.6 8.7 %collective-permute-start.22 = (f32[2,256,768]{2,1,0:T(8,128)}, f32[2,256,768]{2,1,0:T(8,128)}, u32[]{:S(2)}, u32[]{:S(2)}) collective-permute-start(f32[2,256,768]{2,1,0:T(8,128)} %project_in.3), channel_id=1, source_target_pairs={{0,1},{1,0},{2,3},{3,2},{4,5},{5,4},{6,7},{7,6},{8,9},{9,8},{10,11... | collective-permute-start | bytes 4718600 | tf_op jit(solution)/shard_map/ppermute | solution.py:26
  120.3 42.8 %collective-permute-start.27 = (bf16[1024,1024]{1,0:T(8,128)(2,1)}, bf16[1024,1024]{1,0:T(8,128)(2,1)}, u32[]{:S(2)}, u32[]{:S(2)}) collective-permute-start(bf16[1024,1024]{1,0:T(8,128)(2,1)} %bitcast.48.near_ref), channel_id=1, source_target_pairs={{0,1},{1,0},{2,3},{3,2},{4,5},{5,4},{6,7},{7,6},{8,9},{9,8},{10,11... | collective-permute-start | bytes 6291464 | tf_op jit(solution)/shard_map/ppermute | solution.py:26
  120.8 2.2 copy-start.1
  123.0 3.4 %copy-start.2 = (f32[256,128]{1,0:T(8,128)S(1)}, f32[256,128]{1,0:T(8,128)}, u32[]{:S(2)}) copy-start(f32[256,128]{1,0:T(8,128)} %constant.259.clone.turn_ref) | copy-start | bytes 393220
  130.1 1.5 collective-permute-start.30
  132.8 48.5 %all-to-all-start = ((bf16[64,5,512]{2,1,0:T(8,128)(2,1)}), bf16[64,5,512]{2,1,0:T(8,128)(2,1)S(1)}, u32[]{:S(2)}, u32[]{:S(2)}) async-start(bf16[64,5,512]{2,1,0:T(8,128)(2,1)} %concatenate.34.clone), calls=%async_computation | async-start | bytes 1048576 | tf_op jit(solution)/shard_map/all_to_all | solution.py:281
  143.8 16.9 %collective-permute-start.24 = (bf16[512,512]{1,0:T(8,128)(2,1)S(1)}, bf16[512,512]{1,0:T(8,128)(2,1)S(1)}, u32[]{:S(2)}, u32[]{:S(2)}) collective-permute-start(bf16[512,512]{1,0:T(8,128)(2,1)S(1)} %get-tuple-element.63.a0), channel_id=1, source_target_pairs={{0,32},{1,33},{2,34},{3,35},{4,36},{5,37},{6,38},{7,39},{8,40},{9,... | collective-permute-start | bytes 1572872 | tf_op jit(solution)/shard_map/ppermute | solution.py:26
  144.6 18.3 %collective-permute-start.23 = (bf16[512,512]{1,0:T(8,128)(2,1)S(1)}, bf16[512,512]{1,0:T(8,128)(2,1)S(1)}, u32[]{:S(2)}, u32[]{:S(2)}) collective-permute-start(bf16[512,512]{1,0:T(8,128)(2,1)S(1)} %get-tuple-element.63.a0), channel_id=1, source_target_pairs={{0,96},{1,97},{2,98},{3,99},{4,100},{5,101},{6,102},{7,103},{8,104... | collective-permute-start | bytes 1572872 | tf_op jit(solution)/shard_map/ppermute | solution.py:26
  160.7 8.1 %collective-permute-start.25 = (bf16[256,512]{1,0:T(8,128)(2,1)S(1)}, bf16[256,512]{1,0:T(8,128)(2,1)S(1)}, u32[]{:S(2)}, u32[]{:S(2)}) collective-permute-start(bf16[256,512]{1,0:T(8,128)(2,1)S(1)} %slice.190), channel_id=1, source_target_pairs={{0,32},{1,33},{2,34},{3,35},{4,36},{5,37},{6,38},{7,39},{8,40},{9,... | collective-permute-start | bytes 786440 | tf_op jit(solution)/shard_map/ppermute | solution.py:26
  162.9 9.1 %collective-permute-start.26 = (bf16[256,512]{1,0:T(8,128)(2,1)S(1)}, bf16[256,512]{1,0:T(8,128)(2,1)S(1)}, u32[]{:S(2)}, u32[]{:S(2)}) collective-permute-start(bf16[256,512]{1,0:T(8,128)(2,1)S(1)} %slice.191), channel_id=1, source_target_pairs={{0,96},{1,97},{2,98},{3,99},{4,100},{5,101},{6,102},{7,103},{8,104... | collective-permute-start | bytes 786440 | tf_op jit(solution)/shard_map/ppermute | solution.py:26
  177.8 25.3 %collective-permute-start.28 = (bf16[256,1024]{1,0:T(8,128)(2,1)}, bf16[256,1024]{1,0:T(8,128)(2,1)S(1)}, u32[]{:S(2)}, u32[]{:S(2)}) collective-permute-start(bf16[256,1024]{1,0:T(8,128)(2,1)} %get-tuple-element.80), channel_id=1, source_target_pairs={{0,32},{1,96},{2,34},{3,98},{4,36},{5,100},{6,38},{7,102},{8,40},{... | collective-permute-start | bytes 1572872 | tf_op jit(solution)/shard_map/ppermute | solution.py:26
  177.8 25.3 %collective-permute-start.29 = (bf16[256,1024]{1,0:T(8,128)(2,1)S(1)}, bf16[256,1024]{1,0:T(8,128)(2,1)S(1)}, u32[]{:S(2)}, u32[]{:S(2)}) collective-permute-start(bf16[256,1024]{1,0:T(8,128)(2,1)S(1)} %get-tuple-element.81), channel_id=1, source_target_pairs={{0,0},{1,64},{2,2},{3,66},{4,4},{5,68},{6,6},{7,70},{8,8},{9,72},{... | collective-permute-start | bytes 1572872 | tf_op jit(solution)/shard_map/ppermute | solution.py:26
  185.5 35.8 %all-to-all-start.1 = ((bf16[64,4,512]{2,1,0:T(4,128)(2,1)}), bf16[64,4,512]{2,1,0:T(4,128)(2,1)S(1)}, u32[]{:S(2)}, u32[]{:S(2)}) async-start(bf16[64,4,512]{2,1,0:T(4,128)(2,1)} %broadcast_select_fusion.2), calls=%async_computation.1 | async-start | bytes 524288 | tf_op jit(solution)/shard_map/all_to_all | solution.py:292
where the time goes:
time: 223 us; the launch traced here: 222 us
  starting transfers between devices  94.4 us (42%)
  waiting for transfers between devices  74.8 us (34%)
  local copies, waits for them, and re-layouts  28.4 us (13%)
  Pallas kernels  16.5 us (7%)
  other arithmetic  5.32 us (2%)
  between operations  2.72 us (1%)
    ppermute x31, starting transfers between devices, move(): return lax.ppermute(array, ('dp', 'tensor'), pairs)  65.8 us
    ppermute x31, waiting for transfers between devices, move(): return lax.ppermute(array, ('dp', 'tensor'), pairs)  57.8 us
    all_to_all x1, starting transfers between devices, on_device(): lax.all_to_all(outgoing.reshape(count, X, -1), 'dp', split_axis=0, concat...  17.6 us
    all_to_all x1, waiting for transfers between devices, on_device(): lax.all_to_all(outgoing.reshape(count, X, -1), 'dp', split_axis=0, concat...  17 us
    dynamic_update_slice x17, local copies, waits for them, and re-layouts, place(): lax.dynamic_update_slice(full[1], block[None, :, 2 * wide:], at)  13.1 us
    all_to_all x1, starting transfers between devices, on_device(): lax.all_to_all(jnp.concatenate([flat, label], axis=1), 'dp', 0, 0, tiled=...  11 us
    pallas_call x2, Pallas kernels, project_in(): pl.pallas_call(project_kernel, grid_spec=pltpu.PrefetchScalarGridSpec(num...  7.83 us
    pallas_call x1, Pallas kernels, project_out(): pl.pallas_call(output_kernel, grid_spec=pltpu.PrefetchScalarGridSpec(num_...  4.96 us
  transfers between devices with their start and end apart: 33, of which 15 were waited for; matrix products, arithmetic and copies ran while one was open for 11% of the time, Pallas kernels for 5%

commit v1 on v0

v1 whole, which is shorter than its diff:
```python
import functools
import math

import jax
import jax.numpy as jnp
import numpy as np
from jax import lax
from jax.experimental import pallas as pl
from jax.experimental.pallas import tpu as pltpu
from jax.sharding import Mesh
from jax.sharding import PartitionSpec as P

HD = 128
ROPE_BASE = 500000.0
START = 2
X = 4


def mover(ring):
    def move(array, where):
        pairs = []
        for x in range(X):
            for z in range(ring):
                for t in range(2):
                    a, b, c = where(x, z, t)
                    target = ((a % X) * ring + b % ring) * 2 + c
                    pairs.append(((x * ring + z) * 2 + t, target))
        return lax.ppermute(array, ("x", "z", "tensor"), pairs)

    return move


def project_kernel(pair_ref, x_ref, w_ref, out_ref):
    slots, total, depth = x_ref.shape
    weights = w_ref[...].reshape(depth, w_ref.shape[2])
    product = jnp.dot(
        x_ref[...].reshape(slots * total, depth), weights, preferred_element_type=jnp.float32
    ).reshape(slots, total, -1)
    width = weights.shape[1]
    columns = pl.ds(pl.multiple_of(pl.program_id(1) * width, width), width)

    @pl.when(pl.program_id(0) == 0)
    def _():
        out_ref[:, :, columns] = product

    @pl.when(pl.program_id(0) > 0)
    def _():
        out_ref[:, :, columns] += product


def project_in(states, weights, pair, first, pieces):
    _, total, half = states.shape
    ring, rows, both = weights.shape
    width = 2 * HD
    jump = both // 2 // width
    return pl.pallas_call(
        project_kernel,
        grid_spec=pltpu.PrefetchScalarGridSpec(
            num_scalar_prefetch=1,
            grid=(2, pieces),
            in_specs=[
                pl.BlockSpec((2, total, half // 2), lambda b, n, p: (p[0], 0, b)),
                pl.BlockSpec((ring, rows, width), lambda b, n, p: (0, 0, b * jump + first + n)),
            ],
            out_specs=pl.BlockSpec((2, total, pieces * width), lambda b, n, p: (0, 0, 0)),
        ),
        out_shape=jax.ShapeDtypeStruct((2, total, pieces * width), jnp.float32),
        compiler_params=pltpu.CompilerParams(vmem_limit_bytes=24 << 20),
        name="project_in",
    )(pair.reshape(1), states, weights)


def turned(values, turn_ref):
    cosine = jnp.concatenate([turn_ref[:, : HD // 2]] * 2, axis=1)
    sine = jnp.concatenate([-turn_ref[:, HD // 2 :], turn_ref[:, HD // 2 :]], axis=1)
    swapped = pltpu.roll(values, HD // 2, 1)
    return (values * cosine + swapped * sine).astype(jnp.bfloat16)


def length_of(slot, first_ref, second_ref):
    note = jnp.where(slot == 0, first_ref[:1, :1], second_ref[:1, :1])
    return note.astype(jnp.float32).astype(jnp.int32)


def cache_kernel(a_ref, b_ref, n0_ref, n1_ref, turn_ref, keys_ref, values_ref, sent_ref):
    slot = pl.program_id(0)
    length = length_of(slot, n0_ref, n1_ref)
    total = a_ref.shape[1]
    sums = a_ref[0] + b_ref[0]
    keys = turned(sums[:, :HD], turn_ref)
    values = sums[:, HD:].astype(jnp.bfloat16)
    keys_ref[0] = keys
    values_ref[0] = values
    live = lax.broadcasted_iota(jnp.int32, (total, HD), 0) < length
    zero = jnp.zeros((), jnp.bfloat16)
    ring, cores, _, piece, _ = sent_ref.shape
    count = ring // 2
    for index, array in enumerate((keys, values)):
        kept = jnp.where(live, array, zero).reshape(cores, count, piece, HD)
        for core in range(cores):
            sent_ref[index * count : (index + 1) * count, core, slot] = kept[core]

    @pl.when(slot == 0)
    def _():
        lane = lax.broadcasted_iota(jnp.int32, (piece, HD), 1)
        half = HD // 2
        label = jnp.where(lane == 0, n0_ref[:1, half : half + 1], n1_ref[:1, half : half + 1])
        sent_ref[:, :, 2] = jnp.broadcast_to(label, (ring, cores, piece, HD))


def make_cache(kept, other, first, second, ring):
    _, total, wide = kept.shape
    rows = pl.BlockSpec((1, total, wide), lambda s: (s, 0, 0))
    note = pl.BlockSpec((16, HD), lambda s: (0, first.shape[1] // HD - 1))
    each = pl.BlockSpec((1, total, HD), lambda s: (s, 0, 0))
    sent = (ring, 2, 3, 2 * total // 2 // ring, HD)
    return pl.pallas_call(
        cache_kernel,
        grid=(2,),
        in_specs=[rows, rows, note, note, pl.BlockSpec((total, HD), lambda s: (0, 0))],
        out_specs=[each, each, pl.BlockSpec(sent, lambda s: (0, 0, 0, 0, 0))],
        out_shape=[
            jax.ShapeDtypeStruct((2, total, HD), jnp.bfloat16),
            jax.ShapeDtypeStruct((2, total, HD), jnp.bfloat16),
            jax.ShapeDtypeStruct(sent, jnp.bfloat16),
        ],
        compiler_params=pltpu.CompilerParams(vmem_limit_bytes=24 << 20),
        name="make_cache",
    )(kept, other, first, second, turns(total))


def sort_kernel(in_ref, out_ref, label_ref, where_ref, sem):
    labels = in_ref[:, 2].astype(jnp.float32)[:, 0, :].astype(jnp.int32)
    label_ref[...] = labels
    copy = pltpu.make_async_copy(label_ref, where_ref, sem)
    copy.start()
    copy.wait()

    def one(i, carry):
        for slot in range(2):
            out_ref[where_ref[i, slot]] = in_ref[i, slot]
        return carry

    lax.fori_loop(0, in_ref.shape[0], one, 0)


def sort_pieces(spread):
    count, _, piece, lanes = spread.shape
    return pl.pallas_call(
        sort_kernel,
        in_specs=[pl.BlockSpec(memory_space=pltpu.VMEM)],
        out_specs=pl.BlockSpec(memory_space=pltpu.VMEM),
        out_shape=jax.ShapeDtypeStruct((2 * count, piece, lanes), spread.dtype),
        scratch_shapes=[
            pltpu.VMEM((count, lanes), jnp.int32),
            pltpu.SMEM((count, lanes), jnp.int32),
            pltpu.SemaphoreType.DMA,
        ],
        compiler_params=pltpu.CompilerParams(vmem_limit_bytes=8 << 20),
        name="sort_pieces",
    )(spread)


def blank(shape, dtype):
    return pl.pallas_call(
        lambda out_ref: None,
        out_specs=pl.BlockSpec(memory_space=pl.ANY),
        out_shape=jax.ShapeDtypeStruct(shape, dtype),
        name="blank",
    )()


def attend_kernel(heads, a_ref, b_ref, k_ref, v_ref, n0_ref, n1_ref, turn_ref, out_ref):
    length = length_of(pl.program_id(0), n0_ref, n1_ref)
    total = a_ref.shape[1]
    keys, values = k_ref[0], v_ref[0]
    row = lax.broadcasted_iota(jnp.int32, (total, total), 0)
    column = lax.broadcasted_iota(jnp.int32, (total, total), 1)
    allowed = (row >= column) & (column < length)
    for h in range(heads):
        columns = slice(h * HD, (h + 1) * HD)
        query = turned(a_ref[0, :, columns] + b_ref[0, :, columns], turn_ref)
        scores = lax.dot_general(
            query, keys, (((1,), (1,)), ((), ())), preferred_element_type=jnp.float32
        ) * (1.0 / math.sqrt(HD))
        scores = jnp.where(allowed, scores, -jnp.inf)
        peak = jnp.max(scores, axis=-1, keepdims=True)
        expo = jnp.exp(scores - peak)
        share = 1.0 / jnp.sum(expo, axis=-1, keepdims=True)
        weights = (expo * share).astype(jnp.bfloat16)
        out_ref[:, columns] = jnp.dot(
            weights, values, preferred_element_type=jnp.float32
        ).astype(jnp.bfloat16)


def turns(total):
    steps = np.arange(HD // 2, dtype=np.float32) * np.float32(2.0 / HD)
    freq = np.power(np.float32(ROPE_BASE), -steps)
    angle = np.arange(total, dtype=np.float32)[:, None] * freq[None, :]
    return np.concatenate([np.cos(angle), np.sin(angle)], axis=1).astype(np.float32)


def attend(kept, other, keys, values, first, second):
    _, total, wide = kept.shape
    rows = pl.BlockSpec((1, total, wide), lambda s: (s, 0, 0))
    note = pl.BlockSpec((16, HD), lambda s: (0, first.shape[1] // HD - 1))
    each = pl.BlockSpec((1, total, HD), lambda s: (s, 0, 0))
    return pl.pallas_call(
        functools.partial(attend_kernel, wide // HD),
        grid=(2,),
        in_specs=[rows, rows, each, each, note, note, pl.BlockSpec((total, HD), lambda s: (0, 0))],
        out_specs=pl.BlockSpec((total, wide), lambda s: (s, 0)),
        out_shape=jax.ShapeDtypeStruct((2 * total, wide), jnp.bfloat16),
        compiler_params=pltpu.CompilerParams(vmem_limit_bytes=24 << 20),
        name="attend",
    )(kept, other, keys, values, first, second, turns(total))


def output_kernel(shift_ref, a0, a1, a2, a3, a4, near_ref, far_ref, out_ref, line_ref):
    half = a0.shape[0] // 2

    @pl.when(pl.program_id(0) == 0)
    def _():
        for d, start, rows in ((0, 0, a0), (1, 0, a1), (2, 0, a2), (2, half, a3), (3, 0, a4)):
            place = (d + shift_ref[0]) % X
            line_ref[place, start : start + rows.shape[0], :] = rows[...]

    group = a0.shape[1]
    total = 0.0
    for place in range(X):
        ref = near_ref if place < X // 2 else far_ref
        start = place % (X // 2) * group
        total += lax.dot_general(
            line_ref[place],
            ref[:, start : start + group],
            (((1,), (1,)), ((), ())),
            preferred_element_type=jnp.float32,
        )
    out_ref[...] = total.astype(out_ref.dtype)


def project_out(mine, after, across, before, near, far, shift, pieces=4):
    total, group = mine.shape
    columns = near.shape[0]
    whole = part = pl.BlockSpec(memory_space=pltpu.VMEM)
    weights = pl.BlockSpec((columns // pieces, near.shape[1]), lambda i, w: (i, 0))
    return pl.pallas_call(
        output_kernel,
        grid_spec=pltpu.PrefetchScalarGridSpec(
            num_scalar_prefetch=1,
            grid=(pieces,),
            in_specs=[whole, whole, part, part, whole, weights, weights],
            out_specs=pl.BlockSpec((total, columns // pieces), lambda i, w: (0, i)),
            scratch_shapes=[pltpu.VMEM((X, total, group), mine.dtype)],
        ),
        out_shape=jax.ShapeDtypeStruct((total, columns), jnp.bfloat16),
        compiler_params=pltpu.CompilerParams(vmem_limit_bytes=24 << 20),
        name="project_out",
    )(shift.reshape(1), mine, after, *across, before, near, far)


def on_device(normed, q_weight, kv_weight, o_weight, lengths, destinations):
    ring = lax.axis_size("z")
    move = mover(ring)
    x, z, t = lax.axis_index("x"), lax.axis_index("z"), lax.axis_index("tensor")
    odd = x % 2 == 1

    total, width = normed.shape[1:]
    rows = q_weight.shape[0]
    group = q_weight.shape[1] // 2
    plus = lambda x, z, t: (x + 1, z, t)
    minus = lambda x, z, t: (x - 1, z, t)
    up = lambda x, z, t: (x, z + 1, t)
    down = lambda x, z, t: (x, z - 1, t)
    swap = lambda x, z, t: (x, z, 1 - t)

    note = jnp.repeat(jnp.stack([lengths, destinations], axis=1), HD // 2, axis=1)
    note = jnp.broadcast_to(note.astype(jnp.bfloat16), (rows, HD))

    def columns(b):
        q = lax.dynamic_slice(q_weight, (0, b * group), (rows, group))
        kv = lax.dynamic_slice(kv_weight, (0, 0, b * HD), (rows, 2, HD))
        return jnp.concatenate([q, kv[:, 0], kv[:, 1], note], axis=1)

    part0 = move(columns(x % 2), lambda x, z, t: (2 * t + x % 2, z, x // 2))
    part1 = move(columns((x + 1) % 2), lambda x, z, t: (2 * t + (x + 1) % 2, z, x // 2))
    first = jnp.where(odd, part1, part0)
    second = jnp.where(odd, part0, part1)
    wide = group + 2 * HD

    block = jnp.concatenate([first[:, :wide], second[:, :wide], o_weight.T], axis=1)
    full_in = blank((ring, rows, 2 * wide), block.dtype)
    full_out = blank((ring, rows, block.shape[1] - 2 * wide), block.dtype)

    def place(full, block, index, row=0):
        at = (index % ring, row, 0)
        return (
            lax.dynamic_update_slice(full[0], block[None, :, : 2 * wide], at),
            lax.dynamic_update_slice(full[1], block[None, :, 2 * wide :], at),
        )

    full = full_in, full_out
    rising = falling = block
    last = ring // 2
    for k in range(1, last):
        placed = place(full, rising, z - k + 1)
        if k > 1:
            placed = place(placed, falling, z + k - 1)
        rising = move(rising, up)
        falling = move(falling, down)
        rising, falling, full = lax.optimization_barrier((rising, falling, placed))
        if k == START:
            half = width // 2
            rising, normed = lax.optimization_barrier((rising, normed))
            own = lax.dynamic_slice(normed[0], (0, t * half), (total, half))
            before = move(own, plus)
            after = move(own, minus)
            across0 = move(before[: total // 2], plus)
            across1 = move(after[total // 2 :], minus)
    full = place(place(full, rising, z - last + 1), falling, z + last - 1)
    cut = rows // 2
    full = place(full, move(rising[:cut], up), z - last)
    full_in, full_out = place(full, move(falling[cut:], down), z + last, cut)

    o_half = full_out.reshape(ring * rows, -1)
    o_other = move(o_half, swap)

    states = blank((X, total, half), own.dtype)
    for piece, d, row in (
        (own, 0, 0),
        (before, -1, 0),
        (after, 1, 0),
        (across0, 2, 0),
        (across1, 2, total // 2),
    ):
        states = lax.dynamic_update_slice(states, piece[None], ((x + d) % X, row, 0))
    pieces = group // (2 * HD)
    other = move(project_in(states, full_in, 1 - t, pieces, 1), swap)
    kept = project_in(states, full_in, t, pieces, 1)
    keys, values, sent = make_cache(kept, other, first, second, ring)
    spread = lax.all_to_all(
        sent.reshape(-1, *sent.shape[2:]), ("z", "tensor"), 0, 0, tiled=True
    )
    other = move(project_in(states, full_in, 1 - t, 0, pieces), swap)
    kept = project_in(states, full_in, t, 0, pieces)

    mixed = attend(kept, other, keys, values, first, second)
    from_before = move(mixed, plus)
    from_after = move(mixed, minus)
    across = move(from_before[:total], plus), move(from_after[total:], minus)
    out = project_out(
        mixed, from_after, across, from_before, o_half, o_other, (x - 2 * t) % X
    )
    out0 = lax.dynamic_slice(out, (x % 2 * total, 0), (total, out.shape[1]))
    out1 = lax.dynamic_slice(out, ((x + 1) % 2 * total, 0), (total, out.shape[1]))
    home0 = move(out0, lambda x, z, t: (2 * t + x % 2, z, x // 2))
    home1 = move(out1, lambda x, z, t: (2 * t + (x + 1) % 2, z, x // 2))
    projected = jnp.concatenate(
        [jnp.where(odd, home1, home0), jnp.where(odd, home0, home1)], axis=1
    )

    sorted_pieces = sort_pieces(spread)
    arrived = lax.all_to_all(sorted_pieces, ("x", "z"), 0, 0, tiled=True)
    routed = arrived.reshape(X, 2, total // 2, HD).transpose(1, 0, 2, 3)
    return (projected[None], routed[None])


def solution(mesh):
    parts, count, cores = mesh.devices.shape
    torus = Mesh(
        mesh.devices.reshape(parts, X, count // X, cores), ("parts", "x", "z", "tensor")
    )
    placed = (
        P(("parts", "x", "z"), None, None),
        P(("x", "z"), "tensor"),
        P(("x", "z"), None, "tensor"),
        P("tensor", ("x", "z")),
        P(("parts", "x", "z")),
        P(("parts", "x", "z")),
    )

    return jax.shard_map(
        on_device,
        mesh=torus,
        in_specs=placed,
        out_specs=(
            P(("parts", "x", "z"), None, "tensor"),
            P(("parts", "x", "z"), None, None, "tensor", None),
        ),
        check_vma=False,
    )
```

time: 223 us -> 217 us (0.973)
  waiting for transfers between devices: 74.8 us -> 63.3 us
  Pallas kernels: 16.5 us -> 21.4 us
  local copies, waits for them, and re-layouts: 28.4 us -> 31.1 us
  other arithmetic: 5.32 us -> 2.93 us
    ppermute x31, waiting for transfers between devices: 57.8 us -> 46.3 us  [move(): return lax.ppermute(array, ('x', 'z', 'tensor'), pairs)]
    unnamed x17 -> x32, local copies, waits for them, and re-layouts: 4.38 us -> 9.47 us
    pallas_call x1 -> x6, Pallas kernels: 3.75 us -> 8.48 us  [the longest x1 5.17 us: attend(): pl.pallas_call(functools.partial(attend_kernel, wide // HD), grid=(2,), i...]
    broadcast_in_dim x4 -> x1, local copies, waits for them, and re-layouts: 2.48 us -> 0.07 us  [on_device(): jnp.repeat(jnp.stack([lengths, destinations], axis=1), HD // 2, axis=1)]
    pallas_call x2 -> x4, Pallas kernels: 7.83 us -> 7.97 us  [project_in(): pl.pallas_call(project_kernel, grid_spec=pltpu.PrefetchScalarGridSpec(num...]
  transfers between devices with their start and end apart: 33 -> 33, of which waited for: 15 -> 14; matrix products, arithmetic and copies ran while one was open for 11% -> 8% of each run, Pallas kernels for 5% -> 10%
where the time goes in v1:
time: 217 us; the launch traced here: 216 us
  starting transfers between devices  94.8 us (44%)
  waiting for transfers between devices  63.3 us (29%)
  local copies, waits for them, and re-layouts  31.1 us (14%)
  Pallas kernels  21.4 us (10%)
  other arithmetic  2.93 us (1%)
  between operations  2.6 us (1%)
    ppermute x31, starting transfers between devices, move(): return lax.ppermute(array, ('x', 'z', 'tensor'), pairs)  66.3 us
    ppermute x31, waiting for transfers between devices, move(): return lax.ppermute(array, ('x', 'z', 'tensor'), pairs)  46.3 us
    all_to_all x1, starting transfers between devices, on_device(): arrived = lax.all_to_all(sorted_pieces, ('x', 'z'), 0, 0, tiled=True)  19 us
    all_to_all x1, waiting for transfers between devices, on_device(): arrived = lax.all_to_all(sorted_pieces, ('x', 'z'), 0, 0, tiled=True)  17 us
    dynamic_update_slice x17, local copies, waits for them, and re-layouts, place(): lax.dynamic_update_slice(full[1], block[None, :, 2 * wide:], at)  13.1 us
    unnamed x32, local copies, waits for them, and re-layouts  9.47 us
    all_to_all x1, starting transfers between devices, on_device(): lax.all_to_all(sent.reshape(-1, *sent.shape[2:]), ('z', 'tensor'), 0, 0,...  9.47 us
    pallas_call x4, Pallas kernels, project_in(): pl.pallas_call(project_kernel, grid_spec=pltpu.PrefetchScalarGridSpec(num...  7.97 us
  transfers between devices with their start and end apart: 33, of which 14 were waited for; matrix products, arithmetic and copies ran while one was open for 8% of the time, Pallas kernels for 10%

profile of v1, /device:TPU:38, one launch (start us, length us, event | category | flops | bytes accessed | tf_op | source)
XLA Modules:
  0.0 216.1 jit_solution(1404990110867431854)
XLA Ops:
  2.2 1.0 constant_dynamic-slice_fusion.1
  4.4 4.4 %collective-permute-start.1 = (bf16[64,896]{1,0:T(8,128)(2,1)S(1)}, bf16[64,896]{1,0:T(8,128)(2,1)S(1)}, u32[]{:S(2)}, u32[]{:S(2)}) collective-permute-start(bf16[64,896]{1,0:T(8,128)(2,1)S(1)} %get-tuple-element.83), channel_id=1, source_target_pairs={{0,0},{1,64},{2,2},{3,66},{4,4},{5,68},{6,6},{7,70},{8,8},{9,72},{... | collective-permute-start | bytes 344072 | tf_op jit(solution)/shard_map/ppermute | solution.py:28
  8.8 1.0 collective-permute-done
  9.8 2.2 %collective-permute-done.1 = bf16[64,896]{1,0:T(8,128)(2,1)S(1)} collective-permute-done((bf16[64,896]{1,0:T(8,128)(2,1)S(1)}, bf16[64,896]{1,0:T(8,128)(2,1)S(1)}, u32[]{:S(2)}, u32[]{:S(2)}) %collective-permute-start.1) | collective-permute-done | bytes 114720 | tf_op jit(solution)/shard_map/ppermute | solution.py:28
  12.9 2.8 %collective-permute-start.2 = (bf16[64,2560]{1,0:T(8,128)(2,1)}, bf16[64,2560]{1,0:T(8,128)(2,1)}, u32[]{:S(2)}, u32[]{:S(2)}) collective-permute-start(bf16[64,2560]{1,0:T(8,128)(2,1)} %pad_maximum_fusion), channel_id=1, source_target_pairs={{0,2},{1,3},{2,4},{3,5},{4,6},{5,7},{6,8},{7,9},{8,10},{9,11},{10,... | collective-permute-start | bytes 983048 | tf_op jit(solution)/shard_map/ppermute | solution.py:28
  15.6 19.6 %collective-permute-start.3 = (bf16[64,2560]{1,0:T(8,128)(2,1)}, bf16[64,2560]{1,0:T(8,128)(2,1)}, u32[]{:S(2)}, u32[]{:S(2)}) collective-permute-start(bf16[64,2560]{1,0:T(8,128)(2,1)} %pad_maximum_fusion), channel_id=1, source_target_pairs={{0,30},{1,31},{2,0},{3,1},{4,2},{5,3},{6,4},{7,5},{8,6},{9,7},{10,... | collective-permute-start | bytes 983048 | tf_op jit(solution)/shard_map/ppermute | solution.py:28
  35.9 1.9 copy-done.3
  38.7 2.7 %collective-permute-done.2 = bf16[64,2560]{1,0:T(8,128)(2,1)} collective-permute-done((bf16[64,2560]{1,0:T(8,128)(2,1)}, bf16[64,2560]{1,0:T(8,128)(2,1)}, u32[]{:S(2)}, u32[]{:S(2)}) %collective-permute-start.2) | collective-permute-done | bytes 327712 | tf_op jit(solution)/shard_map/ppermute | solution.py:28
  41.5 3.5 %collective-permute-start.5 = (bf16[64,2560]{1,0:T(8,128)(2,1)}, bf16[64,2560]{1,0:T(8,128)(2,1)S(1)}, u32[]{:S(2)}, u32[]{:S(2)}) collective-permute-start(bf16[64,2560]{1,0:T(8,128)(2,1)} %collective-permute-done.3), channel_id=1, source_target_pairs={{0,30},{1,31},{2,0},{3,1},{4,2},{5,3},{6,4},{7,5},{8,6},{9,7},{10,... | collective-permute-start | bytes 983048 | tf_op jit(solution)/shard_map/ppermute | solution.py:28
  45.0 0.9 bitcast_dynamic-update-slice_fusion.17
  45.9 0.9 bitcast_dynamic-update-slice_fusion.16
  46.9 1.6 bitcast_dynamic-update-slice_fusion.32
  48.5 1.6 bitcast_dynamic-update-slice_fusion.31
  50.3 2.3 %dynamic-slice_bitcast_fusion = (bf16[256,2048]{1,0:T(8,128)(2,1)S(1)}, bf16[4,256,2048]{2,1,0:T(8,128)(2,1)}) fusion(bf16[1,256,4096]{2,1,0:T(8,128)(2,1)} %param.8, s32[]{:T(128)S(6)} %select_n.250, bf16[4,256,2048]{2,1,0:T(8,128)(2,1)} %blank.3, s32[]{:T(128)S(6)} %select_n.252), kind=kLoop, calls=%fused_computation.3 | loop fusion | bytes 3145736 | tf_op jit(solution)/shard_map/dynamic_slice | solution.py:315
  52.6 2.0 collective-permute-start.7
  54.6 3.2 %collective-permute-start.11 = (bf16[64,2560]{1,0:T(8,128)(2,1)S(1)}, bf16[64,2560]{1,0:T(8,128)(2,1)S(1)}, u32[]{:S(2)}, u32[]{:S(2)}) collective-permute-start(bf16[64,2560]{1,0:T(8,128)(2,1)S(1)} %collective-permute-done.5), channel_id=1, source_target_pairs={{0,30},{1,31},{2,0},{3,1},{4,2},{5,3},{6,4},{7,5},{8,6},{9,7},{10,... | collective-permute-start | bytes 983048 | tf_op jit(solution)/shard_map/ppermute | solution.py:28
  59.3 5.0 %collective-permute-done.10 = bf16[64,2560]{1,0:T(8,128)(2,1)S(1)} collective-permute-done((bf16[64,2560]{1,0:T(8,128)(2,1)S(1)}, bf16[64,2560]{1,0:T(8,128)(2,1)S(1)}, u32[]{:S(2)}, u32[]{:S(2)}) %collective-permute-start.10) | collective-permute-done | bytes 327712 | tf_op jit(solution)/shard_map/ppermute | solution.py:28
  64.2 3.2 %collective-permute-start.13 = (bf16[64,2560]{1,0:T(8,128)(2,1)S(1)}, bf16[64,2560]{1,0:T(8,128)(2,1)S(1)}, u32[]{:S(2)}, u32[]{:S(2)}) collective-permute-start(bf16[64,2560]{1,0:T(8,128)(2,1)S(1)} %collective-permute-done.11), channel_id=1, source_target_pairs={{0,30},{1,31},{2,0},{3,1},{4,2},{5,3},{6,4},{7,5},{8,6},{9,7},{10,... | collective-permute-start | bytes 983048 | tf_op jit(solution)/shard_map/ppermute | solution.py:28
  68.8 4.1 %collective-permute-done.12 = bf16[64,2560]{1,0:T(8,128)(2,1)S(1)} collective-permute-done((bf16[64,2560]{1,0:T(8,128)(2,1)S(1)}, bf16[64,2560]{1,0:T(8,128)(2,1)S(1)}, u32[]{:S(2)}, u32[]{:S(2)}) %collective-permute-start.12) | collective-permute-done | bytes 327712 | tf_op jit(solution)/shard_map/ppermute | solution.py:28
  73.0 3.2 %collective-permute-start.15 = (bf16[64,2560]{1,0:T(8,128)(2,1)S(1)}, bf16[64,2560]{1,0:T(8,128)(2,1)S(1)}, u32[]{:S(2)}, u32[]{:S(2)}) collective-permute-start(bf16[64,2560]{1,0:T(8,128)(2,1)S(1)} %collective-permute-done.13), channel_id=1, source_target_pairs={{0,30},{1,31},{2,0},{3,1},{4,2},{5,3},{6,4},{7,5},{8,6},{9,7},{10,... | collective-permute-start | bytes 983048 | tf_op jit(solution)/shard_map/ppermute | solution.py:28
  77.6 3.7 %collective-permute-done.14 = bf16[64,2560]{1,0:T(8,128)(2,1)S(1)} collective-permute-done((bf16[64,2560]{1,0:T(8,128)(2,1)S(1)}, bf16[64,2560]{1,0:T(8,128)(2,1)S(1)}, u32[]{:S(2)}, u32[]{:S(2)}) %collective-permute-start.14) | collective-permute-done | bytes 327712 | tf_op jit(solution)/shard_map/ppermute | solution.py:28
  81.3 3.5 %collective-permute-start.17 = (bf16[64,2560]{1,0:T(8,128)(2,1)S(1)}, bf16[64,2560]{1,0:T(8,128)(2,1)S(1)}, u32[]{:S(2)}, u32[]{:S(2)}) collective-permute-start(bf16[64,2560]{1,0:T(8,128)(2,1)S(1)} %collective-permute-done.15), channel_id=1, source_target_pairs={{0,30},{1,31},{2,0},{3,1},{4,2},{5,3},{6,4},{7,5},{8,6},{9,7},{10,... | collective-permute-start | bytes 983048 | tf_op jit(solution)/shard_map/ppermute | solution.py:28
  86.2 5.9 %collective-permute-start.8 = (bf16[128,2048]{1,0:T(8,128)(2,1)S(1)}, bf16[128,2048]{1,0:T(8,128)(2,1)S(1)}, u32[]{:S(2)}, u32[]{:S(2)}) collective-permute-start(bf16[128,2048]{1,0:T(8,128)(2,1)S(1)} %slice.180), channel_id=1, source_target_pairs={{0,32},{1,33},{2,34},{3,35},{4,36},{5,37},{6,38},{7,39},{8,40},{9,... | collective-permute-start | bytes 1572872 | tf_op jit(solution)/shard_map/ppermute | solution.py:28
  92.6 3.2 %collective-permute-start.19 = (bf16[64,2560]{1,0:T(8,128)(2,1)S(1)}, bf16[64,2560]{1,0:T(8,128)(2,1)S(1)}, u32[]{:S(2)}, u32[]{:S(2)}) collective-permute-start(bf16[64,2560]{1,0:T(8,128)(2,1)S(1)} %collective-permute-done.17), channel_id=1, source_target_pairs={{0,30},{1,31},{2,0},{3,1},{4,2},{5,3},{6,4},{7,5},{8,6},{9,7},{10,... | collective-permute-start | bytes 983048 | tf_op jit(solution)/shard_map/ppermute | solution.py:28
  97.2 3.6 %collective-permute-done.8 = bf16[128,2048]{1,0:T(8,128)(2,1)S(1)} collective-permute-done((bf16[128,2048]{1,0:T(8,128)(2,1)S(1)}, bf16[128,2048]{1,0:T(8,128)(2,1)S(1)}, u32[]{:S(2)}, u32[]{:S(2)}) %collective-permute-start.8) | collective-permute-done | bytes 524320 | tf_op jit(solution)/shard_map/ppermute | solution.py:28
  100.8 3.5 %collective-permute-done.9 = bf16[128,2048]{1,0:T(8,128)(2,1)S(1)} collective-permute-done((bf16[128,2048]{1,0:T(8,128)(2,1)S(1)}, bf16[128,2048]{1,0:T(8,128)(2,1)S(1)}, u32[]{:S(2)}, u32[]{:S(2)}) %collective-permute-start.9) | collective-permute-done | bytes 524320 | tf_op jit(solution)/shard_map/ppermute | solution.py:28
  104.6 3.3 %collective-permute-start.21 = (bf16[32,2560]{1,0:T(8,128)(2,1)S(1)}, bf16[32,2560]{1,0:T(8,128)(2,1)S(1)}, u32[]{:S(2)}, u32[]{:S(2)}) collective-permute-start(bf16[32,2560]{1,0:T(8,128)(2,1)S(1)} %slice.170), channel_id=1, source_target_pairs={{0,30},{1,31},{2,0},{3,1},{4,2},{5,3},{6,4},{7,5},{8,6},{9,7},{10,... | collective-permute-start | bytes 491528 | tf_op jit(solution)/shard_map/ppermute | solution.py:28
  109.3 1.8 collective-permute-done.20
  112.4 1.2 project_in.7
  114.3 3.2 %project_in.5 = f32[2,256,512]{2,1,0:T(8,128)} custom-call(s32[1]{0:T(128)} %bitcast.45.pair_ref, bf16[4,256,2048]{2,1,0:T(8,128)(2,1)S(1)} %bitcast_dynamic-update-slice_fusion.2.x_ref, bf16[16,64,1536]{2,1,0:T(8,128)(2,1)S(1)} %fusion.1.w_ref), custom_call_target="tpu_custom_call" | custom-call | tf_op jit(solution)/shard_map/project_in/pallas_call | solution.py:56
  117.6 1.2 project_in.6.a_ref
  121.4 9.5 %all-to-all-start = ((bf16[32,3,16,128]{3,2,1,0:T(8,128)(2,1)}), bf16[32,3,16,128]{3,2,1,0:T(8,128)(2,1)}, u32[]{:S(2)}, u32[]{:S(2)}) async-start(bf16[32,3,16,128]{3,2,1,0:T(8,128)(2,1)} %bitcast.115), calls=%async_computation | async-start | bytes 786432 | tf_op jit(solution)/shard_map/all_to_all | solution.py:341
  130.9 2.2 %copy-done.2 = bf16[4,256,2048]{2,1,0:T(8,128)(2,1)S(1)} copy-done((bf16[4,256,2048]{2,1,0:T(8,128)(2,1)S(1)}, bf16[4,256,2048]{2,1,0:T(8,128)(2,1)}, u32[]{:S(2)}) %copy-start.2) | copy-done | bytes 4194328
  133.1 2.3 %project_in.4.a_ref = f32[2,256,512]{2,1,0:T(8,128)S(1)} custom-call(s32[1]{0:T(128)} %bitcast.1.pair_ref, bf16[4,256,2048]{2,1,0:T(8,128)(2,1)S(1)} %copy-done.2, bf16[16,64,1536]{2,1,0:T(8,128)(2,1)S(1)} %fusion.1.w_ref), custom_call_target="tpu_custom_call" | custom-call | tf_op jit(solution)/shard_map/project_in/pallas_call | solution.py:56
  135.4 5.2 %attend.1.a0 = bf16[512,512]{1,0:T(8,128)(2,1)S(1)} custom-call(f32[2,256,512]{2,1,0:T(8,128)S(1)} %project_in.4.a_ref, f32[2,256,512]{2,1,0:T(8,128)} %collective-permute-done.22.b_ref, bf16[2,256,128]{2,1,0:T(8,128)(2,1)S(1)} %copy-done.11, bf16[2,256,128]{2,1,0:T(8,128)(2,1)S(1)} %copy-done.13, bf16[64,896]{1,0:T(8,128)(2,1)S(1)} %get-tuple-element.74.n0_ref, ...), custom_call_target="tpu_custom_call" | custom-call | tf_op jit(solution)/shard_map/attend/pallas_call | solution.py:208
  140.7 2.0 collective-permute-start.24
  142.7 11.4 %collective-permute-done.25.a4 = bf16[512,512]{1,0:T(8,128)(2,1)S(1)} collective-permute-done((bf16[512,512]{1,0:T(8,128)(2,1)S(1)}, bf16[512,512]{1,0:T(8,128)(2,1)S(1)}, u32[]{:S(2)}, u32[]{:S(2)}) %collective-permute-start.25) | collective-permute-done | bytes 524320 | tf_op jit(solution)/shard_map/ppermute | solution.py:28
  154.2 1.6 collective-permute-start.26
  156.5 4.8 %collective-permute-done.26.a2 = bf16[256,512]{1,0:T(8,128)(2,1)S(1)} collective-permute-done((bf16[256,512]{1,0:T(8,128)(2,1)S(1)}, bf16[256,512]{1,0:T(8,128)(2,1)S(1)}, u32[]{:S(2)}, u32[]{:S(2)}) %collective-permute-start.26) | collective-permute-done | bytes 262176 | tf_op jit(solution)/shard_map/ppermute | solution.py:28
  162.0 2.3 %collective-permute-done.27.a3 = bf16[256,512]{1,0:T(8,128)(2,1)S(1)} collective-permute-done((bf16[256,512]{1,0:T(8,128)(2,1)S(1)}, bf16[256,512]{1,0:T(8,128)(2,1)S(1)}, u32[]{:S(2)}, u32[]{:S(2)}) %collective-permute-start.27) | collective-permute-done | bytes 262176 | tf_op jit(solution)/shard_map/ppermute | solution.py:28
  164.9 0.9 copy-done.7
  165.9 0.9 copy-done.9
  166.8 5.0 %project_out.1 = bf16[512,1024]{1,0:T(8,128)(2,1)S(1)} custom-call(s32[1]{0:T(128)} %bitcast.shift_ref, bf16[512,512]{1,0:T(8,128)(2,1)S(1)} %attend.1.a0, bf16[512,512]{1,0:T(8,128)(2,1)S(1)} %collective-permute-done.24.a1, bf16[256,512]{1,0:T(8,128)(2,1)S(1)} %copy-done.7, bf16[256,512]{1,0:T(8,128)(2,1)S(1)} %copy-done.9, ...), custom_call_target="tpu_custom_call" | custom-call | tf_op jit(solution)/shard_map/project_out/pallas_call | solution.py:247
  172.7 2.8 %collective-permute-start.30 = (bf16[256,1024]{1,0:T(8,128)(2,1)S(1)}, bf16[256,1024]{1,0:T(8,128)(2,1)S(1)}, u32[]{:S(2)}, u32[]{:S(2)}) collective-permute-start(bf16[256,1024]{1,0:T(8,128)(2,1)S(1)} %get-tuple-element.73), channel_id=1, source_target_pairs={{0,0},{1,64},{2,2},{3,66},{4,4},{5,68},{6,6},{7,70},{8,8},{9,72},{... | collective-permute-start | bytes 1572872 | tf_op jit(solution)/shard_map/ppermute | solution.py:28
  175.5 2.8 %sort_pieces.1 = bf16[64,16,128]{2,1,0:T(8,128)(2,1)} custom-call(bf16[32,3,16,128]{3,2,1,0:T(8,128)(2,1)} %all-to-all-done.in_ref), custom_call_target="tpu_custom_call" | custom-call | tf_op jit(solution)/shard_map/sort_pieces/pallas_call | solution.py:149
  178.3 19.0 %all-to-all-start.1 = ((bf16[64,16,128]{2,1,0:T(8,128)(2,1)}), bf16[64,16,128]{2,1,0:T(8,128)(2,1)S(1)}, u32[]{:S(2)}, u32[]{:S(2)}) async-start(bf16[64,16,128]{2,1,0:T(8,128)(2,1)} %sort_pieces.1), calls=%async_computation.1 | async-start | bytes 524288 | tf_op jit(solution)/shard_map/all_to_all | solution.py:363
  197.4 1.1 maximum_bitcast_fusion
  198.4 17.0 %all-to-all-done.1 = bf16[64,16,128]{2,1,0:T(8,128)(2,1)S(1)} async-done(((bf16[64,16,128]{2,1,0:T(8,128)(2,1)}), bf16[64,16,128]{2,1,0:T(8,128)(2,1)S(1)}, u32[]{:S(2)}, u32[]{:S(2)}) %all-to-all-start.1) | async-done | bytes 262176 | tf_op jit(solution)/shard_map/all_to_all | solution.py:363
  (123 shorter events, 21.5 us)
Async XLA Ops:
  0.6 11.5 %copy-start.15 = (bf16[1024,64]{0,1:T(8,128)(2,1)S(1)}, bf16[1024,64]{0,1:T(8,128)(2,1)}, u32[]{:S(2)}) copy-start(bf16[1024,64]{0,1:T(8,128)(2,1)} %param.11) | copy-start | bytes 393220
  4.2 5.6 %collective-permute-start = (bf16[64,896]{1,0:T(8,128)(2,1)S(1)}, bf16[64,896]{1,0:T(8,128)(2,1)S(1)}, u32[]{:S(2)}, u32[]{:S(2)}) collective-permute-start(bf16[64,896]{1,0:T(8,128)(2,1)S(1)} %get-tuple-element.82), channel_id=1, source_target_pairs={{0,32},{1,96},{2,34},{3,98},{4,36},{5,100},{6,38},{7,102},{8,40},{... | collective-permute-start | bytes 344072 | tf_op jit(solution)/shard_map/ppermute | solution.py:28
  4.4 7.6 %collective-permute-start.1 = (bf16[64,896]{1,0:T(8,128)(2,1)S(1)}, bf16[64,896]{1,0:T(8,128)(2,1)S(1)}, u32[]{:S(2)}, u32[]{:S(2)}) collective-permute-start(bf16[64,896]{1,0:T(8,128)(2,1)S(1)} %get-tuple-element.83), channel_id=1, source_target_pairs={{0,0},{1,64},{2,2},{3,66},{4,4},{5,68},{6,6},{7,70},{8,8},{9,72},{... | collective-permute-start | bytes 344072 | tf_op jit(solution)/shard_map/ppermute | solution.py:28
  12.1 23.8 %copy-start.14 = (bf16[64,768]{1,0:T(8,128)(2,1)}, bf16[64,768]{1,0:T(8,128)(2,1)S(1)}, u32[]{:S(2)}) copy-start(bf16[64,768]{1,0:T(8,128)(2,1)S(1)} %slice.178) | copy-start | bytes 294916
  12.9 28.6 %collective-permute-start.2 = (bf16[64,2560]{1,0:T(8,128)(2,1)}, bf16[64,2560]{1,0:T(8,128)(2,1)}, u32[]{:S(2)}, u32[]{:S(2)}) collective-permute-start(bf16[64,2560]{1,0:T(8,128)(2,1)} %pad_maximum_fusion), channel_id=1, source_target_pairs={{0,2},{1,3},{2,4},{3,5},{4,6},{5,7},{6,8},{7,9},{8,10},{9,11},{10,... | collective-permute-start | bytes 983048 | tf_op jit(solution)/shard_map/ppermute | solution.py:28
  15.6 25.8 %collective-permute-start.3 = (bf16[64,2560]{1,0:T(8,128)(2,1)}, bf16[64,2560]{1,0:T(8,128)(2,1)}, u32[]{:S(2)}, u32[]{:S(2)}) collective-permute-start(bf16[64,2560]{1,0:T(8,128)(2,1)} %pad_maximum_fusion), channel_id=1, source_target_pairs={{0,30},{1,31},{2,0},{3,1},{4,2},{5,3},{6,4},{7,5},{8,6},{9,7},{10,... | collective-permute-start | bytes 983048 | tf_op jit(solution)/shard_map/ppermute | solution.py:28
  35.9 1.9 copy-start.3
  41.5 8.8 %collective-permute-start.4 = (bf16[64,2560]{1,0:T(8,128)(2,1)}, bf16[64,2560]{1,0:T(8,128)(2,1)S(1)}, u32[]{:S(2)}, u32[]{:S(2)}) collective-permute-start(bf16[64,2560]{1,0:T(8,128)(2,1)} %collective-permute-done.2), channel_id=1, source_target_pairs={{0,2},{1,3},{2,4},{3,5},{4,6},{5,7},{6,8},{7,9},{8,10},{9,11},{10,... | collective-permute-start | bytes 983048 | tf_op jit(solution)/shard_map/ppermute | solution.py:28
  41.5 8.8 %collective-permute-start.5 = (bf16[64,2560]{1,0:T(8,128)(2,1)}, bf16[64,2560]{1,0:T(8,128)(2,1)S(1)}, u32[]{:S(2)}, u32[]{:S(2)}) collective-permute-start(bf16[64,2560]{1,0:T(8,128)(2,1)} %collective-permute-done.3), channel_id=1, source_target_pairs={{0,30},{1,31},{2,0},{3,1},{4,2},{5,3},{6,4},{7,5},{8,6},{9,7},{10,... | collective-permute-start | bytes 983048 | tf_op jit(solution)/shard_map/ppermute | solution.py:28
  52.6 33.5 %collective-permute-start.6 = (bf16[256,2048]{1,0:T(8,128)(2,1)S(1)}, bf16[256,2048]{1,0:T(8,128)(2,1)S(1)}, u32[]{:S(2)}, u32[]{:S(2)}) collective-permute-start(bf16[256,2048]{1,0:T(8,128)(2,1)S(1)} %get-tuple-element.68), channel_id=1, source_target_pairs={{0,32},{1,33},{2,34},{3,35},{4,36},{5,37},{6,38},{7,39},{8,40},{9,... | collective-permute-start | bytes 3145736 | tf_op jit(solution)/shard_map/ppermute | solution.py:28
  52.6 39.4 %collective-permute-start.7 = (bf16[256,2048]{1,0:T(8,128)(2,1)S(1)}, bf16[256,2048]{1,0:T(8,128)(2,1)S(1)}, u32[]{:S(2)}, u32[]{:S(2)}) collective-permute-start(bf16[256,2048]{1,0:T(8,128)(2,1)S(1)} %get-tuple-element.68), channel_id=1, source_target_pairs={{0,96},{1,97},{2,98},{3,99},{4,100},{5,101},{6,102},{7,103},{8,104... | collective-permute-start | bytes 3145736 | tf_op jit(solution)/shard_map/ppermute | solution.py:28
  54.6 9.6 %collective-permute-start.10 = (bf16[64,2560]{1,0:T(8,128)(2,1)S(1)}, bf16[64,2560]{1,0:T(8,128)(2,1)S(1)}, u32[]{:S(2)}, u32[]{:S(2)}) collective-permute-start(bf16[64,2560]{1,0:T(8,128)(2,1)S(1)} %collective-permute-done.4), channel_id=1, source_target_pairs={{0,2},{1,3},{2,4},{3,5},{4,6},{5,7},{6,8},{7,9},{8,10},{9,11},{10,... | collective-permute-start | bytes 983048 | tf_op jit(solution)/shard_map/ppermute | solution.py:28
  54.6 9.6 %collective-permute-start.11 = (bf16[64,2560]{1,0:T(8,128)(2,1)S(1)}, bf16[64,2560]{1,0:T(8,128)(2,1)S(1)}, u32[]{:S(2)}, u32[]{:S(2)}) collective-permute-start(bf16[64,2560]{1,0:T(8,128)(2,1)S(1)} %collective-permute-done.5), channel_id=1, source_target_pairs={{0,30},{1,31},{2,0},{3,1},{4,2},{5,3},{6,4},{7,5},{8,6},{9,7},{10,... | collective-permute-start | bytes 983048 | tf_op jit(solution)/shard_map/ppermute | solution.py:28
  58.6 33.7 %copy-start = (bf16[4,256,2048]{2,1,0:T(8,128)(2,1)S(1)}, bf16[4,256,2048]{2,1,0:T(8,128)(2,1)}, u32[]{:S(2)}) copy-start(bf16[4,256,2048]{2,1,0:T(8,128)(2,1)} %get-tuple-element.69) | copy-start | bytes 12582916
  64.2 8.7 %collective-permute-start.12 = (bf16[64,2560]{1,0:T(8,128)(2,1)S(1)}, bf16[64,2560]{1,0:T(8,128)(2,1)S(1)}, u32[]{:S(2)}, u32[]{:S(2)}) collective-permute-start(bf16[64,2560]{1,0:T(8,128)(2,1)S(1)} %collective-permute-done.10), channel_id=1, source_target_pairs={{0,2},{1,3},{2,4},{3,5},{4,6},{5,7},{6,8},{7,9},{8,10},{9,11},{10,... | collective-permute-start | bytes 983048 | tf_op jit(solution)/shard_map/ppermute | solution.py:28
  64.2 8.7 %collective-permute-start.13 = (bf16[64,2560]{1,0:T(8,128)(2,1)S(1)}, bf16[64,2560]{1,0:T(8,128)(2,1)S(1)}, u32[]{:S(2)}, u32[]{:S(2)}) collective-permute-start(bf16[64,2560]{1,0:T(8,128)(2,1)S(1)} %collective-permute-done.11), channel_id=1, source_target_pairs={{0,30},{1,31},{2,0},{3,1},{4,2},{5,3},{6,4},{7,5},{8,6},{9,7},{10,... | collective-permute-start | bytes 983048 | tf_op jit(solution)/shard_map/ppermute | solution.py:28
  73.0 8.3 %collective-permute-start.14 = (bf16[64,2560]{1,0:T(8,128)(2,1)S(1)}, bf16[64,2560]{1,0:T(8,128)(2,1)S(1)}, u32[]{:S(2)}, u32[]{:S(2)}) collective-permute-start(bf16[64,2560]{1,0:T(8,128)(2,1)S(1)} %collective-permute-done.12), channel_id=1, source_target_pairs={{0,2},{1,3},{2,4},{3,5},{4,6},{5,7},{6,8},{7,9},{8,10},{9,11},{10,... | collective-permute-start | bytes 983048 | tf_op jit(solution)/shard_map/ppermute | solution.py:28
  73.0 8.3 %collective-permute-start.15 = (bf16[64,2560]{1,0:T(8,128)(2,1)S(1)}, bf16[64,2560]{1,0:T(8,128)(2,1)S(1)}, u32[]{:S(2)}, u32[]{:S(2)}) collective-permute-start(bf16[64,2560]{1,0:T(8,128)(2,1)S(1)} %collective-permute-done.13), channel_id=1, source_target_pairs={{0,30},{1,31},{2,0},{3,1},{4,2},{5,3},{6,4},{7,5},{8,6},{9,7},{10,... | collective-permute-start | bytes 983048 | tf_op jit(solution)/shard_map/ppermute | solution.py:28
  81.3 11.2 %collective-permute-start.16 = (bf16[64,2560]{1,0:T(8,128)(2,1)S(1)}, bf16[64,2560]{1,0:T(8,128)(2,1)S(1)}, u32[]{:S(2)}, u32[]{:S(2)}) collective-permute-start(bf16[64,2560]{1,0:T(8,128)(2,1)S(1)} %collective-permute-done.14), channel_id=1, source_target_pairs={{0,2},{1,3},{2,4},{3,5},{4,6},{5,7},{6,8},{7,9},{8,10},{9,11},{10,... | collective-permute-start | bytes 983048 | tf_op jit(solution)/shard_map/ppermute | solution.py:28
  81.3 11.2 %collective-permute-start.17 = (bf16[64,2560]{1,0:T(8,128)(2,1)S(1)}, bf16[64,2560]{1,0:T(8,128)(2,1)S(1)}, u32[]{:S(2)}, u32[]{:S(2)}) collective-permute-start(bf16[64,2560]{1,0:T(8,128)(2,1)S(1)} %collective-permute-done.15), channel_id=1, source_target_pairs={{0,30},{1,31},{2,0},{3,1},{4,2},{5,3},{6,4},{7,5},{8,6},{9,7},{10,... | collective-permute-start | bytes 983048 | tf_op jit(solution)/shard_map/ppermute | solution.py:28
  86.2 14.6 %collective-permute-start.8 = (bf16[128,2048]{1,0:T(8,128)(2,1)S(1)}, bf16[128,2048]{1,0:T(8,128)(2,1)S(1)}, u32[]{:S(2)}, u32[]{:S(2)}) collective-permute-start(bf16[128,2048]{1,0:T(8,128)(2,1)S(1)} %slice.180), channel_id=1, source_target_pairs={{0,32},{1,33},{2,34},{3,35},{4,36},{5,37},{6,38},{7,39},{8,40},{9,... | collective-permute-start | bytes 1572872 | tf_op jit(solution)/shard_map/ppermute | solution.py:28
  92.1 12.2 %collective-permute-start.9 = (bf16[128,2048]{1,0:T(8,128)(2,1)S(1)}, bf16[128,2048]{1,0:T(8,128)(2,1)S(1)}, u32[]{:S(2)}, u32[]{:S(2)}) collective-permute-start(bf16[128,2048]{1,0:T(8,128)(2,1)S(1)} %slice.181), channel_id=1, source_target_pairs={{0,96},{1,97},{2,98},{3,99},{4,100},{5,101},{6,102},{7,103},{8,104... | collective-permute-start | bytes 1572872 | tf_op jit(solution)/shard_map/ppermute | solution.py:28
  92.5 11.9 %collective-permute-start.18 = (bf16[64,2560]{1,0:T(8,128)(2,1)S(1)}, bf16[64,2560]{1,0:T(8,128)(2,1)S(1)}, u32[]{:S(2)}, u32[]{:S(2)}) collective-permute-start(bf16[64,2560]{1,0:T(8,128)(2,1)S(1)} %collective-permute-done.16), channel_id=1, source_target_pairs={{0,2},{1,3},{2,4},{3,5},{4,6},{5,7},{6,8},{7,9},{8,10},{9,11},{10,... | collective-permute-start | bytes 983048 | tf_op jit(solution)/shard_map/ppermute | solution.py:28
  92.6 11.8 %collective-permute-start.19 = (bf16[64,2560]{1,0:T(8,128)(2,1)S(1)}, bf16[64,2560]{1,0:T(8,128)(2,1)S(1)}, u32[]{:S(2)}, u32[]{:S(2)}) collective-permute-start(bf16[64,2560]{1,0:T(8,128)(2,1)S(1)} %collective-permute-done.17), channel_id=1, source_target_pairs={{0,30},{1,31},{2,0},{3,1},{4,2},{5,3},{6,4},{7,5},{8,6},{9,7},{10,... | collective-permute-start | bytes 983048 | tf_op jit(solution)/shard_map/ppermute | solution.py:28
  104.4 13.2 %copy-start.1 = (bf16[4,256,2048]{2,1,0:T(8,128)(2,1)}, bf16[4,256,2048]{2,1,0:T(8,128)(2,1)S(1)}, u32[]{:S(2)}) copy-start(bf16[4,256,2048]{2,1,0:T(8,128)(2,1)S(1)} %bitcast_dynamic-update-slice_fusion.2.x_ref) | copy-start | bytes 12582916
  104.5 6.6 %collective-permute-start.20 = (bf16[32,2560]{1,0:T(8,128)(2,1)S(1)}, bf16[32,2560]{1,0:T(8,128)(2,1)S(1)}, u32[]{:S(2)}, u32[]{:S(2)}) collective-permute-start(bf16[32,2560]{1,0:T(8,128)(2,1)S(1)} %slice.168), channel_id=1, source_target_pairs={{0,2},{1,3},{2,4},{3,5},{4,6},{5,7},{6,8},{7,9},{8,10},{9,11},{10,... | collective-permute-start | bytes 491528 | tf_op jit(solution)/shard_map/ppermute | solution.py:28
  104.6 7.1 %collective-permute-start.21 = (bf16[32,2560]{1,0:T(8,128)(2,1)S(1)}, bf16[32,2560]{1,0:T(8,128)(2,1)S(1)}, u32[]{:S(2)}, u32[]{:S(2)}) collective-permute-start(bf16[32,2560]{1,0:T(8,128)(2,1)S(1)} %slice.170), channel_id=1, source_target_pairs={{0,30},{1,31},{2,0},{3,1},{4,2},{5,3},{6,4},{7,5},{8,6},{9,7},{10,... | collective-permute-start | bytes 491528 | tf_op jit(solution)/shard_map/ppermute | solution.py:28
  112.4 52.6 %collective-permute-start.28 = (bf16[1024,1024]{1,0:T(8,128)(2,1)}, bf16[1024,1024]{1,0:T(8,128)(2,1)}, u32[]{:S(2)}, u32[]{:S(2)}) collective-permute-start(bf16[1024,1024]{1,0:T(8,128)(2,1)} %bitcast.50.near_ref), channel_id=1, source_target_pairs={{0,1},{1,0},{2,3},{3,2},{4,5},{5,4},{6,7},{7,6},{8,9},{9,8},{10,11... | collective-permute-start | bytes 6291464 | tf_op jit(solution)/shard_map/ppermute | solution.py:28
  113.6 5.2 %collective-permute-start.23 = (f32[2,256,256]{2,1,0:T(8,128)S(1)}, f32[2,256,256]{2,1,0:T(8,128)S(1)}, u32[]{:S(2)}, u32[]{:S(2)}) collective-permute-start(f32[2,256,256]{2,1,0:T(8,128)S(1)} %project_in.7), channel_id=1, source_target_pairs={{0,1},{1,0},{2,3},{3,2},{4,5},{5,4},{6,7},{7,6},{8,9},{9,8},{10,11... | collective-permute-start | bytes 1572872 | tf_op jit(solution)/shard_map/ppermute | solution.py:28
  117.5 17.9 %collective-permute-start.22 = (f32[2,256,512]{2,1,0:T(8,128)}, f32[2,256,512]{2,1,0:T(8,128)}, u32[]{:S(2)}, u32[]{:S(2)}) collective-permute-start(f32[2,256,512]{2,1,0:T(8,128)} %project_in.5), channel_id=1, source_target_pairs={{0,1},{1,0},{2,3},{3,2},{4,5},{5,4},{6,7},{7,6},{8,9},{9,8},{10,11... | collective-permute-start | bytes 3145736 | tf_op jit(solution)/shard_map/ppermute | solution.py:28
  117.6 1.2 copy-start.4
  119.3 0.8 copy-start.5
  120.1 0.7 copy-start.10
  121.4 54.1 %all-to-all-start = ((bf16[32,3,16,128]{3,2,1,0:T(8,128)(2,1)}), bf16[32,3,16,128]{3,2,1,0:T(8,128)(2,1)}, u32[]{:S(2)}, u32[]{:S(2)}) async-start(bf16[32,3,16,128]{3,2,1,0:T(8,128)(2,1)} %bitcast.115), calls=%async_computation | async-start | bytes 786432 | tf_op jit(solution)/shard_map/all_to_all | solution.py:341
  130.9 2.2 %copy-start.2 = (bf16[4,256,2048]{2,1,0:T(8,128)(2,1)S(1)}, bf16[4,256,2048]{2,1,0:T(8,128)(2,1)}, u32[]{:S(2)}) copy-start(bf16[4,256,2048]{2,1,0:T(8,128)(2,1)} %copy-done.1) | copy-start | bytes 12582916
  133.1 2.3 %copy-start.11 = (bf16[2,256,128]{2,1,0:T(8,128)(2,1)S(1)}, bf16[2,256,128]{2,1,0:T(8,128)(2,1)}, u32[]{:S(2)}) copy-start(bf16[2,256,128]{2,1,0:T(8,128)(2,1)} %copy-done.10) | copy-start | bytes 393220
  133.1 2.3 %copy-start.13 = (bf16[2,256,128]{2,1,0:T(8,128)(2,1)S(1)}, bf16[2,256,128]{2,1,0:T(8,128)(2,1)}, u32[]{:S(2)}) copy-start(bf16[2,256,128]{2,1,0:T(8,128)(2,1)} %copy-done.12) | copy-start | bytes 393220
  140.6 13.5 %collective-permute-start.25 = (bf16[512,512]{1,0:T(8,128)(2,1)S(1)}, bf16[512,512]{1,0:T(8,128)(2,1)S(1)}, u32[]{:S(2)}, u32[]{:S(2)}) collective-permute-start(bf16[512,512]{1,0:T(8,128)(2,1)S(1)} %attend.1.a0), channel_id=1, source_target_pairs={{0,32},{1,33},{2,34},{3,35},{4,36},{5,37},{6,38},{7,39},{8,40},{9,... | collective-permute-start | bytes 1572872 | tf_op jit(solution)/shard_map/ppermute | solution.py:28
  140.7 15.1 %collective-permute-start.24 = (bf16[512,512]{1,0:T(8,128)(2,1)S(1)}, bf16[512,512]{1,0:T(8,128)(2,1)S(1)}, u32[]{:S(2)}, u32[]{:S(2)}) collective-permute-start(bf16[512,512]{1,0:T(8,128)(2,1)S(1)} %attend.1.a0), channel_id=1, source_target_pairs={{0,96},{1,97},{2,98},{3,99},{4,100},{5,101},{6,102},{7,103},{8,104... | collective-permute-start | bytes 1572872 | tf_op jit(solution)/shard_map/ppermute | solution.py:28
  154.2 7.1 %collective-permute-start.26 = (bf16[256,512]{1,0:T(8,128)(2,1)S(1)}, bf16[256,512]{1,0:T(8,128)(2,1)S(1)}, u32[]{:S(2)}, u32[]{:S(2)}) collective-permute-start(bf16[256,512]{1,0:T(8,128)(2,1)S(1)} %slice.184), channel_id=1, source_target_pairs={{0,32},{1,33},{2,34},{3,35},{4,36},{5,37},{6,38},{7,39},{8,40},{9,... | collective-permute-start | bytes 786440 | tf_op jit(solution)/shard_map/ppermute | solution.py:28
  155.8 8.4 %collective-permute-start.27 = (bf16[256,512]{1,0:T(8,128)(2,1)S(1)}, bf16[256,512]{1,0:T(8,128)(2,1)S(1)}, u32[]{:S(2)}, u32[]{:S(2)}) collective-permute-start(bf16[256,512]{1,0:T(8,128)(2,1)S(1)} %slice.185), channel_id=1, source_target_pairs={{0,96},{1,97},{2,98},{3,99},{4,100},{5,101},{6,102},{7,103},{8,104... | collective-permute-start | bytes 786440 | tf_op jit(solution)/shard_map/ppermute | solution.py:28
  161.2 0.7 copy-start.6
  164.2 0.7 copy-start.8
  164.9 1.0 copy-start.7
  165.9 0.9 copy-start.9
  172.7 24.6 %collective-permute-start.29 = (bf16[256,1024]{1,0:T(8,128)(2,1)}, bf16[256,1024]{1,0:T(8,128)(2,1)S(1)}, u32[]{:S(2)}, u32[]{:S(2)}) collective-permute-start(bf16[256,1024]{1,0:T(8,128)(2,1)} %get-tuple-element.72), channel_id=1, source_target_pairs={{0,32},{1,96},{2,34},{3,98},{4,36},{5,100},{6,38},{7,102},{8,40},{... | collective-permute-start | bytes 1572872 | tf_op jit(solution)/shard_map/ppermute | solution.py:28
  172.7 24.6 %collective-permute-start.30 = (bf16[256,1024]{1,0:T(8,128)(2,1)S(1)}, bf16[256,1024]{1,0:T(8,128)(2,1)S(1)}, u32[]{:S(2)}, u32[]{:S(2)}) collective-permute-start(bf16[256,1024]{1,0:T(8,128)(2,1)S(1)} %get-tuple-element.73), channel_id=1, source_target_pairs={{0,0},{1,64},{2,2},{3,66},{4,4},{5,68},{6,6},{7,70},{8,8},{9,72},{... | collective-permute-start | bytes 1572872 | tf_op jit(solution)/shard_map/ppermute | solution.py:28
  178.3 37.1 %all-to-all-start.1 = ((bf16[64,16,128]{2,1,0:T(8,128)(2,1)}), bf16[64,16,128]{2,1,0:T(8,128)(2,1)S(1)}, u32[]{:S(2)}, u32[]{:S(2)}) async-start(bf16[64,16,128]{2,1,0:T(8,128)(2,1)} %sort_pieces.1), calls=%async_computation.1 | async-start | bytes 524288 | tf_op jit(solution)/shard_map/all_to_all | solution.py:363
  (1 other events, 0.6 us)

commit v2 on v1

--- a/solution.py
+++ b/solution.py
@@ -13,6 +13,7 @@
 HD = 128
 ROPE_BASE = 500000.0
 START = 2
+LABEL = 8
 X = 4
 
 
@@ -93,19 +94,22 @@
     values_ref[0] = values
     live = lax.broadcasted_iota(jnp.int32, (total, HD), 0) < length
     zero = jnp.zeros((), jnp.bfloat16)
-    ring, cores, _, piece, _ = sent_ref.shape
+    ring, cores, piece, _ = sent_ref.shape
+    piece = (piece - LABEL) // 2
     count = ring // 2
+    at = pl.ds(pl.multiple_of(slot * piece, piece), piece)
     for index, array in enumerate((keys, values)):
         kept = jnp.where(live, array, zero).reshape(cores, count, piece, HD)
         for core in range(cores):
-            sent_ref[index * count : (index + 1) * count, core, slot] = kept[core]
+            sent_ref[index * count : (index + 1) * count, core, at] = kept[core]
 
     @pl.when(slot == 0)
     def _():
-        lane = lax.broadcasted_iota(jnp.int32, (piece, HD), 1)
+        lane = lax.broadcasted_iota(jnp.int32, (LABEL, HD), 1)
         half = HD // 2
         label = jnp.where(lane == 0, n0_ref[:1, half : half + 1], n1_ref[:1, half : half + 1])
-        sent_ref[:, :, 2] = jnp.broadcast_to(label, (ring, cores, piece, HD))
+        label = jnp.broadcast_to(label, (ring, cores, LABEL, HD))
+        sent_ref[:, :, 2 * piece :] = label
 
 
 def make_cache(kept, other, first, second, ring):
@@ -113,12 +117,12 @@
     rows = pl.BlockSpec((1, total, wide), lambda s: (s, 0, 0))
     note = pl.BlockSpec((16, HD), lambda s: (0, first.shape[1] // HD - 1))
     each = pl.BlockSpec((1, total, HD), lambda s: (s, 0, 0))
-    sent = (ring, 2, 3, 2 * total // 2 // ring, HD)
+    sent = (ring, 2, 2 * (total // ring) + LABEL, HD)
     return pl.pallas_call(
         cache_kernel,
         grid=(2,),
         in_specs=[rows, rows, note, note, pl.BlockSpec((total, HD), lambda s: (0, 0))],
-        out_specs=[each, each, pl.BlockSpec(sent, lambda s: (0, 0, 0, 0, 0))],
+        out_specs=[each, each, pl.BlockSpec(sent, lambda s: (0, 0, 0, 0))],
         out_shape=[
             jax.ShapeDtypeStruct((2, total, HD), jnp.bfloat16),
             jax.ShapeDtypeStruct((2, total, HD), jnp.bfloat16),
@@ -130,7 +134,8 @@
 
 
 def sort_kernel(in_ref, out_ref, label_ref, where_ref, sem):
-    labels = in_ref[:, 2].astype(jnp.float32)[:, 0, :].astype(jnp.int32)
+    piece = out_ref.shape[1]
+    labels = in_ref[:, 2 * piece :].astype(jnp.float32)[:, 0, :].astype(jnp.int32)
     label_ref[...] = labels
     copy = pltpu.make_async_copy(label_ref, where_ref, sem)
     copy.start()
@@ -138,14 +143,15 @@
 
     def one(i, carry):
         for slot in range(2):
-            out_ref[where_ref[i, slot]] = in_ref[i, slot]
+            out_ref[where_ref[i, slot]] = in_ref[i, slot * piece : (slot + 1) * piece]
         return carry
 
     lax.fori_loop(0, in_ref.shape[0], one, 0)
 
 
 def sort_pieces(spread):
-    count, _, piece, lanes = spread.shape
+    count, piece, lanes = spread.shape
+    piece = (piece - LABEL) // 2
     return pl.pallas_call(
         sort_kernel,
         in_specs=[pl.BlockSpec(memory_space=pltpu.VMEM)],
@@ -341,7 +347,8 @@
     spread = lax.all_to_all(
         sent.reshape(-1, *sent.shape[2:]), ("z", "tensor"), 0, 0, tiled=True
     )
-    other = move(project_in(states, full_in, 1 - t, 0, pieces), swap)
+    other = project_in(states, full_in, 1 - t, 0, pieces)
+    other = move(other, swap)
     kept = project_in(states, full_in, t, 0, pieces)
 
     mixed = attend(kept, other, keys, values, first, second)

time: 217 us -> 217 us (level)
  transfers between devices with their start and end apart: 33 -> 33, of which waited for: 14 -> 15; matrix products, arithmetic and copies ran while one was open for 8% -> 8% of each run, Pallas kernels for 10% -> 10%
where the time goes in v2:
time: 217 us
  starting transfers between devices  94.8 us (44%)
  waiting for transfers between devices  63.8 us (29%)
  local copies, waits for them, and re-layouts  31.1 us (14%)
  Pallas kernels  21.4 us (10%)
  other arithmetic  2.93 us (1%)
  between operations  2.6 us (1%)
    ppermute x31, starting transfers between devices, move(): return lax.ppermute(array, ('x', 'z', 'tensor'), pairs)  66.3 us
    ppermute x31, waiting for transfers between devices, move(): return lax.ppermute(array, ('x', 'z', 'tensor'), pairs)  46.8 us
    all_to_all x1, starting transfers between devices, on_device(): arrived = lax.all_to_all(sorted_pieces, ('x', 'z'), 0, 0, tiled=True)  19.1 us
    all_to_all x1, waiting for transfers between devices, on_device(): arrived = lax.all_to_all(sorted_pieces, ('x', 'z'), 0, 0, tiled=True)  17 us
    dynamic_update_slice x17, local copies, waits for them, and re-layouts, place(): lax.dynamic_update_slice(full[1], block[None, :, 2 * wide:], at)  13.1 us
    unnamed x32, local copies, waits for them, and re-layouts  9.47 us
    all_to_all x1, starting transfers between devices, on_device(): lax.all_to_all(sent.reshape(-1, *sent.shape[2:]), ('z', 'tensor'), 0, 0,...  9.4 us
    pallas_call x4, Pallas kernels, project_in(): pl.pallas_call(project_kernel, grid_spec=pltpu.PrefetchScalarGridSpec(num...  8 us
  transfers between devices with their start and end apart: 33, of which 15 were waited for; matrix products, arithmetic and copies ran while one was open for 8% of the time, Pallas kernels for 10%

profile of v2, /device:TPU:38, one launch (start us, length us, event | category | flops | bytes accessed | tf_op | source)
XLA Modules:
  0.0 216.6 jit_solution(14137963988737814052)
XLA Ops:
  2.2 1.0 constant_dynamic-slice_fusion.1
  4.4 4.4 %collective-permute-start.1 = (bf16[64,896]{1,0:T(8,128)(2,1)S(1)}, bf16[64,896]{1,0:T(8,128)(2,1)S(1)}, u32[]{:S(2)}, u32[]{:S(2)}) collective-permute-start(bf16[64,896]{1,0:T(8,128)(2,1)S(1)} %get-tuple-element.83), channel_id=1, source_target_pairs={{0,0},{1,64},{2,2},{3,66},{4,4},{5,68},{6,6},{7,70},{8,8},{9,72},{... | collective-permute-start | bytes 344072 | tf_op jit(solution)/shard_map/ppermute | solution.py:29
  8.8 1.0 collective-permute-done
  9.8 2.2 %collective-permute-done.1 = bf16[64,896]{1,0:T(8,128)(2,1)S(1)} collective-permute-done((bf16[64,896]{1,0:T(8,128)(2,1)S(1)}, bf16[64,896]{1,0:T(8,128)(2,1)S(1)}, u32[]{:S(2)}, u32[]{:S(2)}) %collective-permute-start.1) | collective-permute-done | bytes 114720 | tf_op jit(solution)/shard_map/ppermute | solution.py:29
  12.9 2.8 %collective-permute-start.2 = (bf16[64,2560]{1,0:T(8,128)(2,1)}, bf16[64,2560]{1,0:T(8,128)(2,1)}, u32[]{:S(2)}, u32[]{:S(2)}) collective-permute-start(bf16[64,2560]{1,0:T(8,128)(2,1)} %pad_maximum_fusion), channel_id=1, source_target_pairs={{0,2},{1,3},{2,4},{3,5},{4,6},{5,7},{6,8},{7,9},{8,10},{9,11},{10,... | collective-permute-start | bytes 983048 | tf_op jit(solution)/shard_map/ppermute | solution.py:29
  15.6 19.6 %collective-permute-start.3 = (bf16[64,2560]{1,0:T(8,128)(2,1)}, bf16[64,2560]{1,0:T(8,128)(2,1)}, u32[]{:S(2)}, u32[]{:S(2)}) collective-permute-start(bf16[64,2560]{1,0:T(8,128)(2,1)} %pad_maximum_fusion), channel_id=1, source_target_pairs={{0,30},{1,31},{2,0},{3,1},{4,2},{5,3},{6,4},{7,5},{8,6},{9,7},{10,... | collective-permute-start | bytes 983048 | tf_op jit(solution)/shard_map/ppermute | solution.py:29
  35.9 1.9 copy-done.3
  38.7 2.7 %collective-permute-done.2 = bf16[64,2560]{1,0:T(8,128)(2,1)} collective-permute-done((bf16[64,2560]{1,0:T(8,128)(2,1)}, bf16[64,2560]{1,0:T(8,128)(2,1)}, u32[]{:S(2)}, u32[]{:S(2)}) %collective-permute-start.2) | collective-permute-done | bytes 327712 | tf_op jit(solution)/shard_map/ppermute | solution.py:29
  41.5 3.5 %collective-permute-start.5 = (bf16[64,2560]{1,0:T(8,128)(2,1)}, bf16[64,2560]{1,0:T(8,128)(2,1)S(1)}, u32[]{:S(2)}, u32[]{:S(2)}) collective-permute-start(bf16[64,2560]{1,0:T(8,128)(2,1)} %collective-permute-done.3), channel_id=1, source_target_pairs={{0,30},{1,31},{2,0},{3,1},{4,2},{5,3},{6,4},{7,5},{8,6},{9,7},{10,... | collective-permute-start | bytes 983048 | tf_op jit(solution)/shard_map/ppermute | solution.py:29
  45.0 0.9 bitcast_dynamic-update-slice_fusion.17
  45.9 0.9 bitcast_dynamic-update-slice_fusion.16
  46.9 1.6 bitcast_dynamic-update-slice_fusion.32
  48.5 1.6 bitcast_dynamic-update-slice_fusion.31
  50.3 2.3 %dynamic-slice_bitcast_fusion = (bf16[256,2048]{1,0:T(8,128)(2,1)S(1)}, bf16[4,256,2048]{2,1,0:T(8,128)(2,1)}) fusion(bf16[1,256,4096]{2,1,0:T(8,128)(2,1)} %param.8, s32[]{:T(128)S(6)} %select_n.250, bf16[4,256,2048]{2,1,0:T(8,128)(2,1)} %blank.3, s32[]{:T(128)S(6)} %select_n.252), kind=kLoop, calls=%fused_computation.3 | loop fusion | bytes 3145736 | tf_op jit(solution)/shard_map/dynamic_slice | solution.py:321
  52.6 2.0 collective-permute-start.7
  54.6 3.2 %collective-permute-start.11 = (bf16[64,2560]{1,0:T(8,128)(2,1)S(1)}, bf16[64,2560]{1,0:T(8,128)(2,1)S(1)}, u32[]{:S(2)}, u32[]{:S(2)}) collective-permute-start(bf16[64,2560]{1,0:T(8,128)(2,1)S(1)} %collective-permute-done.5), channel_id=1, source_target_pairs={{0,30},{1,31},{2,0},{3,1},{4,2},{5,3},{6,4},{7,5},{8,6},{9,7},{10,... | collective-permute-start | bytes 983048 | tf_op jit(solution)/shard_map/ppermute | solution.py:29
  59.3 5.0 %collective-permute-done.10 = bf16[64,2560]{1,0:T(8,128)(2,1)S(1)} collective-permute-done((bf16[64,2560]{1,0:T(8,128)(2,1)S(1)}, bf16[64,2560]{1,0:T(8,128)(2,1)S(1)}, u32[]{:S(2)}, u32[]{:S(2)}) %collective-permute-start.10) | collective-permute-done | bytes 327712 | tf_op jit(solution)/shard_map/ppermute | solution.py:29
  64.2 3.2 %collective-permute-start.13 = (bf16[64,2560]{1,0:T(8,128)(2,1)S(1)}, bf16[64,2560]{1,0:T(8,128)(2,1)S(1)}, u32[]{:S(2)}, u32[]{:S(2)}) collective-permute-start(bf16[64,2560]{1,0:T(8,128)(2,1)S(1)} %collective-permute-done.11), channel_id=1, source_target_pairs={{0,30},{1,31},{2,0},{3,1},{4,2},{5,3},{6,4},{7,5},{8,6},{9,7},{10,... | collective-permute-start | bytes 983048 | tf_op jit(solution)/shard_map/ppermute | solution.py:29
  68.8 4.1 %collective-permute-done.12 = bf16[64,2560]{1,0:T(8,128)(2,1)S(1)} collective-permute-done((bf16[64,2560]{1,0:T(8,128)(2,1)S(1)}, bf16[64,2560]{1,0:T(8,128)(2,1)S(1)}, u32[]{:S(2)}, u32[]{:S(2)}) %collective-permute-start.12) | collective-permute-done | bytes 327712 | tf_op jit(solution)/shard_map/ppermute | solution.py:29
  73.0 3.2 %collective-permute-start.15 = (bf16[64,2560]{1,0:T(8,128)(2,1)S(1)}, bf16[64,2560]{1,0:T(8,128)(2,1)S(1)}, u32[]{:S(2)}, u32[]{:S(2)}) collective-permute-start(bf16[64,2560]{1,0:T(8,128)(2,1)S(1)} %collective-permute-done.13), channel_id=1, source_target_pairs={{0,30},{1,31},{2,0},{3,1},{4,2},{5,3},{6,4},{7,5},{8,6},{9,7},{10,... | collective-permute-start | bytes 983048 | tf_op jit(solution)/shard_map/ppermute | solution.py:29
  77.6 3.7 %collective-permute-done.14 = bf16[64,2560]{1,0:T(8,128)(2,1)S(1)} collective-permute-done((bf16[64,2560]{1,0:T(8,128)(2,1)S(1)}, bf16[64,2560]{1,0:T(8,128)(2,1)S(1)}, u32[]{:S(2)}, u32[]{:S(2)}) %collective-permute-start.14) | collective-permute-done | bytes 327712 | tf_op jit(solution)/shard_map/ppermute | solution.py:29
  81.3 3.5 %collective-permute-start.17 = (bf16[64,2560]{1,0:T(8,128)(2,1)S(1)}, bf16[64,2560]{1,0:T(8,128)(2,1)S(1)}, u32[]{:S(2)}, u32[]{:S(2)}) collective-permute-start(bf16[64,2560]{1,0:T(8,128)(2,1)S(1)} %collective-permute-done.15), channel_id=1, source_target_pairs={{0,30},{1,31},{2,0},{3,1},{4,2},{5,3},{6,4},{7,5},{8,6},{9,7},{10,... | collective-permute-start | bytes 983048 | tf_op jit(solution)/shard_map/ppermute | solution.py:29
  86.2 5.9 %collective-permute-start.8 = (bf16[128,2048]{1,0:T(8,128)(2,1)S(1)}, bf16[128,2048]{1,0:T(8,128)(2,1)S(1)}, u32[]{:S(2)}, u32[]{:S(2)}) collective-permute-start(bf16[128,2048]{1,0:T(8,128)(2,1)S(1)} %slice.180), channel_id=1, source_target_pairs={{0,32},{1,33},{2,34},{3,35},{4,36},{5,37},{6,38},{7,39},{8,40},{9,... | collective-permute-start | bytes 1572872 | tf_op jit(solution)/shard_map/ppermute | solution.py:29
  92.6 3.2 %collective-permute-start.19 = (bf16[64,2560]{1,0:T(8,128)(2,1)S(1)}, bf16[64,2560]{1,0:T(8,128)(2,1)S(1)}, u32[]{:S(2)}, u32[]{:S(2)}) collective-permute-start(bf16[64,2560]{1,0:T(8,128)(2,1)S(1)} %collective-permute-done.17), channel_id=1, source_target_pairs={{0,30},{1,31},{2,0},{3,1},{4,2},{5,3},{6,4},{7,5},{8,6},{9,7},{10,... | collective-permute-start | bytes 983048 | tf_op jit(solution)/shard_map/ppermute | solution.py:29
  97.2 3.6 %collective-permute-done.8 = bf16[128,2048]{1,0:T(8,128)(2,1)S(1)} collective-permute-done((bf16[128,2048]{1,0:T(8,128)(2,1)S(1)}, bf16[128,2048]{1,0:T(8,128)(2,1)S(1)}, u32[]{:S(2)}, u32[]{:S(2)}) %collective-permute-start.8) | collective-permute-done | bytes 524320 | tf_op jit(solution)/shard_map/ppermute | solution.py:29
  100.8 3.5 %collective-permute-done.9 = bf16[128,2048]{1,0:T(8,128)(2,1)S(1)} collective-permute-done((bf16[128,2048]{1,0:T(8,128)(2,1)S(1)}, bf16[128,2048]{1,0:T(8,128)(2,1)S(1)}, u32[]{:S(2)}, u32[]{:S(2)}) %collective-permute-start.9) | collective-permute-done | bytes 524320 | tf_op jit(solution)/shard_map/ppermute | solution.py:29
  104.6 3.3 %collective-permute-start.21 = (bf16[32,2560]{1,0:T(8,128)(2,1)S(1)}, bf16[32,2560]{1,0:T(8,128)(2,1)S(1)}, u32[]{:S(2)}, u32[]{:S(2)}) collective-permute-start(bf16[32,2560]{1,0:T(8,128)(2,1)S(1)} %slice.170), channel_id=1, source_target_pairs={{0,30},{1,31},{2,0},{3,1},{4,2},{5,3},{6,4},{7,5},{8,6},{9,7},{10,... | collective-permute-start | bytes 491528 | tf_op jit(solution)/shard_map/ppermute | solution.py:29
  109.3 1.8 collective-permute-done.20
  112.4 3.3 %project_in.5 = f32[2,256,512]{2,1,0:T(8,128)} custom-call(s32[1]{0:T(128)} %bitcast.45.pair_ref, bf16[4,256,2048]{2,1,0:T(8,128)(2,1)S(1)} %bitcast_dynamic-update-slice_fusion.2.x_ref, bf16[16,64,1536]{2,1,0:T(8,128)(2,1)S(1)} %fusion.1.w_ref), custom_call_target="tpu_custom_call" | custom-call | tf_op jit(solution)/shard_map/project_in/pallas_call | solution.py:57
  116.2 1.2 project_in.7
  117.6 1.2 project_in.6.a_ref
  122.0 9.4 %all-to-all-start = ((bf16[32,40,128]{2,1,0:T(8,128)(2,1)}), bf16[32,40,128]{2,1,0:T(8,128)(2,1)}, u32[]{:S(2)}, u32[]{:S(2)}) async-start(bf16[32,40,128]{2,1,0:T(8,128)(2,1)} %bitcast.115), calls=%async_computation | async-start | bytes 655360 | tf_op jit(solution)/shard_map/all_to_all | solution.py:347
  131.4 2.2 %copy-done.2 = bf16[4,256,2048]{2,1,0:T(8,128)(2,1)S(1)} copy-done((bf16[4,256,2048]{2,1,0:T(8,128)(2,1)S(1)}, bf16[4,256,2048]{2,1,0:T(8,128)(2,1)}, u32[]{:S(2)}) %copy-start.2) | copy-done | bytes 4194328
  133.6 2.3 %project_in.4.a_ref = f32[2,256,512]{2,1,0:T(8,128)S(1)} custom-call(s32[1]{0:T(128)} %bitcast.1.pair_ref, bf16[4,256,2048]{2,1,0:T(8,128)(2,1)S(1)} %copy-done.2, bf16[16,64,1536]{2,1,0:T(8,128)(2,1)S(1)} %fusion.1.w_ref), custom_call_target="tpu_custom_call" | custom-call | tf_op jit(solution)/shard_map/project_in/pallas_call | solution.py:57
  135.9 5.2 %attend.1.a0 = bf16[512,512]{1,0:T(8,128)(2,1)S(1)} custom-call(f32[2,256,512]{2,1,0:T(8,128)S(1)} %project_in.4.a_ref, f32[2,256,512]{2,1,0:T(8,128)} %collective-permute-done.22.b_ref, bf16[2,256,128]{2,1,0:T(8,128)(2,1)S(1)} %copy-done.11, bf16[2,256,128]{2,1,0:T(8,128)(2,1)S(1)} %copy-done.13, bf16[64,896]{1,0:T(8,128)(2,1)S(1)} %get-tuple-element.74.n0_ref, ...), custom_call_target="tpu_custom_call" | custom-call | tf_op jit(solution)/shard_map/attend/pallas_call | solution.py:214
  141.3 2.0 collective-permute-start.24
  143.3 11.4 %collective-permute-done.25.a4 = bf16[512,512]{1,0:T(8,128)(2,1)S(1)} collective-permute-done((bf16[512,512]{1,0:T(8,128)(2,1)S(1)}, bf16[512,512]{1,0:T(8,128)(2,1)S(1)}, u32[]{:S(2)}, u32[]{:S(2)}) %collective-permute-start.25) | collective-permute-done | bytes 524320 | tf_op jit(solution)/shard_map/ppermute | solution.py:29
  154.7 1.6 collective-permute-start.26
  157.0 4.9 %collective-permute-done.26.a2 = bf16[256,512]{1,0:T(8,128)(2,1)S(1)} collective-permute-done((bf16[256,512]{1,0:T(8,128)(2,1)S(1)}, bf16[256,512]{1,0:T(8,128)(2,1)S(1)}, u32[]{:S(2)}, u32[]{:S(2)}) %collective-permute-start.26) | collective-permute-done | bytes 262176 | tf_op jit(solution)/shard_map/ppermute | solution.py:29
  162.6 2.0 collective-permute-done.27.a3
  165.3 0.9 copy-done.7
  166.3 0.9 copy-done.9
  167.2 5.0 %project_out.1 = bf16[512,1024]{1,0:T(8,128)(2,1)S(1)} custom-call(s32[1]{0:T(128)} %bitcast.shift_ref, bf16[512,512]{1,0:T(8,128)(2,1)S(1)} %attend.1.a0, bf16[512,512]{1,0:T(8,128)(2,1)S(1)} %collective-permute-done.24.a1, bf16[256,512]{1,0:T(8,128)(2,1)S(1)} %copy-done.7, bf16[256,512]{1,0:T(8,128)(2,1)S(1)} %copy-done.9, ...), custom_call_target="tpu_custom_call" | custom-call | tf_op jit(solution)/shard_map/project_out/pallas_call | solution.py:253
  173.1 2.9 %collective-permute-start.30 = (bf16[256,1024]{1,0:T(8,128)(2,1)S(1)}, bf16[256,1024]{1,0:T(8,128)(2,1)S(1)}, u32[]{:S(2)}, u32[]{:S(2)}) collective-permute-start(bf16[256,1024]{1,0:T(8,128)(2,1)S(1)} %get-tuple-element.73), channel_id=1, source_target_pairs={{0,0},{1,64},{2,2},{3,66},{4,4},{5,68},{6,6},{7,70},{8,8},{9,72},{... | collective-permute-start | bytes 1572872 | tf_op jit(solution)/shard_map/ppermute | solution.py:29
  175.9 2.7 %sort_pieces.1 = bf16[64,16,128]{2,1,0:T(8,128)(2,1)} custom-call(bf16[32,40,128]{2,1,0:T(8,128)(2,1)} %all-to-all-done.in_ref), custom_call_target="tpu_custom_call" | custom-call | tf_op jit(solution)/shard_map/sort_pieces/pallas_call | solution.py:155
  178.7 19.1 %all-to-all-start.1 = ((bf16[64,16,128]{2,1,0:T(8,128)(2,1)}), bf16[64,16,128]{2,1,0:T(8,128)(2,1)S(1)}, u32[]{:S(2)}, u32[]{:S(2)}) async-start(bf16[64,16,128]{2,1,0:T(8,128)(2,1)} %sort_pieces.1), calls=%async_computation.1 | async-start | bytes 524288 | tf_op jit(solution)/shard_map/all_to_all | solution.py:370
  197.9 1.1 maximum_bitcast_fusion
  198.9 17.0 %all-to-all-done.1 = bf16[64,16,128]{2,1,0:T(8,128)(2,1)S(1)} async-done(((bf16[64,16,128]{2,1,0:T(8,128)(2,1)}), bf16[64,16,128]{2,1,0:T(8,128)(2,1)S(1)}, u32[]{:S(2)}, u32[]{:S(2)}) %all-to-all-start.1) | async-done | bytes 262176 | tf_op jit(solution)/shard_map/all_to_all | solution.py:370
  (123 shorter events, 22.0 us)
Async XLA Ops:
  0.6 11.5 %copy-start.15 = (bf16[1024,64]{0,1:T(8,128)(2,1)S(1)}, bf16[1024,64]{0,1:T(8,128)(2,1)}, u32[]{:S(2)}) copy-start(bf16[1024,64]{0,1:T(8,128)(2,1)} %param.11) | copy-start | bytes 393220
  4.2 5.6 %collective-permute-start = (bf16[64,896]{1,0:T(8,128)(2,1)S(1)}, bf16[64,896]{1,0:T(8,128)(2,1)S(1)}, u32[]{:S(2)}, u32[]{:S(2)}) collective-permute-start(bf16[64,896]{1,0:T(8,128)(2,1)S(1)} %get-tuple-element.82), channel_id=1, source_target_pairs={{0,32},{1,96},{2,34},{3,98},{4,36},{5,100},{6,38},{7,102},{8,40},{... | collective-permute-start | bytes 344072 | tf_op jit(solution)/shard_map/ppermute | solution.py:29
  4.4 7.6 %collective-permute-start.1 = (bf16[64,896]{1,0:T(8,128)(2,1)S(1)}, bf16[64,896]{1,0:T(8,128)(2,1)S(1)}, u32[]{:S(2)}, u32[]{:S(2)}) collective-permute-start(bf16[64,896]{1,0:T(8,128)(2,1)S(1)} %get-tuple-element.83), channel_id=1, source_target_pairs={{0,0},{1,64},{2,2},{3,66},{4,4},{5,68},{6,6},{7,70},{8,8},{9,72},{... | collective-permute-start | bytes 344072 | tf_op jit(solution)/shard_map/ppermute | solution.py:29
  12.1 23.8 %copy-start.14 = (bf16[64,768]{1,0:T(8,128)(2,1)}, bf16[64,768]{1,0:T(8,128)(2,1)S(1)}, u32[]{:S(2)}) copy-start(bf16[64,768]{1,0:T(8,128)(2,1)S(1)} %slice.178) | copy-start | bytes 294916
  12.9 28.6 %collective-permute-start.2 = (bf16[64,2560]{1,0:T(8,128)(2,1)}, bf16[64,2560]{1,0:T(8,128)(2,1)}, u32[]{:S(2)}, u32[]{:S(2)}) collective-permute-start(bf16[64,2560]{1,0:T(8,128)(2,1)} %pad_maximum_fusion), channel_id=1, source_target_pairs={{0,2},{1,3},{2,4},{3,5},{4,6},{5,7},{6,8},{7,9},{8,10},{9,11},{10,... | collective-permute-start | bytes 983048 | tf_op jit(solution)/shard_map/ppermute | solution.py:29
  15.6 25.8 %collective-permute-start.3 = (bf16[64,2560]{1,0:T(8,128)(2,1)}, bf16[64,2560]{1,0:T(8,128)(2,1)}, u32[]{:S(2)}, u32[]{:S(2)}) collective-permute-start(bf16[64,2560]{1,0:T(8,128)(2,1)} %pad_maximum_fusion), channel_id=1, source_target_pairs={{0,30},{1,31},{2,0},{3,1},{4,2},{5,3},{6,4},{7,5},{8,6},{9,7},{10,... | collective-permute-start | bytes 983048 | tf_op jit(solution)/shard_map/ppermute | solution.py:29
  35.9 1.9 copy-start.3
  41.5 8.8 %collective-permute-start.4 = (bf16[64,2560]{1,0:T(8,128)(2,1)}, bf16[64,2560]{1,0:T(8,128)(2,1)S(1)}, u32[]{:S(2)}, u32[]{:S(2)}) collective-permute-start(bf16[64,2560]{1,0:T(8,128)(2,1)} %collective-permute-done.2), channel_id=1, source_target_pairs={{0,2},{1,3},{2,4},{3,5},{4,6},{5,7},{6,8},{7,9},{8,10},{9,11},{10,... | collective-permute-start | bytes 983048 | tf_op jit(solution)/shard_map/ppermute | solution.py:29
  41.5 8.8 %collective-permute-start.5 = (bf16[64,2560]{1,0:T(8,128)(2,1)}, bf16[64,2560]{1,0:T(8,128)(2,1)S(1)}, u32[]{:S(2)}, u32[]{:S(2)}) collective-permute-start(bf16[64,2560]{1,0:T(8,128)(2,1)} %collective-permute-done.3), channel_id=1, source_target_pairs={{0,30},{1,31},{2,0},{3,1},{4,2},{5,3},{6,4},{7,5},{8,6},{9,7},{10,... | collective-permute-start | bytes 983048 | tf_op jit(solution)/shard_map/ppermute | solution.py:29
  52.6 33.5 %collective-permute-start.6 = (bf16[256,2048]{1,0:T(8,128)(2,1)S(1)}, bf16[256,2048]{1,0:T(8,128)(2,1)S(1)}, u32[]{:S(2)}, u32[]{:S(2)}) collective-permute-start(bf16[256,2048]{1,0:T(8,128)(2,1)S(1)} %get-tuple-element.68), channel_id=1, source_target_pairs={{0,32},{1,33},{2,34},{3,35},{4,36},{5,37},{6,38},{7,39},{8,40},{9,... | collective-permute-start | bytes 3145736 | tf_op jit(solution)/shard_map/ppermute | solution.py:29
  52.6 39.4 %collective-permute-start.7 = (bf16[256,2048]{1,0:T(8,128)(2,1)S(1)}, bf16[256,2048]{1,0:T(8,128)(2,1)S(1)}, u32[]{:S(2)}, u32[]{:S(2)}) collective-permute-start(bf16[256,2048]{1,0:T(8,128)(2,1)S(1)} %get-tuple-element.68), channel_id=1, source_target_pairs={{0,96},{1,97},{2,98},{3,99},{4,100},{5,101},{6,102},{7,103},{8,104... | collective-permute-start | bytes 3145736 | tf_op jit(solution)/shard_map/ppermute | solution.py:29
  54.6 9.6 %collective-permute-start.10 = (bf16[64,2560]{1,0:T(8,128)(2,1)S(1)}, bf16[64,2560]{1,0:T(8,128)(2,1)S(1)}, u32[]{:S(2)}, u32[]{:S(2)}) collective-permute-start(bf16[64,2560]{1,0:T(8,128)(2,1)S(1)} %collective-permute-done.4), channel_id=1, source_target_pairs={{0,2},{1,3},{2,4},{3,5},{4,6},{5,7},{6,8},{7,9},{8,10},{9,11},{10,... | collective-permute-start | bytes 983048 | tf_op jit(solution)/shard_map/ppermute | solution.py:29
  54.6 9.6 %collective-permute-start.11 = (bf16[64,2560]{1,0:T(8,128)(2,1)S(1)}, bf16[64,2560]{1,0:T(8,128)(2,1)S(1)}, u32[]{:S(2)}, u32[]{:S(2)}) collective-permute-start(bf16[64,2560]{1,0:T(8,128)(2,1)S(1)} %collective-permute-done.5), channel_id=1, source_target_pairs={{0,30},{1,31},{2,0},{3,1},{4,2},{5,3},{6,4},{7,5},{8,6},{9,7},{10,... | collective-permute-start | bytes 983048 | tf_op jit(solution)/shard_map/ppermute | solution.py:29
  58.6 33.7 %copy-start = (bf16[4,256,2048]{2,1,0:T(8,128)(2,1)S(1)}, bf16[4,256,2048]{2,1,0:T(8,128)(2,1)}, u32[]{:S(2)}) copy-start(bf16[4,256,2048]{2,1,0:T(8,128)(2,1)} %get-tuple-element.69) | copy-start | bytes 12582916
  64.2 8.7 %collective-permute-start.12 = (bf16[64,2560]{1,0:T(8,128)(2,1)S(1)}, bf16[64,2560]{1,0:T(8,128)(2,1)S(1)}, u32[]{:S(2)}, u32[]{:S(2)}) collective-permute-start(bf16[64,2560]{1,0:T(8,128)(2,1)S(1)} %collective-permute-done.10), channel_id=1, source_target_pairs={{0,2},{1,3},{2,4},{3,5},{4,6},{5,7},{6,8},{7,9},{8,10},{9,11},{10,... | collective-permute-start | bytes 983048 | tf_op jit(solution)/shard_map/ppermute | solution.py:29
  64.2 8.7 %collective-permute-start.13 = (bf16[64,2560]{1,0:T(8,128)(2,1)S(1)}, bf16[64,2560]{1,0:T(8,128)(2,1)S(1)}, u32[]{:S(2)}, u32[]{:S(2)}) collective-permute-start(bf16[64,2560]{1,0:T(8,128)(2,1)S(1)} %collective-permute-done.11), channel_id=1, source_target_pairs={{0,30},{1,31},{2,0},{3,1},{4,2},{5,3},{6,4},{7,5},{8,6},{9,7},{10,... | collective-permute-start | bytes 983048 | tf_op jit(solution)/shard_map/ppermute | solution.py:29
  73.0 8.3 %collective-permute-start.14 = (bf16[64,2560]{1,0:T(8,128)(2,1)S(1)}, bf16[64,2560]{1,0:T(8,128)(2,1)S(1)}, u32[]{:S(2)}, u32[]{:S(2)}) collective-permute-start(bf16[64,2560]{1,0:T(8,128)(2,1)S(1)} %collective-permute-done.12), channel_id=1, source_target_pairs={{0,2},{1,3},{2,4},{3,5},{4,6},{5,7},{6,8},{7,9},{8,10},{9,11},{10,... | collective-permute-start | bytes 983048 | tf_op jit(solution)/shard_map/ppermute | solution.py:29
  73.0 8.3 %collective-permute-start.15 = (bf16[64,2560]{1,0:T(8,128)(2,1)S(1)}, bf16[64,2560]{1,0:T(8,128)(2,1)S(1)}, u32[]{:S(2)}, u32[]{:S(2)}) collective-permute-start(bf16[64,2560]{1,0:T(8,128)(2,1)S(1)} %collective-permute-done.13), channel_id=1, source_target_pairs={{0,30},{1,31},{2,0},{3,1},{4,2},{5,3},{6,4},{7,5},{8,6},{9,7},{10,... | collective-permute-start | bytes 983048 | tf_op jit(solution)/shard_map/ppermute | solution.py:29
  81.3 11.2 %collective-permute-start.16 = (bf16[64,2560]{1,0:T(8,128)(2,1)S(1)}, bf16[64,2560]{1,0:T(8,128)(2,1)S(1)}, u32[]{:S(2)}, u32[]{:S(2)}) collective-permute-start(bf16[64,2560]{1,0:T(8,128)(2,1)S(1)} %collective-permute-done.14), channel_id=1, source_target_pairs={{0,2},{1,3},{2,4},{3,5},{4,6},{5,7},{6,8},{7,9},{8,10},{9,11},{10,... | collective-permute-start | bytes 983048 | tf_op jit(solution)/shard_map/ppermute | solution.py:29
  81.3 11.2 %collective-permute-start.17 = (bf16[64,2560]{1,0:T(8,128)(2,1)S(1)}, bf16[64,2560]{1,0:T(8,128)(2,1)S(1)}, u32[]{:S(2)}, u32[]{:S(2)}) collective-permute-start(bf16[64,2560]{1,0:T(8,128)(2,1)S(1)} %collective-permute-done.15), channel_id=1, source_target_pairs={{0,30},{1,31},{2,0},{3,1},{4,2},{5,3},{6,4},{7,5},{8,6},{9,7},{10,... | collective-permute-start | bytes 983048 | tf_op jit(solution)/shard_map/ppermute | solution.py:29
  86.2 14.6 %collective-permute-start.8 = (bf16[128,2048]{1,0:T(8,128)(2,1)S(1)}, bf16[128,2048]{1,0:T(8,128)(2,1)S(1)}, u32[]{:S(2)}, u32[]{:S(2)}) collective-permute-start(bf16[128,2048]{1,0:T(8,128)(2,1)S(1)} %slice.180), channel_id=1, source_target_pairs={{0,32},{1,33},{2,34},{3,35},{4,36},{5,37},{6,38},{7,39},{8,40},{9,... | collective-permute-start | bytes 1572872 | tf_op jit(solution)/shard_map/ppermute | solution.py:29
  92.1 12.2 %collective-permute-start.9 = (bf16[128,2048]{1,0:T(8,128)(2,1)S(1)}, bf16[128,2048]{1,0:T(8,128)(2,1)S(1)}, u32[]{:S(2)}, u32[]{:S(2)}) collective-permute-start(bf16[128,2048]{1,0:T(8,128)(2,1)S(1)} %slice.181), channel_id=1, source_target_pairs={{0,96},{1,97},{2,98},{3,99},{4,100},{5,101},{6,102},{7,103},{8,104... | collective-permute-start | bytes 1572872 | tf_op jit(solution)/shard_map/ppermute | solution.py:29
  92.5 11.9 %collective-permute-start.18 = (bf16[64,2560]{1,0:T(8,128)(2,1)S(1)}, bf16[64,2560]{1,0:T(8,128)(2,1)S(1)}, u32[]{:S(2)}, u32[]{:S(2)}) collective-permute-start(bf16[64,2560]{1,0:T(8,128)(2,1)S(1)} %collective-permute-done.16), channel_id=1, source_target_pairs={{0,2},{1,3},{2,4},{3,5},{4,6},{5,7},{6,8},{7,9},{8,10},{9,11},{10,... | collective-permute-start | bytes 983048 | tf_op jit(solution)/shard_map/ppermute | solution.py:29
  92.6 11.8 %collective-permute-start.19 = (bf16[64,2560]{1,0:T(8,128)(2,1)S(1)}, bf16[64,2560]{1,0:T(8,128)(2,1)S(1)}, u32[]{:S(2)}, u32[]{:S(2)}) collective-permute-start(bf16[64,2560]{1,0:T(8,128)(2,1)S(1)} %collective-permute-done.17), channel_id=1, source_target_pairs={{0,30},{1,31},{2,0},{3,1},{4,2},{5,3},{6,4},{7,5},{8,6},{9,7},{10,... | collective-permute-start | bytes 983048 | tf_op jit(solution)/shard_map/ppermute | solution.py:29
  104.4 13.1 %copy-start.1 = (bf16[4,256,2048]{2,1,0:T(8,128)(2,1)}, bf16[4,256,2048]{2,1,0:T(8,128)(2,1)S(1)}, u32[]{:S(2)}) copy-start(bf16[4,256,2048]{2,1,0:T(8,128)(2,1)S(1)} %bitcast_dynamic-update-slice_fusion.2.x_ref) | copy-start | bytes 12582916
  104.5 6.6 %collective-permute-start.20 = (bf16[32,2560]{1,0:T(8,128)(2,1)S(1)}, bf16[32,2560]{1,0:T(8,128)(2,1)S(1)}, u32[]{:S(2)}, u32[]{:S(2)}) collective-permute-start(bf16[32,2560]{1,0:T(8,128)(2,1)S(1)} %slice.168), channel_id=1, source_target_pairs={{0,2},{1,3},{2,4},{3,5},{4,6},{5,7},{6,8},{7,9},{8,10},{9,11},{10,... | collective-permute-start | bytes 491528 | tf_op jit(solution)/shard_map/ppermute | solution.py:29
  104.6 7.1 %collective-permute-start.21 = (bf16[32,2560]{1,0:T(8,128)(2,1)S(1)}, bf16[32,2560]{1,0:T(8,128)(2,1)S(1)}, u32[]{:S(2)}, u32[]{:S(2)}) collective-permute-start(bf16[32,2560]{1,0:T(8,128)(2,1)S(1)} %slice.170), channel_id=1, source_target_pairs={{0,30},{1,31},{2,0},{3,1},{4,2},{5,3},{6,4},{7,5},{8,6},{9,7},{10,... | collective-permute-start | bytes 491528 | tf_op jit(solution)/shard_map/ppermute | solution.py:29
  112.4 53.0 %collective-permute-start.28 = (bf16[1024,1024]{1,0:T(8,128)(2,1)}, bf16[1024,1024]{1,0:T(8,128)(2,1)}, u32[]{:S(2)}, u32[]{:S(2)}) collective-permute-start(bf16[1024,1024]{1,0:T(8,128)(2,1)} %bitcast.50.near_ref), channel_id=1, source_target_pairs={{0,1},{1,0},{2,3},{3,2},{4,5},{5,4},{6,7},{7,6},{8,9},{9,8},{10,11... | collective-permute-start | bytes 6291464 | tf_op jit(solution)/shard_map/ppermute | solution.py:29
  115.7 20.2 %collective-permute-start.22 = (f32[2,256,512]{2,1,0:T(8,128)}, f32[2,256,512]{2,1,0:T(8,128)}, u32[]{:S(2)}, u32[]{:S(2)}) collective-permute-start(f32[2,256,512]{2,1,0:T(8,128)} %project_in.5), channel_id=1, source_target_pairs={{0,1},{1,0},{2,3},{3,2},{4,5},{5,4},{6,7},{7,6},{8,9},{9,8},{10,11... | collective-permute-start | bytes 3145736 | tf_op jit(solution)/shard_map/ppermute | solution.py:29
  117.4 2.0 collective-permute-start.23
  117.5 1.9 copy-start.4
  119.9 0.8 copy-start.5
  121.4 0.7 copy-start.12
  122.0 53.9 %all-to-all-start = ((bf16[32,40,128]{2,1,0:T(8,128)(2,1)}), bf16[32,40,128]{2,1,0:T(8,128)(2,1)}, u32[]{:S(2)}, u32[]{:S(2)}) async-start(bf16[32,40,128]{2,1,0:T(8,128)(2,1)} %bitcast.115), calls=%async_computation | async-start | bytes 655360 | tf_op jit(solution)/shard_map/all_to_all | solution.py:347
  131.4 2.2 %copy-start.2 = (bf16[4,256,2048]{2,1,0:T(8,128)(2,1)S(1)}, bf16[4,256,2048]{2,1,0:T(8,128)(2,1)}, u32[]{:S(2)}) copy-start(bf16[4,256,2048]{2,1,0:T(8,128)(2,1)} %copy-done.1) | copy-start | bytes 12582916
  133.6 2.3 %copy-start.11 = (bf16[2,256,128]{2,1,0:T(8,128)(2,1)S(1)}, bf16[2,256,128]{2,1,0:T(8,128)(2,1)}, u32[]{:S(2)}) copy-start(bf16[2,256,128]{2,1,0:T(8,128)(2,1)} %copy-done.10) | copy-start | bytes 393220
  133.6 2.3 %copy-start.13 = (bf16[2,256,128]{2,1,0:T(8,128)(2,1)S(1)}, bf16[2,256,128]{2,1,0:T(8,128)(2,1)}, u32[]{:S(2)}) copy-start(bf16[2,256,128]{2,1,0:T(8,128)(2,1)} %copy-done.12) | copy-start | bytes 393220
  141.1 13.6 %collective-permute-start.25 = (bf16[512,512]{1,0:T(8,128)(2,1)S(1)}, bf16[512,512]{1,0:T(8,128)(2,1)S(1)}, u32[]{:S(2)}, u32[]{:S(2)}) collective-permute-start(bf16[512,512]{1,0:T(8,128)(2,1)S(1)} %attend.1.a0), channel_id=1, source_target_pairs={{0,32},{1,33},{2,34},{3,35},{4,36},{5,37},{6,38},{7,39},{8,40},{9,... | collective-permute-start | bytes 1572872 | tf_op jit(solution)/shard_map/ppermute | solution.py:29
  141.3 15.1 %collective-permute-start.24 = (bf16[512,512]{1,0:T(8,128)(2,1)S(1)}, bf16[512,512]{1,0:T(8,128)(2,1)S(1)}, u32[]{:S(2)}, u32[]{:S(2)}) collective-permute-start(bf16[512,512]{1,0:T(8,128)(2,1)S(1)} %attend.1.a0), channel_id=1, source_target_pairs={{0,96},{1,97},{2,98},{3,99},{4,100},{5,101},{6,102},{7,103},{8,104... | collective-permute-start | bytes 1572872 | tf_op jit(solution)/shard_map/ppermute | solution.py:29
  154.7 7.2 %collective-permute-start.26 = (bf16[256,512]{1,0:T(8,128)(2,1)S(1)}, bf16[256,512]{1,0:T(8,128)(2,1)S(1)}, u32[]{:S(2)}, u32[]{:S(2)}) collective-permute-start(bf16[256,512]{1,0:T(8,128)(2,1)S(1)} %slice.184), channel_id=1, source_target_pairs={{0,32},{1,33},{2,34},{3,35},{4,36},{5,37},{6,38},{7,39},{8,40},{9,... | collective-permute-start | bytes 786440 | tf_op jit(solution)/shard_map/ppermute | solution.py:29
  156.3 8.3 %collective-permute-start.27 = (bf16[256,512]{1,0:T(8,128)(2,1)S(1)}, bf16[256,512]{1,0:T(8,128)(2,1)S(1)}, u32[]{:S(2)}, u32[]{:S(2)}) collective-permute-start(bf16[256,512]{1,0:T(8,128)(2,1)S(1)} %slice.185), channel_id=1, source_target_pairs={{0,96},{1,97},{2,98},{3,99},{4,100},{5,101},{6,102},{7,103},{8,104... | collective-permute-start | bytes 786440 | tf_op jit(solution)/shard_map/ppermute | solution.py:29
  161.9 0.7 copy-start.6
  164.6 0.7 copy-start.8
  165.3 1.0 copy-start.7
  166.3 0.9 copy-start.9
  173.1 24.7 %collective-permute-start.29 = (bf16[256,1024]{1,0:T(8,128)(2,1)}, bf16[256,1024]{1,0:T(8,128)(2,1)S(1)}, u32[]{:S(2)}, u32[]{:S(2)}) collective-permute-start(bf16[256,1024]{1,0:T(8,128)(2,1)} %get-tuple-element.72), channel_id=1, source_target_pairs={{0,32},{1,96},{2,34},{3,98},{4,36},{5,100},{6,38},{7,102},{8,40},{... | collective-permute-start | bytes 1572872 | tf_op jit(solution)/shard_map/ppermute | solution.py:29
  173.1 24.7 %collective-permute-start.30 = (bf16[256,1024]{1,0:T(8,128)(2,1)S(1)}, bf16[256,1024]{1,0:T(8,128)(2,1)S(1)}, u32[]{:S(2)}, u32[]{:S(2)}) collective-permute-start(bf16[256,1024]{1,0:T(8,128)(2,1)S(1)} %get-tuple-element.73), channel_id=1, source_target_pairs={{0,0},{1,64},{2,2},{3,66},{4,4},{5,68},{6,6},{7,70},{8,8},{9,72},{... | collective-permute-start | bytes 1572872 | tf_op jit(solution)/shard_map/ppermute | solution.py:29
  178.7 37.2 %all-to-all-start.1 = ((bf16[64,16,128]{2,1,0:T(8,128)(2,1)}), bf16[64,16,128]{2,1,0:T(8,128)(2,1)S(1)}, u32[]{:S(2)}, u32[]{:S(2)}) async-start(bf16[64,16,128]{2,1,0:T(8,128)(2,1)} %sort_pieces.1), calls=%async_computation.1 | async-start | bytes 524288 | tf_op jit(solution)/shard_map/all_to_all | solution.py:370
  (1 other events, 0.7 us)

commit v3 on v2

--- a/solution.py
+++ b/solution.py
@@ -124,9 +124,9 @@
         in_specs=[rows, rows, note, note, pl.BlockSpec((total, HD), lambda s: (0, 0))],
         out_specs=[each, each, pl.BlockSpec(sent, lambda s: (0, 0, 0, 0))],
         out_shape=[
-            jax.ShapeDtypeStruct((2, total, HD), jnp.bfloat16),
-            jax.ShapeDtypeStruct((2, total, HD), jnp.bfloat16),
-            jax.ShapeDtypeStruct(sent, jnp.bfloat16),
+            pltpu.HBM((2, total, HD), jnp.bfloat16),
+            pltpu.HBM((2, total, HD), jnp.bfloat16),
+            pltpu.HBM(sent, jnp.bfloat16),
         ],
         compiler_params=pltpu.CompilerParams(vmem_limit_bytes=24 << 20),
         name="make_cache",
@@ -222,14 +222,22 @@
     )(kept, other, keys, values, first, second, turns(total))
 
 
-def output_kernel(shift_ref, a0, a1, a2, a3, a4, near_ref, far_ref, out_ref, line_ref):
-    half = a0.shape[0] // 2
+def output_kernel(shift_ref, a0, a1, a2, a3, a4, near_ref, far_ref, out_ref, line_ref, sems):
+    half = a2.shape[0]
 
     @pl.when(pl.program_id(0) == 0)
     def _():
-        for d, start, rows in ((0, 0, a0), (1, 0, a1), (2, 0, a2), (2, half, a3), (3, 0, a4)):
-            place = (d + shift_ref[0]) % X
-            line_ref[place, start : start + rows.shape[0], :] = rows[...]
+        place = (2 + shift_ref[0]) % X
+        copies = [
+            pltpu.make_async_copy(rows, line_ref.at[place, pl.ds(k * half, half)], sems.at[k])
+            for k, rows in enumerate((a2, a3))
+        ]
+        for copy in copies:
+            copy.start()
+        for d, rows in ((0, a0), (1, a1), (3, a4)):
+            line_ref[(d + shift_ref[0]) % X] = rows[...]
+        for copy in copies:
+            copy.wait()
 
     group = a0.shape[1]
     total = 0.0
@@ -248,7 +256,8 @@
 def project_out(mine, after, across, before, near, far, shift, pieces=4):
     total, group = mine.shape
     columns = near.shape[0]
-    whole = part = pl.BlockSpec(memory_space=pltpu.VMEM)
+    whole = pl.BlockSpec(memory_space=pltpu.VMEM)
+    part = pl.BlockSpec(memory_space=pl.ANY)
     weights = pl.BlockSpec((columns // pieces, near.shape[1]), lambda i, w: (i, 0))
     return pl.pallas_call(
         output_kernel,
@@ -257,7 +266,10 @@
             grid=(pieces,),
             in_specs=[whole, whole, part, part, whole, weights, weights],
             out_specs=pl.BlockSpec((total, columns // pieces), lambda i, w: (0, i)),
-            scratch_shapes=[pltpu.VMEM((X, total, group), mine.dtype)],
+            scratch_shapes=[
+                pltpu.VMEM((X, total, group), mine.dtype),
+                pltpu.SemaphoreType.DMA((2,)),
+            ],
         ),
         out_shape=jax.ShapeDtypeStruct((total, columns), jnp.bfloat16),
         compiler_params=pltpu.CompilerParams(vmem_limit_bytes=24 << 20),
@@ -344,9 +356,7 @@
     other = move(project_in(states, full_in, 1 - t, pieces, 1), swap)
     kept = project_in(states, full_in, t, pieces, 1)
     keys, values, sent = make_cache(kept, other, first, second, ring)
-    spread = lax.all_to_all(
-        sent.reshape(-1, *sent.shape[2:]), ("z", "tensor"), 0, 0, tiled=True
-    )
+    spread = lax.all_to_all(sent.reshape(-1, *sent.shape[2:]), ("z", "tensor"), 0, 0, tiled=True)
     other = project_in(states, full_in, 1 - t, 0, pieces)
     other = move(other, swap)
     kept = project_in(states, full_in, t, 0, pieces)

time: 217 us -> 214 us (0.986)
  local copies, waits for them, and re-layouts: 31.1 us -> 25.6 us
    unnamed x32 -> x16, local copies, waits for them, and re-layouts: 9.47 us -> 4.1 us
where the time goes in v3:
time: 214 us
  starting transfers between devices  94.9 us (44%)
  waiting for transfers between devices  64.5 us (30%)
  local copies, waits for them, and re-layouts  25.6 us (12%)
  Pallas kernels  22.2 us (10%)
  other arithmetic  3.82 us (2%)
  between operations  2.57 us (1%)
    ppermute x31, starting transfers between devices, move(): return lax.ppermute(array, ('x', 'z', 'tensor'), pairs)  66.5 us
    ppermute x31, waiting for transfers between devices, move(): return lax.ppermute(array, ('x', 'z', 'tensor'), pairs)  47.6 us
    all_to_all x1, starting transfers between devices, on_device(): arrived = lax.all_to_all(sorted_pieces, ('x', 'z'), 0, 0, tiled=True)  19.1 us
    all_to_all x1, waiting for transfers between devices, on_device(): arrived = lax.all_to_all(sorted_pieces, ('x', 'z'), 0, 0, tiled=True)  16.9 us
    dynamic_update_slice x17, local copies, waits for them, and re-layouts, place(): lax.dynamic_update_slice(full[1], block[None, :, 2 * wide:], at)  13.1 us
    all_to_all x1, starting transfers between devices, on_device(): lax.all_to_all(sent.reshape(-1, *sent.shape[2:]), ('z', 'tensor'), 0, 0,...  9.3 us
    pallas_call x4, Pallas kernels, project_in(): pl.pallas_call(project_kernel, grid_spec=pltpu.PrefetchScalarGridSpec(num...  8.01 us
    pallas_call x1, Pallas kernels, attend(): pl.pallas_call(functools.partial(attend_kernel, wide // HD), grid=(2,), i...  5.17 us
  transfers between devices with their start and end apart: 33, of which 15 were waited for; matrix products, arithmetic and copies ran while one was open for 8% of the time, Pallas kernels for 10%

profile of v3, /device:TPU:38, one launch (start us, length us, event | category | flops | bytes accessed | tf_op | source)
XLA Modules:
  0.0 213.5 jit_solution(5599959925867569040)
XLA Ops:
  2.2 1.0 constant_dynamic-slice_fusion.1
  4.4 4.4 %collective-permute-start.1 = (bf16[64,896]{1,0:T(8,128)(2,1)S(1)}, bf16[64,896]{1,0:T(8,128)(2,1)S(1)}, u32[]{:S(2)}, u32[]{:S(2)}) collective-permute-start(bf16[64,896]{1,0:T(8,128)(2,1)S(1)} %get-tuple-element.83), channel_id=1, source_target_pairs={{0,0},{1,64},{2,2},{3,66},{4,4},{5,68},{6,6},{7,70},{8,8},{9,72},{... | collective-permute-start | bytes 344072 | tf_op jit(solution)/shard_map/ppermute | solution.py:29
  8.8 1.0 collective-permute-done
  9.8 2.2 %collective-permute-done.1 = bf16[64,896]{1,0:T(8,128)(2,1)S(1)} collective-permute-done((bf16[64,896]{1,0:T(8,128)(2,1)S(1)}, bf16[64,896]{1,0:T(8,128)(2,1)S(1)}, u32[]{:S(2)}, u32[]{:S(2)}) %collective-permute-start.1) | collective-permute-done | bytes 114720 | tf_op jit(solution)/shard_map/ppermute | solution.py:29
  12.7 1.6 pad_maximum_fusion
  14.4 2.8 %collective-permute-start.2 = (bf16[64,2560]{1,0:T(8,128)(2,1)}, bf16[64,2560]{1,0:T(8,128)(2,1)}, u32[]{:S(2)}, u32[]{:S(2)}) collective-permute-start(bf16[64,2560]{1,0:T(8,128)(2,1)} %pad_maximum_fusion), channel_id=1, source_target_pairs={{0,2},{1,3},{2,4},{3,5},{4,6},{5,7},{6,8},{7,9},{8,10},{9,11},{10,... | collective-permute-start | bytes 983048 | tf_op jit(solution)/shard_map/ppermute | solution.py:29
  17.1 19.6 %collective-permute-start.3 = (bf16[64,2560]{1,0:T(8,128)(2,1)}, bf16[64,2560]{1,0:T(8,128)(2,1)}, u32[]{:S(2)}, u32[]{:S(2)}) collective-permute-start(bf16[64,2560]{1,0:T(8,128)(2,1)} %pad_maximum_fusion), channel_id=1, source_target_pairs={{0,30},{1,31},{2,0},{3,1},{4,2},{5,3},{6,4},{7,5},{8,6},{9,7},{10,... | collective-permute-start | bytes 983048 | tf_op jit(solution)/shard_map/ppermute | solution.py:29
  37.4 1.9 copy-done.3
  40.2 2.8 %collective-permute-done.2 = bf16[64,2560]{1,0:T(8,128)(2,1)} collective-permute-done((bf16[64,2560]{1,0:T(8,128)(2,1)}, bf16[64,2560]{1,0:T(8,128)(2,1)}, u32[]{:S(2)}, u32[]{:S(2)}) %collective-permute-start.2) | collective-permute-done | bytes 327712 | tf_op jit(solution)/shard_map/ppermute | solution.py:29
  43.0 3.5 %collective-permute-start.5 = (bf16[64,2560]{1,0:T(8,128)(2,1)}, bf16[64,2560]{1,0:T(8,128)(2,1)S(1)}, u32[]{:S(2)}, u32[]{:S(2)}) collective-permute-start(bf16[64,2560]{1,0:T(8,128)(2,1)} %collective-permute-done.3), channel_id=1, source_target_pairs={{0,30},{1,31},{2,0},{3,1},{4,2},{5,3},{6,4},{7,5},{8,6},{9,7},{10,... | collective-permute-start | bytes 983048 | tf_op jit(solution)/shard_map/ppermute | solution.py:29
  46.5 0.9 bitcast_dynamic-update-slice_fusion.17
  47.4 0.9 bitcast_dynamic-update-slice_fusion.16
  48.4 1.6 bitcast_dynamic-update-slice_fusion.32
  50.0 1.6 bitcast_dynamic-update-slice_fusion.31
  51.8 2.3 %dynamic-slice_bitcast_fusion = (bf16[256,2048]{1,0:T(8,128)(2,1)S(1)}, bf16[4,256,2048]{2,1,0:T(8,128)(2,1)}) fusion(bf16[1,256,4096]{2,1,0:T(8,128)(2,1)} %param.8, s32[]{:T(128)S(6)} %select_n.250, bf16[4,256,2048]{2,1,0:T(8,128)(2,1)} %blank.3, s32[]{:T(128)S(6)} %select_n.252), kind=kLoop, calls=%fused_computation.3 | loop fusion | bytes 3145736 | tf_op jit(solution)/shard_map/dynamic_slice | solution.py:333
  54.1 2.0 collective-permute-start.7
  56.1 3.2 %collective-permute-start.11 = (bf16[64,2560]{1,0:T(8,128)(2,1)S(1)}, bf16[64,2560]{1,0:T(8,128)(2,1)S(1)}, u32[]{:S(2)}, u32[]{:S(2)}) collective-permute-start(bf16[64,2560]{1,0:T(8,128)(2,1)S(1)} %collective-permute-done.5), channel_id=1, source_target_pairs={{0,30},{1,31},{2,0},{3,1},{4,2},{5,3},{6,4},{7,5},{8,6},{9,7},{10,... | collective-permute-start | bytes 983048 | tf_op jit(solution)/shard_map/ppermute | solution.py:29
  60.7 5.0 %collective-permute-done.10 = bf16[64,2560]{1,0:T(8,128)(2,1)S(1)} collective-permute-done((bf16[64,2560]{1,0:T(8,128)(2,1)S(1)}, bf16[64,2560]{1,0:T(8,128)(2,1)S(1)}, u32[]{:S(2)}, u32[]{:S(2)}) %collective-permute-start.10) | collective-permute-done | bytes 327712 | tf_op jit(solution)/shard_map/ppermute | solution.py:29
  65.7 3.2 %collective-permute-start.13 = (bf16[64,2560]{1,0:T(8,128)(2,1)S(1)}, bf16[64,2560]{1,0:T(8,128)(2,1)S(1)}, u32[]{:S(2)}, u32[]{:S(2)}) collective-permute-start(bf16[64,2560]{1,0:T(8,128)(2,1)S(1)} %collective-permute-done.11), channel_id=1, source_target_pairs={{0,30},{1,31},{2,0},{3,1},{4,2},{5,3},{6,4},{7,5},{8,6},{9,7},{10,... | collective-permute-start | bytes 983048 | tf_op jit(solution)/shard_map/ppermute | solution.py:29
  70.4 4.1 %collective-permute-done.12 = bf16[64,2560]{1,0:T(8,128)(2,1)S(1)} collective-permute-done((bf16[64,2560]{1,0:T(8,128)(2,1)S(1)}, bf16[64,2560]{1,0:T(8,128)(2,1)S(1)}, u32[]{:S(2)}, u32[]{:S(2)}) %collective-permute-start.12) | collective-permute-done | bytes 327712 | tf_op jit(solution)/shard_map/ppermute | solution.py:29
  74.5 3.2 %collective-permute-start.15 = (bf16[64,2560]{1,0:T(8,128)(2,1)S(1)}, bf16[64,2560]{1,0:T(8,128)(2,1)S(1)}, u32[]{:S(2)}, u32[]{:S(2)}) collective-permute-start(bf16[64,2560]{1,0:T(8,128)(2,1)S(1)} %collective-permute-done.13), channel_id=1, source_target_pairs={{0,30},{1,31},{2,0},{3,1},{4,2},{5,3},{6,4},{7,5},{8,6},{9,7},{10,... | collective-permute-start | bytes 983048 | tf_op jit(solution)/shard_map/ppermute | solution.py:29
  79.1 3.7 %collective-permute-done.14 = bf16[64,2560]{1,0:T(8,128)(2,1)S(1)} collective-permute-done((bf16[64,2560]{1,0:T(8,128)(2,1)S(1)}, bf16[64,2560]{1,0:T(8,128)(2,1)S(1)}, u32[]{:S(2)}, u32[]{:S(2)}) %collective-permute-start.14) | collective-permute-done | bytes 327712 | tf_op jit(solution)/shard_map/ppermute | solution.py:29
  82.8 3.5 %collective-permute-start.17 = (bf16[64,2560]{1,0:T(8,128)(2,1)S(1)}, bf16[64,2560]{1,0:T(8,128)(2,1)S(1)}, u32[]{:S(2)}, u32[]{:S(2)}) collective-permute-start(bf16[64,2560]{1,0:T(8,128)(2,1)S(1)} %collective-permute-done.15), channel_id=1, source_target_pairs={{0,30},{1,31},{2,0},{3,1},{4,2},{5,3},{6,4},{7,5},{8,6},{9,7},{10,... | collective-permute-start | bytes 983048 | tf_op jit(solution)/shard_map/ppermute | solution.py:29
  87.7 5.9 %collective-permute-start.8 = (bf16[128,2048]{1,0:T(8,128)(2,1)S(1)}, bf16[128,2048]{1,0:T(8,128)(2,1)S(1)}, u32[]{:S(2)}, u32[]{:S(2)}) collective-permute-start(bf16[128,2048]{1,0:T(8,128)(2,1)S(1)} %slice.180), channel_id=1, source_target_pairs={{0,32},{1,33},{2,34},{3,35},{4,36},{5,37},{6,38},{7,39},{8,40},{9,... | collective-permute-start | bytes 1572872 | tf_op jit(solution)/shard_map/ppermute | solution.py:29
  94.2 3.2 %collective-permute-start.19 = (bf16[64,2560]{1,0:T(8,128)(2,1)S(1)}, bf16[64,2560]{1,0:T(8,128)(2,1)S(1)}, u32[]{:S(2)}, u32[]{:S(2)}) collective-permute-start(bf16[64,2560]{1,0:T(8,128)(2,1)S(1)} %collective-permute-done.17), channel_id=1, source_target_pairs={{0,30},{1,31},{2,0},{3,1},{4,2},{5,3},{6,4},{7,5},{8,6},{9,7},{10,... | collective-permute-start | bytes 983048 | tf_op jit(solution)/shard_map/ppermute | solution.py:29
  98.8 3.6 %collective-permute-done.8 = bf16[128,2048]{1,0:T(8,128)(2,1)S(1)} collective-permute-done((bf16[128,2048]{1,0:T(8,128)(2,1)S(1)}, bf16[128,2048]{1,0:T(8,128)(2,1)S(1)}, u32[]{:S(2)}, u32[]{:S(2)}) %collective-permute-start.8) | collective-permute-done | bytes 524320 | tf_op jit(solution)/shard_map/ppermute | solution.py:29
  102.4 3.5 %collective-permute-done.9 = bf16[128,2048]{1,0:T(8,128)(2,1)S(1)} collective-permute-done((bf16[128,2048]{1,0:T(8,128)(2,1)S(1)}, bf16[128,2048]{1,0:T(8,128)(2,1)S(1)}, u32[]{:S(2)}, u32[]{:S(2)}) %collective-permute-start.9) | collective-permute-done | bytes 524320 | tf_op jit(solution)/shard_map/ppermute | solution.py:29
  106.2 3.3 %collective-permute-start.21 = (bf16[32,2560]{1,0:T(8,128)(2,1)S(1)}, bf16[32,2560]{1,0:T(8,128)(2,1)S(1)}, u32[]{:S(2)}, u32[]{:S(2)}) collective-permute-start(bf16[32,2560]{1,0:T(8,128)(2,1)S(1)} %slice.170), channel_id=1, source_target_pairs={{0,30},{1,31},{2,0},{3,1},{4,2},{5,3},{6,4},{7,5},{8,6},{9,7},{10,... | collective-permute-start | bytes 491528 | tf_op jit(solution)/shard_map/ppermute | solution.py:29
  110.9 1.8 collective-permute-done.20
  114.0 3.3 %project_in.5 = f32[2,256,512]{2,1,0:T(8,128)} custom-call(s32[1]{0:T(128)} %bitcast.45.pair_ref, bf16[4,256,2048]{2,1,0:T(8,128)(2,1)S(1)} %bitcast_dynamic-update-slice_fusion.2.x_ref, bf16[16,64,1536]{2,1,0:T(8,128)(2,1)S(1)} %fusion.1.w_ref), custom_call_target="tpu_custom_call" | custom-call | tf_op jit(solution)/shard_map/project_in/pallas_call | solution.py:57
  117.8 1.2 project_in.7
  119.2 1.2 project_in.6.a_ref
  121.0 1.3 make_cache.1
  122.3 9.3 %all-to-all-start = ((bf16[32,40,128]{2,1,0:T(8,128)(2,1)}), bf16[32,40,128]{2,1,0:T(8,128)(2,1)}, u32[]{:S(2)}, u32[]{:S(2)}) async-start(bf16[32,40,128]{2,1,0:T(8,128)(2,1)} %bitcast.117), calls=%async_computation | async-start | bytes 655360 | tf_op jit(solution)/shard_map/all_to_all | solution.py:359
  131.6 2.2 %copy-done.2 = bf16[4,256,2048]{2,1,0:T(8,128)(2,1)S(1)} copy-done((bf16[4,256,2048]{2,1,0:T(8,128)(2,1)S(1)}, bf16[4,256,2048]{2,1,0:T(8,128)(2,1)}, u32[]{:S(2)}) %copy-start.2) | copy-done | bytes 4194328
  133.8 2.3 %project_in.4.a_ref = f32[2,256,512]{2,1,0:T(8,128)S(1)} custom-call(s32[1]{0:T(128)} %bitcast.1.pair_ref, bf16[4,256,2048]{2,1,0:T(8,128)(2,1)S(1)} %copy-done.2, bf16[16,64,1536]{2,1,0:T(8,128)(2,1)S(1)} %fusion.1.w_ref), custom_call_target="tpu_custom_call" | custom-call | tf_op jit(solution)/shard_map/project_in/pallas_call | solution.py:57
  136.2 5.2 %attend.1.a0 = bf16[512,512]{1,0:T(8,128)(2,1)S(1)} custom-call(f32[2,256,512]{2,1,0:T(8,128)S(1)} %project_in.4.a_ref, f32[2,256,512]{2,1,0:T(8,128)} %collective-permute-done.22.b_ref, bf16[2,256,128]{2,1,0:T(8,128)(2,1)S(1)} %copy-done.5, bf16[2,256,128]{2,1,0:T(8,128)(2,1)S(1)} %copy-done.6, bf16[64,896]{1,0:T(8,128)(2,1)S(1)} %get-tuple-element.74.n0_ref, ...), custom_call_target="tpu_custom_call" | custom-call | tf_op jit(solution)/shard_map/attend/pallas_call | solution.py:214
  141.5 2.0 collective-permute-start.24
  143.5 11.4 %collective-permute-done.25.a4 = bf16[512,512]{1,0:T(8,128)(2,1)S(1)} collective-permute-done((bf16[512,512]{1,0:T(8,128)(2,1)S(1)}, bf16[512,512]{1,0:T(8,128)(2,1)S(1)}, u32[]{:S(2)}, u32[]{:S(2)}) %collective-permute-start.25) | collective-permute-done | bytes 524320 | tf_op jit(solution)/shard_map/ppermute | solution.py:29
  154.9 1.6 collective-permute-start.26
  157.2 4.9 %collective-permute-done.26.a2 = bf16[256,512]{1,0:T(8,128)(2,1)S(1)} collective-permute-done((bf16[256,512]{1,0:T(8,128)(2,1)S(1)}, bf16[256,512]{1,0:T(8,128)(2,1)S(1)}, u32[]{:S(2)}, u32[]{:S(2)}) %collective-permute-start.26) | collective-permute-done | bytes 262176 | tf_op jit(solution)/shard_map/ppermute | solution.py:29
  162.1 2.8 %collective-permute-done.27.a3 = bf16[256,512]{1,0:T(8,128)(2,1)S(1)} collective-permute-done((bf16[256,512]{1,0:T(8,128)(2,1)S(1)}, bf16[256,512]{1,0:T(8,128)(2,1)S(1)}, u32[]{:S(2)}, u32[]{:S(2)}) %collective-permute-start.27) | collective-permute-done | bytes 262176 | tf_op jit(solution)/shard_map/ppermute | solution.py:29
  164.8 5.0 %project_out.1 = bf16[512,1024]{1,0:T(8,128)(2,1)S(1)} custom-call(s32[1]{0:T(128)} %bitcast.shift_ref, bf16[512,512]{1,0:T(8,128)(2,1)S(1)} %attend.1.a0, bf16[512,512]{1,0:T(8,128)(2,1)S(1)} %collective-permute-done.24.a1, bf16[256,512]{1,0:T(8,128)(2,1)S(1)} %collective-permute-done.26.a2, bf16[256,512]{1,0:T(8,128)(2,1)S(1)} %collective-permute-done.27.a3, ...), custom_call_target="tpu_custom_call" | custom-call | tf_op jit(solution)/shard_map/project_out/pallas_call | solution.py:262
  170.0 2.8 %collective-permute-start.30 = (bf16[256,1024]{1,0:T(8,128)(2,1)S(1)}, bf16[256,1024]{1,0:T(8,128)(2,1)S(1)}, u32[]{:S(2)}, u32[]{:S(2)}) collective-permute-start(bf16[256,1024]{1,0:T(8,128)(2,1)S(1)} %get-tuple-element.73), channel_id=1, source_target_pairs={{0,0},{1,64},{2,2},{3,66},{4,4},{5,68},{6,6},{7,70},{8,8},{9,72},{... | collective-permute-start | bytes 1572872 | tf_op jit(solution)/shard_map/ppermute | solution.py:29
  172.9 2.7 %sort_pieces.1 = bf16[64,16,128]{2,1,0:T(8,128)(2,1)} custom-call(bf16[32,40,128]{2,1,0:T(8,128)(2,1)} %all-to-all-done.in_ref), custom_call_target="tpu_custom_call" | custom-call | tf_op jit(solution)/shard_map/sort_pieces/pallas_call | solution.py:155
  175.6 19.1 %all-to-all-start.1 = ((bf16[64,16,128]{2,1,0:T(8,128)(2,1)}), bf16[64,16,128]{2,1,0:T(8,128)(2,1)S(1)}, u32[]{:S(2)}, u32[]{:S(2)}) async-start(bf16[64,16,128]{2,1,0:T(8,128)(2,1)} %sort_pieces.1), calls=%async_computation.1 | async-start | bytes 524288 | tf_op jit(solution)/shard_map/all_to_all | solution.py:380
  194.9 1.1 maximum_bitcast_fusion
  195.9 16.9 %all-to-all-done.1 = bf16[64,16,128]{2,1,0:T(8,128)(2,1)S(1)} async-done(((bf16[64,16,128]{2,1,0:T(8,128)(2,1)}), bf16[64,16,128]{2,1,0:T(8,128)(2,1)S(1)}, u32[]{:S(2)}, u32[]{:S(2)}) %all-to-all-start.1) | async-done | bytes 262176 | tf_op jit(solution)/shard_map/all_to_all | solution.py:380
  (107 shorter events, 17.3 us)
Async XLA Ops:
  0.6 12.1 %copy-start.7 = (bf16[1024,64]{0,1:T(8,128)(2,1)S(1)}, bf16[1024,64]{0,1:T(8,128)(2,1)}, u32[]{:S(2)}) copy-start(bf16[1024,64]{0,1:T(8,128)(2,1)} %param.11) | copy-start | bytes 393220
  4.2 5.6 %collective-permute-start = (bf16[64,896]{1,0:T(8,128)(2,1)S(1)}, bf16[64,896]{1,0:T(8,128)(2,1)S(1)}, u32[]{:S(2)}, u32[]{:S(2)}) collective-permute-start(bf16[64,896]{1,0:T(8,128)(2,1)S(1)} %get-tuple-element.82), channel_id=1, source_target_pairs={{0,32},{1,96},{2,34},{3,98},{4,36},{5,100},{6,38},{7,102},{8,40},{... | collective-permute-start | bytes 344072 | tf_op jit(solution)/shard_map/ppermute | solution.py:29
  4.4 7.6 %collective-permute-start.1 = (bf16[64,896]{1,0:T(8,128)(2,1)S(1)}, bf16[64,896]{1,0:T(8,128)(2,1)S(1)}, u32[]{:S(2)}, u32[]{:S(2)}) collective-permute-start(bf16[64,896]{1,0:T(8,128)(2,1)S(1)} %get-tuple-element.83), channel_id=1, source_target_pairs={{0,0},{1,64},{2,2},{3,66},{4,4},{5,68},{6,6},{7,70},{8,8},{9,72},{... | collective-permute-start | bytes 344072 | tf_op jit(solution)/shard_map/ppermute | solution.py:29
  14.4 28.6 %collective-permute-start.2 = (bf16[64,2560]{1,0:T(8,128)(2,1)}, bf16[64,2560]{1,0:T(8,128)(2,1)}, u32[]{:S(2)}, u32[]{:S(2)}) collective-permute-start(bf16[64,2560]{1,0:T(8,128)(2,1)} %pad_maximum_fusion), channel_id=1, source_target_pairs={{0,2},{1,3},{2,4},{3,5},{4,6},{5,7},{6,8},{7,9},{8,10},{9,11},{10,... | collective-permute-start | bytes 983048 | tf_op jit(solution)/shard_map/ppermute | solution.py:29
  17.1 25.8 %collective-permute-start.3 = (bf16[64,2560]{1,0:T(8,128)(2,1)}, bf16[64,2560]{1,0:T(8,128)(2,1)}, u32[]{:S(2)}, u32[]{:S(2)}) collective-permute-start(bf16[64,2560]{1,0:T(8,128)(2,1)} %pad_maximum_fusion), channel_id=1, source_target_pairs={{0,30},{1,31},{2,0},{3,1},{4,2},{5,3},{6,4},{7,5},{8,6},{9,7},{10,... | collective-permute-start | bytes 983048 | tf_op jit(solution)/shard_map/ppermute | solution.py:29
  37.4 1.9 copy-start.3
  43.0 8.8 %collective-permute-start.4 = (bf16[64,2560]{1,0:T(8,128)(2,1)}, bf16[64,2560]{1,0:T(8,128)(2,1)S(1)}, u32[]{:S(2)}, u32[]{:S(2)}) collective-permute-start(bf16[64,2560]{1,0:T(8,128)(2,1)} %collective-permute-done.2), channel_id=1, source_target_pairs={{0,2},{1,3},{2,4},{3,5},{4,6},{5,7},{6,8},{7,9},{8,10},{9,11},{10,... | collective-permute-start | bytes 983048 | tf_op jit(solution)/shard_map/ppermute | solution.py:29
  43.0 8.8 %collective-permute-start.5 = (bf16[64,2560]{1,0:T(8,128)(2,1)}, bf16[64,2560]{1,0:T(8,128)(2,1)S(1)}, u32[]{:S(2)}, u32[]{:S(2)}) collective-permute-start(bf16[64,2560]{1,0:T(8,128)(2,1)} %collective-permute-done.3), channel_id=1, source_target_pairs={{0,30},{1,31},{2,0},{3,1},{4,2},{5,3},{6,4},{7,5},{8,6},{9,7},{10,... | collective-permute-start | bytes 983048 | tf_op jit(solution)/shard_map/ppermute | solution.py:29
  54.1 33.6 %collective-permute-start.6 = (bf16[256,2048]{1,0:T(8,128)(2,1)S(1)}, bf16[256,2048]{1,0:T(8,128)(2,1)S(1)}, u32[]{:S(2)}, u32[]{:S(2)}) collective-permute-start(bf16[256,2048]{1,0:T(8,128)(2,1)S(1)} %get-tuple-element.68), channel_id=1, source_target_pairs={{0,32},{1,33},{2,34},{3,35},{4,36},{5,37},{6,38},{7,39},{8,40},{9,... | collective-permute-start | bytes 3145736 | tf_op jit(solution)/shard_map/ppermute | solution.py:29
  54.1 39.5 %collective-permute-start.7 = (bf16[256,2048]{1,0:T(8,128)(2,1)S(1)}, bf16[256,2048]{1,0:T(8,128)(2,1)S(1)}, u32[]{:S(2)}, u32[]{:S(2)}) collective-permute-start(bf16[256,2048]{1,0:T(8,128)(2,1)S(1)} %get-tuple-element.68), channel_id=1, source_target_pairs={{0,96},{1,97},{2,98},{3,99},{4,100},{5,101},{6,102},{7,103},{8,104... | collective-permute-start | bytes 3145736 | tf_op jit(solution)/shard_map/ppermute | solution.py:29
  56.1 9.6 %collective-permute-start.10 = (bf16[64,2560]{1,0:T(8,128)(2,1)S(1)}, bf16[64,2560]{1,0:T(8,128)(2,1)S(1)}, u32[]{:S(2)}, u32[]{:S(2)}) collective-permute-start(bf16[64,2560]{1,0:T(8,128)(2,1)S(1)} %collective-permute-done.4), channel_id=1, source_target_pairs={{0,2},{1,3},{2,4},{3,5},{4,6},{5,7},{6,8},{7,9},{8,10},{9,11},{10,... | collective-permute-start | bytes 983048 | tf_op jit(solution)/shard_map/ppermute | solution.py:29
  56.1 9.6 %collective-permute-start.11 = (bf16[64,2560]{1,0:T(8,128)(2,1)S(1)}, bf16[64,2560]{1,0:T(8,128)(2,1)S(1)}, u32[]{:S(2)}, u32[]{:S(2)}) collective-permute-start(bf16[64,2560]{1,0:T(8,128)(2,1)S(1)} %collective-permute-done.5), channel_id=1, source_target_pairs={{0,30},{1,31},{2,0},{3,1},{4,2},{5,3},{6,4},{7,5},{8,6},{9,7},{10,... | collective-permute-start | bytes 983048 | tf_op jit(solution)/shard_map/ppermute | solution.py:29
  60.1 33.7 %copy-start = (bf16[4,256,2048]{2,1,0:T(8,128)(2,1)S(1)}, bf16[4,256,2048]{2,1,0:T(8,128)(2,1)}, u32[]{:S(2)}) copy-start(bf16[4,256,2048]{2,1,0:T(8,128)(2,1)} %get-tuple-element.69) | copy-start | bytes 12582916
  65.7 8.7 %collective-permute-start.12 = (bf16[64,2560]{1,0:T(8,128)(2,1)S(1)}, bf16[64,2560]{1,0:T(8,128)(2,1)S(1)}, u32[]{:S(2)}, u32[]{:S(2)}) collective-permute-start(bf16[64,2560]{1,0:T(8,128)(2,1)S(1)} %collective-permute-done.10), channel_id=1, source_target_pairs={{0,2},{1,3},{2,4},{3,5},{4,6},{5,7},{6,8},{7,9},{8,10},{9,11},{10,... | collective-permute-start | bytes 983048 | tf_op jit(solution)/shard_map/ppermute | solution.py:29
  65.7 8.7 %collective-permute-start.13 = (bf16[64,2560]{1,0:T(8,128)(2,1)S(1)}, bf16[64,2560]{1,0:T(8,128)(2,1)S(1)}, u32[]{:S(2)}, u32[]{:S(2)}) collective-permute-start(bf16[64,2560]{1,0:T(8,128)(2,1)S(1)} %collective-permute-done.11), channel_id=1, source_target_pairs={{0,30},{1,31},{2,0},{3,1},{4,2},{5,3},{6,4},{7,5},{8,6},{9,7},{10,... | collective-permute-start | bytes 983048 | tf_op jit(solution)/shard_map/ppermute | solution.py:29
  74.5 8.3 %collective-permute-start.14 = (bf16[64,2560]{1,0:T(8,128)(2,1)S(1)}, bf16[64,2560]{1,0:T(8,128)(2,1)S(1)}, u32[]{:S(2)}, u32[]{:S(2)}) collective-permute-start(bf16[64,2560]{1,0:T(8,128)(2,1)S(1)} %collective-permute-done.12), channel_id=1, source_target_pairs={{0,2},{1,3},{2,4},{3,5},{4,6},{5,7},{6,8},{7,9},{8,10},{9,11},{10,... | collective-permute-start | bytes 983048 | tf_op jit(solution)/shard_map/ppermute | solution.py:29
  74.5 8.3 %collective-permute-start.15 = (bf16[64,2560]{1,0:T(8,128)(2,1)S(1)}, bf16[64,2560]{1,0:T(8,128)(2,1)S(1)}, u32[]{:S(2)}, u32[]{:S(2)}) collective-permute-start(bf16[64,2560]{1,0:T(8,128)(2,1)S(1)} %collective-permute-done.13), channel_id=1, source_target_pairs={{0,30},{1,31},{2,0},{3,1},{4,2},{5,3},{6,4},{7,5},{8,6},{9,7},{10,... | collective-permute-start | bytes 983048 | tf_op jit(solution)/shard_map/ppermute | solution.py:29
  82.8 11.2 %collective-permute-start.16 = (bf16[64,2560]{1,0:T(8,128)(2,1)S(1)}, bf16[64,2560]{1,0:T(8,128)(2,1)S(1)}, u32[]{:S(2)}, u32[]{:S(2)}) collective-permute-start(bf16[64,2560]{1,0:T(8,128)(2,1)S(1)} %collective-permute-done.14), channel_id=1, source_target_pairs={{0,2},{1,3},{2,4},{3,5},{4,6},{5,7},{6,8},{7,9},{8,10},{9,11},{10,... | collective-permute-start | bytes 983048 | tf_op jit(solution)/shard_map/ppermute | solution.py:29
  82.8 11.3 %collective-permute-start.17 = (bf16[64,2560]{1,0:T(8,128)(2,1)S(1)}, bf16[64,2560]{1,0:T(8,128)(2,1)S(1)}, u32[]{:S(2)}, u32[]{:S(2)}) collective-permute-start(bf16[64,2560]{1,0:T(8,128)(2,1)S(1)} %collective-permute-done.15), channel_id=1, source_target_pairs={{0,30},{1,31},{2,0},{3,1},{4,2},{5,3},{6,4},{7,5},{8,6},{9,7},{10,... | collective-permute-start | bytes 983048 | tf_op jit(solution)/shard_map/ppermute | solution.py:29
  87.7 14.6 %collective-permute-start.8 = (bf16[128,2048]{1,0:T(8,128)(2,1)S(1)}, bf16[128,2048]{1,0:T(8,128)(2,1)S(1)}, u32[]{:S(2)}, u32[]{:S(2)}) collective-permute-start(bf16[128,2048]{1,0:T(8,128)(2,1)S(1)} %slice.180), channel_id=1, source_target_pairs={{0,32},{1,33},{2,34},{3,35},{4,36},{5,37},{6,38},{7,39},{8,40},{9,... | collective-permute-start | bytes 1572872 | tf_op jit(solution)/shard_map/ppermute | solution.py:29
  93.7 12.3 %collective-permute-start.9 = (bf16[128,2048]{1,0:T(8,128)(2,1)S(1)}, bf16[128,2048]{1,0:T(8,128)(2,1)S(1)}, u32[]{:S(2)}, u32[]{:S(2)}) collective-permute-start(bf16[128,2048]{1,0:T(8,128)(2,1)S(1)} %slice.181), channel_id=1, source_target_pairs={{0,96},{1,97},{2,98},{3,99},{4,100},{5,101},{6,102},{7,103},{8,104... | collective-permute-start | bytes 1572872 | tf_op jit(solution)/shard_map/ppermute | solution.py:29
  94.0 12.0 %collective-permute-start.18 = (bf16[64,2560]{1,0:T(8,128)(2,1)S(1)}, bf16[64,2560]{1,0:T(8,128)(2,1)S(1)}, u32[]{:S(2)}, u32[]{:S(2)}) collective-permute-start(bf16[64,2560]{1,0:T(8,128)(2,1)S(1)} %collective-permute-done.16), channel_id=1, source_target_pairs={{0,2},{1,3},{2,4},{3,5},{4,6},{5,7},{6,8},{7,9},{8,10},{9,11},{10,... | collective-permute-start | bytes 983048 | tf_op jit(solution)/shard_map/ppermute | solution.py:29
  94.2 11.8 %collective-permute-start.19 = (bf16[64,2560]{1,0:T(8,128)(2,1)S(1)}, bf16[64,2560]{1,0:T(8,128)(2,1)S(1)}, u32[]{:S(2)}, u32[]{:S(2)}) collective-permute-start(bf16[64,2560]{1,0:T(8,128)(2,1)S(1)} %collective-permute-done.17), channel_id=1, source_target_pairs={{0,30},{1,31},{2,0},{3,1},{4,2},{5,3},{6,4},{7,5},{8,6},{9,7},{10,... | collective-permute-start | bytes 983048 | tf_op jit(solution)/shard_map/ppermute | solution.py:29
  106.0 13.2 %copy-start.1 = (bf16[4,256,2048]{2,1,0:T(8,128)(2,1)}, bf16[4,256,2048]{2,1,0:T(8,128)(2,1)S(1)}, u32[]{:S(2)}) copy-start(bf16[4,256,2048]{2,1,0:T(8,128)(2,1)S(1)} %bitcast_dynamic-update-slice_fusion.2.x_ref) | copy-start | bytes 12582916
  106.0 6.6 %collective-permute-start.20 = (bf16[32,2560]{1,0:T(8,128)(2,1)S(1)}, bf16[32,2560]{1,0:T(8,128)(2,1)S(1)}, u32[]{:S(2)}, u32[]{:S(2)}) collective-permute-start(bf16[32,2560]{1,0:T(8,128)(2,1)S(1)} %slice.168), channel_id=1, source_target_pairs={{0,2},{1,3},{2,4},{3,5},{4,6},{5,7},{6,8},{7,9},{8,10},{9,11},{10,... | collective-permute-start | bytes 491528 | tf_op jit(solution)/shard_map/ppermute | solution.py:29
  106.2 7.1 %collective-permute-start.21 = (bf16[32,2560]{1,0:T(8,128)(2,1)S(1)}, bf16[32,2560]{1,0:T(8,128)(2,1)S(1)}, u32[]{:S(2)}, u32[]{:S(2)}) collective-permute-start(bf16[32,2560]{1,0:T(8,128)(2,1)S(1)} %slice.170), channel_id=1, source_target_pairs={{0,30},{1,31},{2,0},{3,1},{4,2},{5,3},{6,4},{7,5},{8,6},{9,7},{10,... | collective-permute-start | bytes 491528 | tf_op jit(solution)/shard_map/ppermute | solution.py:29
  114.0 50.9 %collective-permute-start.28 = (bf16[1024,1024]{1,0:T(8,128)(2,1)}, bf16[1024,1024]{1,0:T(8,128)(2,1)}, u32[]{:S(2)}, u32[]{:S(2)}) collective-permute-start(bf16[1024,1024]{1,0:T(8,128)(2,1)} %bitcast.50.near_ref), channel_id=1, source_target_pairs={{0,1},{1,0},{2,3},{3,2},{4,5},{5,4},{6,7},{7,6},{8,9},{9,8},{10,11... | collective-permute-start | bytes 6291464 | tf_op jit(solution)/shard_map/ppermute | solution.py:29
  117.3 18.9 %collective-permute-start.22 = (f32[2,256,512]{2,1,0:T(8,128)}, f32[2,256,512]{2,1,0:T(8,128)}, u32[]{:S(2)}, u32[]{:S(2)}) collective-permute-start(f32[2,256,512]{2,1,0:T(8,128)} %project_in.5), channel_id=1, source_target_pairs={{0,1},{1,0},{2,3},{3,2},{4,5},{5,4},{6,7},{7,6},{8,9},{9,8},{10,11... | collective-permute-start | bytes 3145736 | tf_op jit(solution)/shard_map/ppermute | solution.py:29
  119.0 2.0 collective-permute-start.23
  119.1 1.9 copy-start.4
  122.3 50.6 %all-to-all-start = ((bf16[32,40,128]{2,1,0:T(8,128)(2,1)}), bf16[32,40,128]{2,1,0:T(8,128)(2,1)}, u32[]{:S(2)}, u32[]{:S(2)}) async-start(bf16[32,40,128]{2,1,0:T(8,128)(2,1)} %bitcast.117), calls=%async_computation | async-start | bytes 655360 | tf_op jit(solution)/shard_map/all_to_all | solution.py:359
  131.6 2.2 %copy-start.2 = (bf16[4,256,2048]{2,1,0:T(8,128)(2,1)S(1)}, bf16[4,256,2048]{2,1,0:T(8,128)(2,1)}, u32[]{:S(2)}) copy-start(bf16[4,256,2048]{2,1,0:T(8,128)(2,1)} %copy-done.1) | copy-start | bytes 12582916
  133.8 2.3 %copy-start.5 = (bf16[2,256,128]{2,1,0:T(8,128)(2,1)S(1)}, bf16[2,256,128]{2,1,0:T(8,128)(2,1)}, u32[]{:S(2)}) copy-start(bf16[2,256,128]{2,1,0:T(8,128)(2,1)} %get-tuple-element.64.k_ref) | copy-start | bytes 393220
  133.8 2.3 %copy-start.6 = (bf16[2,256,128]{2,1,0:T(8,128)(2,1)S(1)}, bf16[2,256,128]{2,1,0:T(8,128)(2,1)}, u32[]{:S(2)}) copy-start(bf16[2,256,128]{2,1,0:T(8,128)(2,1)} %get-tuple-element.65.v_ref) | copy-start | bytes 393220
  141.3 13.5 %collective-permute-start.25 = (bf16[512,512]{1,0:T(8,128)(2,1)S(1)}, bf16[512,512]{1,0:T(8,128)(2,1)S(1)}, u32[]{:S(2)}, u32[]{:S(2)}) collective-permute-start(bf16[512,512]{1,0:T(8,128)(2,1)S(1)} %attend.1.a0), channel_id=1, source_target_pairs={{0,32},{1,33},{2,34},{3,35},{4,36},{5,37},{6,38},{7,39},{8,40},{9,... | collective-permute-start | bytes 1572872 | tf_op jit(solution)/shard_map/ppermute | solution.py:29
  141.5 15.0 %collective-permute-start.24 = (bf16[512,512]{1,0:T(8,128)(2,1)S(1)}, bf16[512,512]{1,0:T(8,128)(2,1)S(1)}, u32[]{:S(2)}, u32[]{:S(2)}) collective-permute-start(bf16[512,512]{1,0:T(8,128)(2,1)S(1)} %attend.1.a0), channel_id=1, source_target_pairs={{0,96},{1,97},{2,98},{3,99},{4,100},{5,101},{6,102},{7,103},{8,104... | collective-permute-start | bytes 1572872 | tf_op jit(solution)/shard_map/ppermute | solution.py:29
  154.9 7.2 %collective-permute-start.26 = (bf16[256,512]{1,0:T(8,128)(2,1)S(1)}, bf16[256,512]{1,0:T(8,128)(2,1)S(1)}, u32[]{:S(2)}, u32[]{:S(2)}) collective-permute-start(bf16[256,512]{1,0:T(8,128)(2,1)S(1)} %slice.184), channel_id=1, source_target_pairs={{0,32},{1,33},{2,34},{3,35},{4,36},{5,37},{6,38},{7,39},{8,40},{9,... | collective-permute-start | bytes 786440 | tf_op jit(solution)/shard_map/ppermute | solution.py:29
  156.5 8.3 %collective-permute-start.27 = (bf16[256,512]{1,0:T(8,128)(2,1)S(1)}, bf16[256,512]{1,0:T(8,128)(2,1)S(1)}, u32[]{:S(2)}, u32[]{:S(2)}) collective-permute-start(bf16[256,512]{1,0:T(8,128)(2,1)S(1)} %slice.185), channel_id=1, source_target_pairs={{0,96},{1,97},{2,98},{3,99},{4,100},{5,101},{6,102},{7,103},{8,104... | collective-permute-start | bytes 786440 | tf_op jit(solution)/shard_map/ppermute | solution.py:29
  169.9 24.9 %collective-permute-start.29 = (bf16[256,1024]{1,0:T(8,128)(2,1)S(1)}, bf16[256,1024]{1,0:T(8,128)(2,1)S(1)}, u32[]{:S(2)}, u32[]{:S(2)}) collective-permute-start(bf16[256,1024]{1,0:T(8,128)(2,1)S(1)} %get-tuple-element.72), channel_id=1, source_target_pairs={{0,32},{1,96},{2,34},{3,98},{4,36},{5,100},{6,38},{7,102},{8,40},{... | collective-permute-start | bytes 1572872 | tf_op jit(solution)/shard_map/ppermute | solution.py:29
  170.0 24.7 %collective-permute-start.30 = (bf16[256,1024]{1,0:T(8,128)(2,1)S(1)}, bf16[256,1024]{1,0:T(8,128)(2,1)S(1)}, u32[]{:S(2)}, u32[]{:S(2)}) collective-permute-start(bf16[256,1024]{1,0:T(8,128)(2,1)S(1)} %get-tuple-element.73), channel_id=1, source_target_pairs={{0,0},{1,64},{2,2},{3,66},{4,4},{5,68},{6,6},{7,70},{8,8},{9,72},{... | collective-permute-start | bytes 1572872 | tf_op jit(solution)/shard_map/ppermute | solution.py:29
  175.6 37.2 %all-to-all-start.1 = ((bf16[64,16,128]{2,1,0:T(8,128)(2,1)}), bf16[64,16,128]{2,1,0:T(8,128)(2,1)S(1)}, u32[]{:S(2)}, u32[]{:S(2)}) async-start(bf16[64,16,128]{2,1,0:T(8,128)(2,1)} %sort_pieces.1), calls=%async_computation.1 | async-start | bytes 524288 | tf_op jit(solution)/shard_map/all_to_all | solution.py:380

commit v4 on v3

--- a/solution.py
+++ b/solution.py
@@ -222,22 +222,16 @@
     )(kept, other, keys, values, first, second, turns(total))
 
 
-def output_kernel(shift_ref, a0, a1, a2, a3, a4, near_ref, far_ref, out_ref, line_ref, sems):
-    half = a2.shape[0]
+def output_kernel(shift_ref, a0, a1, a2, a3, near_ref, far_ref, out_ref, line_ref, sem):
 
     @pl.when(pl.program_id(0) == 0)
     def _():
-        place = (2 + shift_ref[0]) % X
-        copies = [
-            pltpu.make_async_copy(rows, line_ref.at[place, pl.ds(k * half, half)], sems.at[k])
-            for k, rows in enumerate((a2, a3))
-        ]
-        for copy in copies:
-            copy.start()
-        for d, rows in ((0, a0), (1, a1), (3, a4)):
+        facing = line_ref.at[(2 + shift_ref[0]) % X]
+        copy = pltpu.make_async_copy(a2, facing, sem)
+        copy.start()
+        for d, rows in ((0, a0), (1, a1), (3, a3)):
             line_ref[(d + shift_ref[0]) % X] = rows[...]
-        for copy in copies:
-            copy.wait()
+        copy.wait()
 
     group = a0.shape[1]
     total = 0.0
@@ -253,7 +247,7 @@
     out_ref[...] = total.astype(out_ref.dtype)
 
 
-def project_out(mine, after, across, before, near, far, shift, pieces=4):
+def project_out(mine, after, facing, before, near, far, shift, pieces=4):
     total, group = mine.shape
     columns = near.shape[0]
     whole = pl.BlockSpec(memory_space=pltpu.VMEM)
@@ -264,17 +258,17 @@
         grid_spec=pltpu.PrefetchScalarGridSpec(
             num_scalar_prefetch=1,
             grid=(pieces,),
-            in_specs=[whole, whole, part, part, whole, weights, weights],
+            in_specs=[whole, whole, part, whole, weights, weights],
             out_specs=pl.BlockSpec((total, columns // pieces), lambda i, w: (0, i)),
             scratch_shapes=[
                 pltpu.VMEM((X, total, group), mine.dtype),
-                pltpu.SemaphoreType.DMA((2,)),
+                pltpu.SemaphoreType.DMA,
             ],
         ),
         out_shape=jax.ShapeDtypeStruct((total, columns), jnp.bfloat16),
         compiler_params=pltpu.CompilerParams(vmem_limit_bytes=24 << 20),
         name="project_out",
-    )(shift.reshape(1), mine, after, *across, before, near, far)
+    )(shift.reshape(1), mine, after, facing, before, near, far)
 
 
 def on_device(normed, q_weight, kv_weight, o_weight, lengths, destinations):
@@ -327,10 +321,12 @@
         rising = move(rising, up)
         falling = move(falling, down)
         rising, falling, full = lax.optimization_barrier((rising, falling, placed))
+        if k == START - 1:
+            half = width // 2
+            block, normed = lax.optimization_barrier((block, normed))
+            own = lax.dynamic_slice(normed[0], (0, t * half), (total, half))
         if k == START:
-            half = width // 2
-            rising, normed = lax.optimization_barrier((rising, normed))
-            own = lax.dynamic_slice(normed[0], (0, t * half), (total, half))
+            rising, own = lax.optimization_barrier((rising, own))
             before = move(own, plus)
             after = move(own, minus)
             across0 = move(before[: total // 2], plus)
@@ -356,7 +352,9 @@
     other = move(project_in(states, full_in, 1 - t, pieces, 1), swap)
     kept = project_in(states, full_in, t, pieces, 1)
     keys, values, sent = make_cache(kept, other, first, second, ring)
-    spread = lax.all_to_all(sent.reshape(-1, *sent.shape[2:]), ("z", "tensor"), 0, 0, tiled=True)
+    spread = lax.all_to_all(
+        sent.reshape(-1, *sent.shape[2:]), ("z", "tensor"), 0, 0, tiled=True
+    )
     other = project_in(states, full_in, 1 - t, 0, pieces)
     other = move(other, swap)
     kept = project_in(states, full_in, t, 0, pieces)
@@ -364,9 +362,9 @@
     mixed = attend(kept, other, keys, values, first, second)
     from_before = move(mixed, plus)
     from_after = move(mixed, minus)
-    across = move(from_before[:total], plus), move(from_after[total:], minus)
+    facing = move(mixed, lambda x, z, t: (x + 2, z, t))
     out = project_out(
-        mixed, from_after, across, from_before, o_half, o_other, (x - 2 * t) % X
+        mixed, from_after, facing, from_before, o_half, o_other, (x - 2 * t) % X
     )
     out0 = lax.dynamic_slice(out, (x % 2 * total, 0), (total, out.shape[1]))
     out1 = lax.dynamic_slice(out, ((x + 1) % 2 * total, 0), (total, out.shape[1]))

time: 214 us -> 218 us (1.019)
  waiting for transfers between devices: 64.5 us -> 67.3 us
    dynamic_update_slice x16, local copies, waits for them, and re-layouts: 2.13 us -> 7.02 us  [place(): lax.dynamic_update_slice(full[0], block[None, :, :2 * wide], at)]
    ppermute x31 -> x30, waiting for transfers between devices: 47.6 us -> 50.2 us  [move(): return lax.ppermute(array, ('x', 'z', 'tensor'), pairs)]
    dynamic_slice x1, local copies, waits for them, and re-layouts: 2.34 us -> 0.07 us  [on_device(): own = lax.dynamic_slice(normed[0], (0, t * half), (total, half))]
    ppermute x31 -> x30, starting transfers between devices: 66.5 us -> 65.7 us  [move(): return lax.ppermute(array, ('x', 'z', 'tensor'), pairs)]
  transfers between devices with their start and end apart: 33 -> 32, of which waited for: 15 -> 14; matrix products, arithmetic and copies ran while one was open for 8% -> 10% of each run, Pallas kernels for 10% -> 10%
where the time goes in v4:
time: 218 us; the launch traced here: 217 us
  starting transfers between devices  94.5 us (43%)
  waiting for transfers between devices  67.3 us (31%)
  local copies, waits for them, and re-layouts  26.6 us (12%)
  Pallas kernels  22.5 us (10%)
  other arithmetic  3.19 us (1%)
  between operations  2.65 us (1%)
    ppermute x30, starting transfers between devices, move(): return lax.ppermute(array, ('x', 'z', 'tensor'), pairs)  65.7 us
    ppermute x30, waiting for transfers between devices, move(): return lax.ppermute(array, ('x', 'z', 'tensor'), pairs)  50.2 us
    all_to_all x1, starting transfers between devices, on_device(): arrived = lax.all_to_all(sorted_pieces, ('x', 'z'), 0, 0, tiled=True)  18.8 us
    all_to_all x1, waiting for transfers between devices, on_device(): arrived = lax.all_to_all(sorted_pieces, ('x', 'z'), 0, 0, tiled=True)  17 us
    dynamic_update_slice x17, local copies, waits for them, and re-layouts, place(): lax.dynamic_update_slice(full[1], block[None, :, 2 * wide:], at)  11.1 us
    all_to_all x1, starting transfers between devices, on_device(): lax.all_to_all(sent.reshape(-1, *sent.shape[2:]), ('z', 'tensor'), 0, 0,...  9.97 us
    pallas_call x4, Pallas kernels, project_in(): pl.pallas_call(project_kernel, grid_spec=pltpu.PrefetchScalarGridSpec(num...  8 us
    dynamic_update_slice x16, local copies, waits for them, and re-layouts, place(): lax.dynamic_update_slice(full[0], block[None, :, :2 * wide], at)  7.02 us
  transfers between devices with their start and end apart: 32, of which 14 were waited for; matrix products, arithmetic and copies ran while one was open for 10% of the time, Pallas kernels for 10%

profile of v4, /device:TPU:38, one launch (start us, length us, event | category | flops | bytes accessed | tf_op | source)
XLA Modules:
  0.0 216.7 jit_solution(11321515151476992667)
XLA Ops:
  2.4 1.0 constant_dynamic-slice_fusion.1
  3.4 0.9 constant_dynamic-slice_fusion.7
  4.5 4.4 %collective-permute-start.1 = (bf16[64,896]{1,0:T(8,128)(2,1)S(1)}, bf16[64,896]{1,0:T(8,128)(2,1)S(1)}, u32[]{:S(2)}, u32[]{:S(2)}) collective-permute-start(bf16[64,896]{1,0:T(8,128)(2,1)S(1)} %get-tuple-element.83), channel_id=1, source_target_pairs={{0,0},{1,64},{2,2},{3,66},{4,4},{5,68},{6,6},{7,70},{8,8},{9,72},{... | collective-permute-start | bytes 344072 | tf_op jit(solution)/shard_map/ppermute | solution.py:29
  9.9 2.2 %collective-permute-done.1 = bf16[64,896]{1,0:T(8,128)(2,1)S(1)} collective-permute-done((bf16[64,896]{1,0:T(8,128)(2,1)S(1)}, bf16[64,896]{1,0:T(8,128)(2,1)S(1)}, u32[]{:S(2)}, u32[]{:S(2)}) %collective-permute-start.1) | collective-permute-done | bytes 114720 | tf_op jit(solution)/shard_map/ppermute | solution.py:29
  12.3 2.9 %collective-permute-start.2 = (bf16[64,2560]{1,0:T(8,128)(2,1)S(1)}, bf16[64,2560]{1,0:T(8,128)(2,1)S(1)}, u32[]{:S(2)}, u32[]{:S(2)}) collective-permute-start(bf16[64,2560]{1,0:T(8,128)(2,1)S(1)} %pad_maximum_fusion), channel_id=1, source_target_pairs={{0,2},{1,3},{2,4},{3,5},{4,6},{5,7},{6,8},{7,9},{8,10},{9,11},{10,... | collective-permute-start | bytes 983048 | tf_op jit(solution)/shard_map/ppermute | solution.py:29
  15.2 19.7 %collective-permute-start.3 = (bf16[64,2560]{1,0:T(8,128)(2,1)S(1)}, bf16[64,2560]{1,0:T(8,128)(2,1)S(1)}, u32[]{:S(2)}, u32[]{:S(2)}) collective-permute-start(bf16[64,2560]{1,0:T(8,128)(2,1)S(1)} %pad_maximum_fusion), channel_id=1, source_target_pairs={{0,30},{1,31},{2,0},{3,1},{4,2},{5,3},{6,4},{7,5},{8,6},{9,7},{10,... | collective-permute-start | bytes 983048 | tf_op jit(solution)/shard_map/ppermute | solution.py:29
  35.7 5.2 %collective-permute-done.2 = bf16[64,2560]{1,0:T(8,128)(2,1)S(1)} collective-permute-done((bf16[64,2560]{1,0:T(8,128)(2,1)S(1)}, bf16[64,2560]{1,0:T(8,128)(2,1)S(1)}, u32[]{:S(2)}, u32[]{:S(2)}) %collective-permute-start.2) | collective-permute-done | bytes 327712 | tf_op jit(solution)/shard_map/ppermute | solution.py:29
  41.0 3.7 %collective-permute-start.5 = (bf16[64,2560]{1,0:T(8,128)(2,1)S(1)}, bf16[64,2560]{1,0:T(8,128)(2,1)S(1)}, u32[]{:S(2)}, u32[]{:S(2)}) collective-permute-start(bf16[64,2560]{1,0:T(8,128)(2,1)S(1)} %collective-permute-done.3), channel_id=1, source_target_pairs={{0,30},{1,31},{2,0},{3,1},{4,2},{5,3},{6,4},{7,5},{8,6},{9,7},{10,... | collective-permute-start | bytes 983048 | tf_op jit(solution)/shard_map/ppermute | solution.py:29
  44.7 0.7 bitcast_dynamic-update-slice_fusion.18
  47.4 2.4 %collective-permute-done.4 = bf16[64,2560]{1,0:T(8,128)(2,1)S(1)} collective-permute-done((bf16[64,2560]{1,0:T(8,128)(2,1)S(1)}, bf16[64,2560]{1,0:T(8,128)(2,1)S(1)}, u32[]{:S(2)}, u32[]{:S(2)}) %collective-permute-start.4) | collective-permute-done | bytes 327712 | tf_op jit(solution)/shard_map/ppermute | solution.py:29
  49.7 2.0 collective-permute-start.7
  51.7 3.2 %collective-permute-start.11 = (bf16[64,2560]{1,0:T(8,128)(2,1)S(1)}, bf16[64,2560]{1,0:T(8,128)(2,1)S(1)}, u32[]{:S(2)}, u32[]{:S(2)}) collective-permute-start(bf16[64,2560]{1,0:T(8,128)(2,1)S(1)} %collective-permute-done.5), channel_id=1, source_target_pairs={{0,30},{1,31},{2,0},{3,1},{4,2},{5,3},{6,4},{7,5},{8,6},{9,7},{10,... | collective-permute-start | bytes 983048 | tf_op jit(solution)/shard_map/ppermute | solution.py:29
  55.8 0.7 bitcast_dynamic-update-slice_fusion.15
  57.8 3.0 %collective-permute-done.10 = bf16[64,2560]{1,0:T(8,128)(2,1)S(1)} collective-permute-done((bf16[64,2560]{1,0:T(8,128)(2,1)S(1)}, bf16[64,2560]{1,0:T(8,128)(2,1)S(1)}, u32[]{:S(2)}, u32[]{:S(2)}) %collective-permute-start.10) | collective-permute-done | bytes 327712 | tf_op jit(solution)/shard_map/ppermute | solution.py:29
  60.8 3.2 %collective-permute-start.13 = (bf16[64,2560]{1,0:T(8,128)(2,1)S(1)}, bf16[64,2560]{1,0:T(8,128)(2,1)S(1)}, u32[]{:S(2)}, u32[]{:S(2)}) collective-permute-start(bf16[64,2560]{1,0:T(8,128)(2,1)S(1)} %collective-permute-done.11), channel_id=1, source_target_pairs={{0,30},{1,31},{2,0},{3,1},{4,2},{5,3},{6,4},{7,5},{8,6},{9,7},{10,... | collective-permute-start | bytes 983048 | tf_op jit(solution)/shard_map/ppermute | solution.py:29
  66.7 2.4 %collective-permute-done.12 = bf16[64,2560]{1,0:T(8,128)(2,1)S(1)} collective-permute-done((bf16[64,2560]{1,0:T(8,128)(2,1)S(1)}, bf16[64,2560]{1,0:T(8,128)(2,1)S(1)}, u32[]{:S(2)}, u32[]{:S(2)}) %collective-permute-start.12) | collective-permute-done | bytes 327712 | tf_op jit(solution)/shard_map/ppermute | solution.py:29
  69.1 3.2 %collective-permute-start.15 = (bf16[64,2560]{1,0:T(8,128)(2,1)S(1)}, bf16[64,2560]{1,0:T(8,128)(2,1)S(1)}, u32[]{:S(2)}, u32[]{:S(2)}) collective-permute-start(bf16[64,2560]{1,0:T(8,128)(2,1)S(1)} %collective-permute-done.13), channel_id=1, source_target_pairs={{0,30},{1,31},{2,0},{3,1},{4,2},{5,3},{6,4},{7,5},{8,6},{9,7},{10,... | collective-permute-start | bytes 983048 | tf_op jit(solution)/shard_map/ppermute | solution.py:29
  73.0 0.7 bitcast_dynamic-update-slice_fusion.11
  75.0 2.9 %collective-permute-done.14 = bf16[64,2560]{1,0:T(8,128)(2,1)S(1)} collective-permute-done((bf16[64,2560]{1,0:T(8,128)(2,1)S(1)}, bf16[64,2560]{1,0:T(8,128)(2,1)S(1)}, u32[]{:S(2)}, u32[]{:S(2)}) %collective-permute-start.14) | collective-permute-done | bytes 327712 | tf_op jit(solution)/shard_map/ppermute | solution.py:29
  77.9 3.5 %collective-permute-start.17 = (bf16[64,2560]{1,0:T(8,128)(2,1)S(1)}, bf16[64,2560]{1,0:T(8,128)(2,1)S(1)}, u32[]{:S(2)}, u32[]{:S(2)}) collective-permute-start(bf16[64,2560]{1,0:T(8,128)(2,1)S(1)} %collective-permute-done.15), channel_id=1, source_target_pairs={{0,30},{1,31},{2,0},{3,1},{4,2},{5,3},{6,4},{7,5},{8,6},{9,7},{10,... | collective-permute-start | bytes 983048 | tf_op jit(solution)/shard_map/ppermute | solution.py:29
  83.4 0.7 bitcast_dynamic-update-slice_fusion.9
  84.2 4.7 %collective-permute-start.8 = (bf16[128,2048]{1,0:T(8,128)(2,1)S(1)}, bf16[128,2048]{1,0:T(8,128)(2,1)S(1)}, u32[]{:S(2)}, u32[]{:S(2)}) collective-permute-start(bf16[128,2048]{1,0:T(8,128)(2,1)S(1)} %slice.172), channel_id=1, source_target_pairs={{0,32},{1,33},{2,34},{3,35},{4,36},{5,37},{6,38},{7,39},{8,40},{9,... | collective-permute-start | bytes 1572872 | tf_op jit(solution)/shard_map/ppermute | solution.py:29
  89.5 3.2 %collective-permute-start.19 = (bf16[64,2560]{1,0:T(8,128)(2,1)S(1)}, bf16[64,2560]{1,0:T(8,128)(2,1)S(1)}, u32[]{:S(2)}, u32[]{:S(2)}) collective-permute-start(bf16[64,2560]{1,0:T(8,128)(2,1)S(1)} %collective-permute-done.17), channel_id=1, source_target_pairs={{0,30},{1,31},{2,0},{3,1},{4,2},{5,3},{6,4},{7,5},{8,6},{9,7},{10,... | collective-permute-start | bytes 983048 | tf_op jit(solution)/shard_map/ppermute | solution.py:29
  94.0 3.1 %collective-permute-done.8 = bf16[128,2048]{1,0:T(8,128)(2,1)S(1)} collective-permute-done((bf16[128,2048]{1,0:T(8,128)(2,1)S(1)}, bf16[128,2048]{1,0:T(8,128)(2,1)S(1)}, u32[]{:S(2)}, u32[]{:S(2)}) %collective-permute-start.8) | collective-permute-done | bytes 524320 | tf_op jit(solution)/shard_map/ppermute | solution.py:29
  97.1 3.5 %collective-permute-done.9 = bf16[128,2048]{1,0:T(8,128)(2,1)S(1)} collective-permute-done((bf16[128,2048]{1,0:T(8,128)(2,1)S(1)}, bf16[128,2048]{1,0:T(8,128)(2,1)S(1)}, u32[]{:S(2)}, u32[]{:S(2)}) %collective-permute-start.9) | collective-permute-done | bytes 524320 | tf_op jit(solution)/shard_map/ppermute | solution.py:29
  100.9 3.3 %collective-permute-start.21 = (bf16[32,2560]{1,0:T(8,128)(2,1)S(1)}, bf16[32,2560]{1,0:T(8,128)(2,1)S(1)}, u32[]{:S(2)}, u32[]{:S(2)}) collective-permute-start(bf16[32,2560]{1,0:T(8,128)(2,1)S(1)} %slice.164), channel_id=1, source_target_pairs={{0,30},{1,31},{2,0},{3,1},{4,2},{5,3},{6,4},{7,5},{8,6},{9,7},{10,... | collective-permute-start | bytes 491528 | tf_op jit(solution)/shard_map/ppermute | solution.py:29
  105.6 1.8 collective-permute-done.20
  108.7 1.2 project_in.7
  110.6 3.3 %project_in.5 = f32[2,256,512]{2,1,0:T(8,128)} custom-call(s32[1]{0:T(128)} %bitcast.46.pair_ref, bf16[4,256,2048]{2,1,0:T(8,128)(2,1)S(1)} %bitcast_dynamic-update-slice_fusion.3.x_ref, bf16[16,64,1536]{2,1,0:T(8,128)(2,1)S(1)} %fusion.1.w_ref), custom_call_target="tpu_custom_call" | custom-call | tf_op jit(solution)/shard_map/project_in/pallas_call | solution.py:57
  113.9 1.2 project_in.6.a_ref
  115.1 1.3 make_cache.1
  116.4 10.0 %all-to-all-start = ((bf16[32,40,128]{2,1,0:T(8,128)(2,1)}), bf16[32,40,128]{2,1,0:T(8,128)(2,1)S(1)}, u32[]{:S(2)}, u32[]{:S(2)}) async-start(bf16[32,40,128]{2,1,0:T(8,128)(2,1)} %bitcast.119), calls=%async_computation | async-start | bytes 655360 | tf_op jit(solution)/shard_map/all_to_all | solution.py:355
  126.4 2.2 %copy-done.3 = bf16[4,256,2048]{2,1,0:T(8,128)(2,1)S(1)} copy-done((bf16[4,256,2048]{2,1,0:T(8,128)(2,1)S(1)}, bf16[4,256,2048]{2,1,0:T(8,128)(2,1)}, u32[]{:S(2)}) %copy-start.3) | copy-done | bytes 4194328
  128.6 1.9 copy-done.6
  130.5 2.3 %project_in.4.a_ref = f32[2,256,512]{2,1,0:T(8,128)S(1)} custom-call(s32[1]{0:T(128)} %bitcast.1.pair_ref, bf16[4,256,2048]{2,1,0:T(8,128)(2,1)S(1)} %copy-done.3, bf16[16,64,1536]{2,1,0:T(8,128)(2,1)S(1)} %copy-done.6), custom_call_target="tpu_custom_call" | custom-call | tf_op jit(solution)/shard_map/project_in/pallas_call | solution.py:57
  132.8 5.2 %attend.1.a0 = bf16[512,512]{1,0:T(8,128)(2,1)S(1)} custom-call(f32[2,256,512]{2,1,0:T(8,128)S(1)} %project_in.4.a_ref, f32[2,256,512]{2,1,0:T(8,128)} %collective-permute-done.22.b_ref, bf16[2,256,128]{2,1,0:T(8,128)(2,1)S(1)} %copy-done.8, bf16[2,256,128]{2,1,0:T(8,128)(2,1)S(1)} %copy-done.9, bf16[64,896]{1,0:T(8,128)(2,1)S(1)} %get-tuple-element.74.n0_ref, ...), custom_call_target="tpu_custom_call" | custom-call | tf_op jit(solution)/shard_map/attend/pallas_call | solution.py:214
  138.5 2.8 %collective-permute-start.26 = (bf16[512,512]{1,0:T(8,128)(2,1)S(1)}, bf16[512,512]{1,0:T(8,128)(2,1)}, u32[]{:S(2)}, u32[]{:S(2)}) collective-permute-start(bf16[512,512]{1,0:T(8,128)(2,1)S(1)} %attend.1.a0), channel_id=1, source_target_pairs={{0,32},{1,33},{2,34},{3,35},{4,36},{5,37},{6,38},{7,39},{8,40},{9,... | collective-permute-start | bytes 1572872 | tf_op jit(solution)/shard_map/ppermute | solution.py:29
  141.4 22.7 %collective-permute-done.24.a1 = bf16[512,512]{1,0:T(8,128)(2,1)} collective-permute-done((bf16[512,512]{1,0:T(8,128)(2,1)S(1)}, bf16[512,512]{1,0:T(8,128)(2,1)}, u32[]{:S(2)}, u32[]{:S(2)}) %collective-permute-start.24) | collective-permute-done | bytes 524320 | tf_op jit(solution)/shard_map/ppermute | solution.py:29
  164.7 6.3 %project_out.1 = bf16[512,1024]{1,0:T(8,128)(2,1)S(1)} custom-call(s32[1]{0:T(128)} %bitcast.shift_ref, bf16[512,512]{1,0:T(8,128)(2,1)S(1)} %attend.1.a0, bf16[512,512]{1,0:T(8,128)(2,1)} %collective-permute-done.24.a1, bf16[512,512]{1,0:T(8,128)(2,1)} %collective-permute-done.25.a2, bf16[512,512]{1,0:T(8,128)(2,1)} %collective-permute-done.26.a3, ...), custom_call_target="tpu_custom_call" | custom-call | tf_op jit(solution)/shard_map/project_out/pallas_call | solution.py:256
  171.0 1.0 constant_dynamic-slice_fusion.3
  172.1 1.7 collective-permute-start.28
  173.8 2.3 %collective-permute-start.29 = (bf16[256,1024]{1,0:T(8,128)(2,1)}, bf16[256,1024]{1,0:T(8,128)(2,1)}, u32[]{:S(2)}, u32[]{:S(2)}) collective-permute-start(bf16[256,1024]{1,0:T(8,128)(2,1)} %get-tuple-element.73), channel_id=1, source_target_pairs={{0,0},{1,64},{2,2},{3,66},{4,4},{5,68},{6,6},{7,70},{8,8},{9,72},{... | collective-permute-start | bytes 1572872 | tf_op jit(solution)/shard_map/ppermute | solution.py:29
  176.1 1.8 sort_pieces.1
  177.8 18.8 %all-to-all-start.1 = ((bf16[64,16,128]{2,1,0:T(8,128)(2,1)}), bf16[64,16,128]{2,1,0:T(8,128)(2,1)S(1)}, u32[]{:S(2)}, u32[]{:S(2)}) async-start(bf16[64,16,128]{2,1,0:T(8,128)(2,1)} %sort_pieces.1), calls=%async_computation.1 | async-start | bytes 524288 | tf_op jit(solution)/shard_map/all_to_all | solution.py:378
  196.6 1.3 broadcast_select_fusion.1
  197.9 1.1 maximum_bitcast_fusion
  199.0 17.0 %all-to-all-done.1 = bf16[64,16,128]{2,1,0:T(8,128)(2,1)S(1)} async-done(((bf16[64,16,128]{2,1,0:T(8,128)(2,1)}), bf16[64,16,128]{2,1,0:T(8,128)(2,1)S(1)}, u32[]{:S(2)}, u32[]{:S(2)}) %all-to-all-start.1) | async-done | bytes 262176 | tf_op jit(solution)/shard_map/all_to_all | solution.py:378
  216.0 0.7 copy.24
  (110 shorter events, 19.7 us)
Async XLA Ops:
  0.6 35.0 %copy-start = (bf16[1,256,4096]{2,1,0:T(8,128)(2,1)S(1)}, bf16[1,256,4096]{2,1,0:T(8,128)(2,1)}, u32[]{:S(2)}) copy-start(bf16[1,256,4096]{2,1,0:T(8,128)(2,1)} %param.8) | copy-start | bytes 6291460
  0.6 8.3 %copy-start.10 = (bf16[1024,64]{0,1:T(8,128)(2,1)S(1)}, bf16[1024,64]{0,1:T(8,128)(2,1)}, u32[]{:S(2)}) copy-start(bf16[1024,64]{0,1:T(8,128)(2,1)} %param.11) | copy-start | bytes 393220
  4.4 5.6 %collective-permute-start = (bf16[64,896]{1,0:T(8,128)(2,1)S(1)}, bf16[64,896]{1,0:T(8,128)(2,1)S(1)}, u32[]{:S(2)}, u32[]{:S(2)}) collective-permute-start(bf16[64,896]{1,0:T(8,128)(2,1)S(1)} %get-tuple-element.82), channel_id=1, source_target_pairs={{0,32},{1,96},{2,34},{3,98},{4,36},{5,100},{6,38},{7,102},{8,40},{... | collective-permute-start | bytes 344072 | tf_op jit(solution)/shard_map/ppermute | solution.py:29
  4.5 7.6 %collective-permute-start.1 = (bf16[64,896]{1,0:T(8,128)(2,1)S(1)}, bf16[64,896]{1,0:T(8,128)(2,1)S(1)}, u32[]{:S(2)}, u32[]{:S(2)}) collective-permute-start(bf16[64,896]{1,0:T(8,128)(2,1)S(1)} %get-tuple-element.83), channel_id=1, source_target_pairs={{0,0},{1,64},{2,2},{3,66},{4,4},{5,68},{6,6},{7,70},{8,8},{9,72},{... | collective-permute-start | bytes 344072 | tf_op jit(solution)/shard_map/ppermute | solution.py:29
  9.6 45.3 %copy-start.1 = (bf16[4,256,2048]{2,1,0:T(8,128)(2,1)S(1)}, bf16[4,256,2048]{2,1,0:T(8,128)(2,1)}, u32[]{:S(2)}) copy-start(bf16[4,256,2048]{2,1,0:T(8,128)(2,1)} %blank.3) | copy-start | bytes 12582916
  12.3 28.6 %collective-permute-start.2 = (bf16[64,2560]{1,0:T(8,128)(2,1)S(1)}, bf16[64,2560]{1,0:T(8,128)(2,1)S(1)}, u32[]{:S(2)}, u32[]{:S(2)}) collective-permute-start(bf16[64,2560]{1,0:T(8,128)(2,1)S(1)} %pad_maximum_fusion), channel_id=1, source_target_pairs={{0,2},{1,3},{2,4},{3,5},{4,6},{5,7},{6,8},{7,9},{8,10},{9,11},{10,... | collective-permute-start | bytes 983048 | tf_op jit(solution)/shard_map/ppermute | solution.py:29
  15.2 25.8 %collective-permute-start.3 = (bf16[64,2560]{1,0:T(8,128)(2,1)S(1)}, bf16[64,2560]{1,0:T(8,128)(2,1)S(1)}, u32[]{:S(2)}, u32[]{:S(2)}) collective-permute-start(bf16[64,2560]{1,0:T(8,128)(2,1)S(1)} %pad_maximum_fusion), channel_id=1, source_target_pairs={{0,30},{1,31},{2,0},{3,1},{4,2},{5,3},{6,4},{7,5},{8,6},{9,7},{10,... | collective-permute-start | bytes 983048 | tf_op jit(solution)/shard_map/ppermute | solution.py:29
  41.0 8.7 %collective-permute-start.4 = (bf16[64,2560]{1,0:T(8,128)(2,1)S(1)}, bf16[64,2560]{1,0:T(8,128)(2,1)S(1)}, u32[]{:S(2)}, u32[]{:S(2)}) collective-permute-start(bf16[64,2560]{1,0:T(8,128)(2,1)S(1)} %collective-permute-done.2), channel_id=1, source_target_pairs={{0,2},{1,3},{2,4},{3,5},{4,6},{5,7},{6,8},{7,9},{8,10},{9,11},{10,... | collective-permute-start | bytes 983048 | tf_op jit(solution)/shard_map/ppermute | solution.py:29
  41.0 8.7 %collective-permute-start.5 = (bf16[64,2560]{1,0:T(8,128)(2,1)S(1)}, bf16[64,2560]{1,0:T(8,128)(2,1)S(1)}, u32[]{:S(2)}, u32[]{:S(2)}) collective-permute-start(bf16[64,2560]{1,0:T(8,128)(2,1)S(1)} %collective-permute-done.3), channel_id=1, source_target_pairs={{0,30},{1,31},{2,0},{3,1},{4,2},{5,3},{6,4},{7,5},{8,6},{9,7},{10,... | collective-permute-start | bytes 983048 | tf_op jit(solution)/shard_map/ppermute | solution.py:29
  49.7 34.4 %collective-permute-start.6 = (bf16[256,2048]{1,0:T(8,128)(2,1)S(1)}, bf16[256,2048]{1,0:T(8,128)(2,1)S(1)}, u32[]{:S(2)}, u32[]{:S(2)}) collective-permute-start(bf16[256,2048]{1,0:T(8,128)(2,1)S(1)} %dynamic-slice_bitcast_fusion), channel_id=1, source_target_pairs={{0,32},{1,33},{2,34},{3,35},{4,36},{5,37},{6,38},{7,39},{8,40},{9,... | collective-permute-start | bytes 3145736 | tf_op jit(solution)/shard_map/ppermute | solution.py:29
  49.7 39.2 %collective-permute-start.7 = (bf16[256,2048]{1,0:T(8,128)(2,1)S(1)}, bf16[256,2048]{1,0:T(8,128)(2,1)S(1)}, u32[]{:S(2)}, u32[]{:S(2)}) collective-permute-start(bf16[256,2048]{1,0:T(8,128)(2,1)S(1)} %dynamic-slice_bitcast_fusion), channel_id=1, source_target_pairs={{0,96},{1,97},{2,98},{3,99},{4,100},{5,101},{6,102},{7,103},{8,104... | collective-permute-start | bytes 3145736 | tf_op jit(solution)/shard_map/ppermute | solution.py:29
  51.7 9.1 %collective-permute-start.10 = (bf16[64,2560]{1,0:T(8,128)(2,1)S(1)}, bf16[64,2560]{1,0:T(8,128)(2,1)S(1)}, u32[]{:S(2)}, u32[]{:S(2)}) collective-permute-start(bf16[64,2560]{1,0:T(8,128)(2,1)S(1)} %collective-permute-done.4), channel_id=1, source_target_pairs={{0,2},{1,3},{2,4},{3,5},{4,6},{5,7},{6,8},{7,9},{8,10},{9,11},{10,... | collective-permute-start | bytes 983048 | tf_op jit(solution)/shard_map/ppermute | solution.py:29
  51.7 9.1 %collective-permute-start.11 = (bf16[64,2560]{1,0:T(8,128)(2,1)S(1)}, bf16[64,2560]{1,0:T(8,128)(2,1)S(1)}, u32[]{:S(2)}, u32[]{:S(2)}) collective-permute-start(bf16[64,2560]{1,0:T(8,128)(2,1)S(1)} %collective-permute-done.5), channel_id=1, source_target_pairs={{0,30},{1,31},{2,0},{3,1},{4,2},{5,3},{6,4},{7,5},{8,6},{9,7},{10,... | collective-permute-start | bytes 983048 | tf_op jit(solution)/shard_map/ppermute | solution.py:29
  60.8 8.3 %collective-permute-start.12 = (bf16[64,2560]{1,0:T(8,128)(2,1)S(1)}, bf16[64,2560]{1,0:T(8,128)(2,1)S(1)}, u32[]{:S(2)}, u32[]{:S(2)}) collective-permute-start(bf16[64,2560]{1,0:T(8,128)(2,1)S(1)} %collective-permute-done.10), channel_id=1, source_target_pairs={{0,2},{1,3},{2,4},{3,5},{4,6},{5,7},{6,8},{7,9},{8,10},{9,11},{10,... | collective-permute-start | bytes 983048 | tf_op jit(solution)/shard_map/ppermute | solution.py:29
  60.8 8.3 %collective-permute-start.13 = (bf16[64,2560]{1,0:T(8,128)(2,1)S(1)}, bf16[64,2560]{1,0:T(8,128)(2,1)S(1)}, u32[]{:S(2)}, u32[]{:S(2)}) collective-permute-start(bf16[64,2560]{1,0:T(8,128)(2,1)S(1)} %collective-permute-done.11), channel_id=1, source_target_pairs={{0,30},{1,31},{2,0},{3,1},{4,2},{5,3},{6,4},{7,5},{8,6},{9,7},{10,... | collective-permute-start | bytes 983048 | tf_op jit(solution)/shard_map/ppermute | solution.py:29
  69.1 8.8 %collective-permute-start.14 = (bf16[64,2560]{1,0:T(8,128)(2,1)S(1)}, bf16[64,2560]{1,0:T(8,128)(2,1)S(1)}, u32[]{:S(2)}, u32[]{:S(2)}) collective-permute-start(bf16[64,2560]{1,0:T(8,128)(2,1)S(1)} %collective-permute-done.12), channel_id=1, source_target_pairs={{0,2},{1,3},{2,4},{3,5},{4,6},{5,7},{6,8},{7,9},{8,10},{9,11},{10,... | collective-permute-start | bytes 983048 | tf_op jit(solution)/shard_map/ppermute | solution.py:29
  69.1 8.8 %collective-permute-start.15 = (bf16[64,2560]{1,0:T(8,128)(2,1)S(1)}, bf16[64,2560]{1,0:T(8,128)(2,1)S(1)}, u32[]{:S(2)}, u32[]{:S(2)}) collective-permute-start(bf16[64,2560]{1,0:T(8,128)(2,1)S(1)} %collective-permute-done.13), channel_id=1, source_target_pairs={{0,30},{1,31},{2,0},{3,1},{4,2},{5,3},{6,4},{7,5},{8,6},{9,7},{10,... | collective-permute-start | bytes 983048 | tf_op jit(solution)/shard_map/ppermute | solution.py:29
  77.9 11.4 %collective-permute-start.16 = (bf16[64,2560]{1,0:T(8,128)(2,1)S(1)}, bf16[64,2560]{1,0:T(8,128)(2,1)S(1)}, u32[]{:S(2)}, u32[]{:S(2)}) collective-permute-start(bf16[64,2560]{1,0:T(8,128)(2,1)S(1)} %collective-permute-done.14), channel_id=1, source_target_pairs={{0,2},{1,3},{2,4},{3,5},{4,6},{5,7},{6,8},{7,9},{8,10},{9,11},{10,... | collective-permute-start | bytes 983048 | tf_op jit(solution)/shard_map/ppermute | solution.py:29
  77.9 11.4 %collective-permute-start.17 = (bf16[64,2560]{1,0:T(8,128)(2,1)S(1)}, bf16[64,2560]{1,0:T(8,128)(2,1)S(1)}, u32[]{:S(2)}, u32[]{:S(2)}) collective-permute-start(bf16[64,2560]{1,0:T(8,128)(2,1)S(1)} %collective-permute-done.15), channel_id=1, source_target_pairs={{0,30},{1,31},{2,0},{3,1},{4,2},{5,3},{6,4},{7,5},{8,6},{9,7},{10,... | collective-permute-start | bytes 983048 | tf_op jit(solution)/shard_map/ppermute | solution.py:29
  84.1 8.6 %copy-start.4 = (bf16[16,64,1536]{2,1,0:T(8,128)(2,1)S(1)}, bf16[16,64,1536]{2,1,0:T(8,128)(2,1)}, u32[]{:S(2)}) copy-start(bf16[16,64,1536]{2,1,0:T(8,128)(2,1)} %bitcast_dynamic-update-slice_fusion.9) | copy-start | bytes 9437188
  84.2 12.9 %collective-permute-start.8 = (bf16[128,2048]{1,0:T(8,128)(2,1)S(1)}, bf16[128,2048]{1,0:T(8,128)(2,1)S(1)}, u32[]{:S(2)}, u32[]{:S(2)}) collective-permute-start(bf16[128,2048]{1,0:T(8,128)(2,1)S(1)} %slice.172), channel_id=1, source_target_pairs={{0,32},{1,33},{2,34},{3,35},{4,36},{5,37},{6,38},{7,39},{8,40},{9,... | collective-permute-start | bytes 1572872 | tf_op jit(solution)/shard_map/ppermute | solution.py:29
  89.0 11.7 %collective-permute-start.9 = (bf16[128,2048]{1,0:T(8,128)(2,1)S(1)}, bf16[128,2048]{1,0:T(8,128)(2,1)S(1)}, u32[]{:S(2)}, u32[]{:S(2)}) collective-permute-start(bf16[128,2048]{1,0:T(8,128)(2,1)S(1)} %slice.173), channel_id=1, source_target_pairs={{0,96},{1,97},{2,98},{3,99},{4,100},{5,101},{6,102},{7,103},{8,104... | collective-permute-start | bytes 1572872 | tf_op jit(solution)/shard_map/ppermute | solution.py:29
  89.3 11.4 %collective-permute-start.18 = (bf16[64,2560]{1,0:T(8,128)(2,1)S(1)}, bf16[64,2560]{1,0:T(8,128)(2,1)S(1)}, u32[]{:S(2)}, u32[]{:S(2)}) collective-permute-start(bf16[64,2560]{1,0:T(8,128)(2,1)S(1)} %collective-permute-done.16), channel_id=1, source_target_pairs={{0,2},{1,3},{2,4},{3,5},{4,6},{5,7},{6,8},{7,9},{8,10},{9,11},{10,... | collective-permute-start | bytes 983048 | tf_op jit(solution)/shard_map/ppermute | solution.py:29
  89.5 11.3 %collective-permute-start.19 = (bf16[64,2560]{1,0:T(8,128)(2,1)S(1)}, bf16[64,2560]{1,0:T(8,128)(2,1)S(1)}, u32[]{:S(2)}, u32[]{:S(2)}) collective-permute-start(bf16[64,2560]{1,0:T(8,128)(2,1)S(1)} %collective-permute-done.17), channel_id=1, source_target_pairs={{0,30},{1,31},{2,0},{3,1},{4,2},{5,3},{6,4},{7,5},{8,6},{9,7},{10,... | collective-permute-start | bytes 983048 | tf_op jit(solution)/shard_map/ppermute | solution.py:29
  100.7 13.2 %copy-start.2 = (bf16[4,256,2048]{2,1,0:T(8,128)(2,1)}, bf16[4,256,2048]{2,1,0:T(8,128)(2,1)S(1)}, u32[]{:S(2)}) copy-start(bf16[4,256,2048]{2,1,0:T(8,128)(2,1)S(1)} %bitcast_dynamic-update-slice_fusion.3.x_ref) | copy-start | bytes 12582916
  100.8 6.6 %collective-permute-start.20 = (bf16[32,2560]{1,0:T(8,128)(2,1)S(1)}, bf16[32,2560]{1,0:T(8,128)(2,1)S(1)}, u32[]{:S(2)}, u32[]{:S(2)}) collective-permute-start(bf16[32,2560]{1,0:T(8,128)(2,1)S(1)} %slice.162), channel_id=1, source_target_pairs={{0,2},{1,3},{2,4},{3,5},{4,6},{5,7},{6,8},{7,9},{8,10},{9,11},{10,... | collective-permute-start | bytes 491528 | tf_op jit(solution)/shard_map/ppermute | solution.py:29
  100.9 7.1 %collective-permute-start.21 = (bf16[32,2560]{1,0:T(8,128)(2,1)S(1)}, bf16[32,2560]{1,0:T(8,128)(2,1)S(1)}, u32[]{:S(2)}, u32[]{:S(2)}) collective-permute-start(bf16[32,2560]{1,0:T(8,128)(2,1)S(1)} %slice.164), channel_id=1, source_target_pairs={{0,30},{1,31},{2,0},{3,1},{4,2},{5,3},{6,4},{7,5},{8,6},{9,7},{10,... | collective-permute-start | bytes 491528 | tf_op jit(solution)/shard_map/ppermute | solution.py:29
  108.7 56.1 %collective-permute-start.27 = (bf16[1024,1024]{1,0:T(8,128)(2,1)}, bf16[1024,1024]{1,0:T(8,128)(2,1)}, u32[]{:S(2)}, u32[]{:S(2)}) collective-permute-start(bf16[1024,1024]{1,0:T(8,128)(2,1)} %bitcast.51.near_ref), channel_id=1, source_target_pairs={{0,1},{1,0},{2,3},{3,2},{4,5},{5,4},{6,7},{7,6},{8,9},{9,8},{10,11... | collective-permute-start | bytes 6291464 | tf_op jit(solution)/shard_map/ppermute | solution.py:29
  108.7 5.2 %copy-start.5 = (bf16[16,64,1536]{2,1,0:T(8,128)(2,1)}, bf16[16,64,1536]{2,1,0:T(8,128)(2,1)S(1)}, u32[]{:S(2)}) copy-start(bf16[16,64,1536]{2,1,0:T(8,128)(2,1)S(1)} %fusion.1.w_ref) | copy-start | bytes 9437188
  109.9 5.2 %collective-permute-start.23 = (f32[2,256,256]{2,1,0:T(8,128)S(1)}, f32[2,256,256]{2,1,0:T(8,128)S(1)}, u32[]{:S(2)}, u32[]{:S(2)}) collective-permute-start(f32[2,256,256]{2,1,0:T(8,128)S(1)} %project_in.7), channel_id=1, source_target_pairs={{0,1},{1,0},{2,3},{3,2},{4,5},{5,4},{6,7},{7,6},{8,9},{9,8},{10,11... | collective-permute-start | bytes 1572872 | tf_op jit(solution)/shard_map/ppermute | solution.py:29
  113.8 19.0 %collective-permute-start.22 = (f32[2,256,512]{2,1,0:T(8,128)}, f32[2,256,512]{2,1,0:T(8,128)}, u32[]{:S(2)}, u32[]{:S(2)}) collective-permute-start(f32[2,256,512]{2,1,0:T(8,128)} %project_in.5), channel_id=1, source_target_pairs={{0,1},{1,0},{2,3},{3,2},{4,5},{5,4},{6,7},{7,6},{8,9},{9,8},{10,11... | collective-permute-start | bytes 3145736 | tf_op jit(solution)/shard_map/ppermute | solution.py:29
  113.9 1.2 copy-start.7
  116.4 59.6 %all-to-all-start = ((bf16[32,40,128]{2,1,0:T(8,128)(2,1)}), bf16[32,40,128]{2,1,0:T(8,128)(2,1)S(1)}, u32[]{:S(2)}, u32[]{:S(2)}) async-start(bf16[32,40,128]{2,1,0:T(8,128)(2,1)} %bitcast.119), calls=%async_computation | async-start | bytes 655360 | tf_op jit(solution)/shard_map/all_to_all | solution.py:355
  126.4 2.2 %copy-start.3 = (bf16[4,256,2048]{2,1,0:T(8,128)(2,1)S(1)}, bf16[4,256,2048]{2,1,0:T(8,128)(2,1)}, u32[]{:S(2)}) copy-start(bf16[4,256,2048]{2,1,0:T(8,128)(2,1)} %copy-done.2) | copy-start | bytes 12582916
  128.6 1.9 copy-start.6
  130.5 2.3 %copy-start.8 = (bf16[2,256,128]{2,1,0:T(8,128)(2,1)S(1)}, bf16[2,256,128]{2,1,0:T(8,128)(2,1)}, u32[]{:S(2)}) copy-start(bf16[2,256,128]{2,1,0:T(8,128)(2,1)} %get-tuple-element.66.k_ref) | copy-start | bytes 393220
  130.5 2.3 %copy-start.9 = (bf16[2,256,128]{2,1,0:T(8,128)(2,1)S(1)}, bf16[2,256,128]{2,1,0:T(8,128)(2,1)}, u32[]{:S(2)}) copy-start(bf16[2,256,128]{2,1,0:T(8,128)(2,1)} %get-tuple-element.67.v_ref) | copy-start | bytes 393220
  138.0 26.1 %collective-permute-start.24 = (bf16[512,512]{1,0:T(8,128)(2,1)S(1)}, bf16[512,512]{1,0:T(8,128)(2,1)}, u32[]{:S(2)}, u32[]{:S(2)}) collective-permute-start(bf16[512,512]{1,0:T(8,128)(2,1)S(1)} %attend.1.a0), channel_id=1, source_target_pairs={{0,96},{1,97},{2,98},{3,99},{4,100},{5,101},{6,102},{7,103},{8,104... | collective-permute-start | bytes 1572872 | tf_op jit(solution)/shard_map/ppermute | solution.py:29
  138.5 25.6 %collective-permute-start.25 = (bf16[512,512]{1,0:T(8,128)(2,1)S(1)}, bf16[512,512]{1,0:T(8,128)(2,1)}, u32[]{:S(2)}, u32[]{:S(2)}) collective-permute-start(bf16[512,512]{1,0:T(8,128)(2,1)S(1)} %attend.1.a0), channel_id=1, source_target_pairs={{0,64},{1,65},{2,66},{3,67},{4,68},{5,69},{6,70},{7,71},{8,72},{9,... | collective-permute-start | bytes 1572872 | tf_op jit(solution)/shard_map/ppermute | solution.py:29
  138.5 26.2 %collective-permute-start.26 = (bf16[512,512]{1,0:T(8,128)(2,1)S(1)}, bf16[512,512]{1,0:T(8,128)(2,1)}, u32[]{:S(2)}, u32[]{:S(2)}) collective-permute-start(bf16[512,512]{1,0:T(8,128)(2,1)S(1)} %attend.1.a0), channel_id=1, source_target_pairs={{0,32},{1,33},{2,34},{3,35},{4,36},{5,37},{6,38},{7,39},{8,40},{9,... | collective-permute-start | bytes 1572872 | tf_op jit(solution)/shard_map/ppermute | solution.py:29
  172.1 24.5 %collective-permute-start.28 = (bf16[256,1024]{1,0:T(8,128)(2,1)}, bf16[256,1024]{1,0:T(8,128)(2,1)}, u32[]{:S(2)}, u32[]{:S(2)}) collective-permute-start(bf16[256,1024]{1,0:T(8,128)(2,1)} %get-tuple-element.72), channel_id=1, source_target_pairs={{0,32},{1,96},{2,34},{3,98},{4,36},{5,100},{6,38},{7,102},{8,40},{... | collective-permute-start | bytes 1572872 | tf_op jit(solution)/shard_map/ppermute | solution.py:29
  173.8 22.8 %collective-permute-start.29 = (bf16[256,1024]{1,0:T(8,128)(2,1)}, bf16[256,1024]{1,0:T(8,128)(2,1)}, u32[]{:S(2)}, u32[]{:S(2)}) collective-permute-start(bf16[256,1024]{1,0:T(8,128)(2,1)} %get-tuple-element.73), channel_id=1, source_target_pairs={{0,0},{1,64},{2,2},{3,66},{4,4},{5,68},{6,6},{7,70},{8,8},{9,72},{... | collective-permute-start | bytes 1572872 | tf_op jit(solution)/shard_map/ppermute | solution.py:29
  177.8 38.2 %all-to-all-start.1 = ((bf16[64,16,128]{2,1,0:T(8,128)(2,1)}), bf16[64,16,128]{2,1,0:T(8,128)(2,1)S(1)}, u32[]{:S(2)}, u32[]{:S(2)}) async-start(bf16[64,16,128]{2,1,0:T(8,128)(2,1)} %sort_pieces.1), calls=%async_computation.1 | async-start | bytes 524288 | tf_op jit(solution)/shard_map/all_to_all | solution.py:378
